TPU v7x, 512 devices: a whole 4x4x16 slice. The times are simulated.
512 devices in a mesh: dp: 64 (over x, y, z_hi, core), emb: 8 (over z_lo).
Axes of the slice: x: 4, y: 4, z: 16 (z_hi: 2, z_lo: 8; z = z_hi * 8 + z_lo), core: 2. Of those that a mesh axis runs over, the one named last changes fastest.
Arguments:
- cur_ids: int32 [131072], P(('dp', 'emb')), may hold values from 0 to 12287, as said below
- prev_ids: int32 [131072], P(('dp', 'emb')), may hold values from 0 to 12287, as said below
- prev_grads: bfloat16 [131072, 128], P(('dp', 'emb')), may hold values from -6 to 6
- row_place: int32 [12288], replicated, may hold values from 0 to 12287, as said below
- table: float32 [12288, 128], P('emb'), may hold values from -6 to 6
- accum: float32 [12288, 128], P('emb'), may hold values from 0.05 to 2
- labels: float32 [131072], P('dp'), may hold values from 0 to 1
- gain: float32 [128], replicated, may hold values from 0.5 to 1.5
- w_gate: bfloat16 [128, 4096], P(None, 'emb'), may hold values from -0.5 to 0.5
- w_up: bfloat16 [128, 4096], P(None, 'emb'), may hold values from -0.5 to 0.5
- w_out: bfloat16 [4096], P('emb'), may hold values from -0.09375 to 0.09375
Outputs:
- new_table: float32 [12288, 128], P('emb')
- new_accum: float32 [12288, 128], P('emb')
- grad_gate: float32 [128, 4096], P(None, 'emb')
- grad_up: float32 [128, 4096], P(None, 'emb')
- emb_grad: float32 [131072, 128], P(('dp', 'emb'))
Inputs may be any that keep to these rules, and one draw needn't show every extreme that they name: A permutation of the table rows; row i is stored on shard row_place[i] // 1536 of emb at position row_place[i] % 1536. `cur_ids`: the 256 ids of one device name rows of one shard at most 64 times, and exactly 64 times for some shard. `prev_ids`: the 256 ids of one device name rows of one shard at most 64 times, and exactly 64 times for some shard.
All inputs are finite; a program needn't handle non-finite values.
Results may differ from a plain program's by a relative error of at most 0.0069.
Values may be sent and summed in bfloat16 or wider, within the bound.
No kernel may reach another device: no remote copies, remote signals or barrier semaphores. Data moves between devices by JAX's collectives and lax.ppermute only.
A program may use at most 64 MiB of HBM per device.

v0:
```python
import math

import jax
import jax.numpy as jnp
from jax import lax
from jax.sharding import Mesh
from jax.sharding import PartitionSpec as P

DP = ("dp_0", "dp_1", "dp_2", "dp_3")
DP_EMB = ("dp_0", "dp_1", "dp_2", "dp_3", "emb")


loss_weight = 64.0
learn_rate = 0.1
norm_eps = 1e-06


def from_everyone(array, axis):
    length = lax.axis_size(axis)
    return lax.all_to_all(
        jnp.broadcast_to(array[None], (length, *array.shape)), axis, 0, 0, tiled=True
    )


def laid_out(pieces, dim):
    pieces = jnp.moveaxis(pieces, 0, dim)
    dims = pieces.shape
    return pieces.reshape(*dims[:dim], dims[dim] * dims[dim + 1], *dims[dim + 2 :])


def gathered_copies(array, axis, dim):
    pieces = from_everyone(array, axis)
    return laid_out(pieces, dim)


def of_everyone(array, axis):
    return from_everyone(array, axis).sum(axis=0)


def cut_along(array, dim, length):
    before, after = (array.shape[:dim], array.shape[dim + 1 :])
    return jnp.moveaxis(array.reshape(*before, length, -1, *after), dim, 0)


def sent_and_summed(array, axis, dim):
    pieces = cut_along(array, dim, lax.axis_size(axis))
    arrived = lax.all_to_all(pieces, axis, split_axis=0, concat_axis=0, tiled=True)
    return arrived.sum(axis=0)


def filled_up(lines, length):
    spare = -len(lines) % length
    return jnp.pad(lines, [(0, spare)] + [(0, 0)] * (lines.ndim - 1))


def whole_of(array, axes, dim):
    far, near = axes
    initial = from_everyone(array, far)
    pieces = jnp.swapaxes(from_everyone(initial, near), 0, 1)
    return laid_out(pieces.reshape(-1, *array.shape), dim)


def sum_in_two_steps(array, axes, dim):
    far, near = axes
    own = sent_and_summed(cut_along(array, dim, lax.axis_size(far)), near, dim + 1)
    return jnp.sum(lax.all_to_all(own, far, 0, 0, tiled=True), axis=0)


def nested_sum(array, axes):
    padded = filled_up(array, lax.axis_size(axes[0]) * lax.axis_size(axes[1]))
    whole = whole_of(sum_in_two_steps(padded, axes, 0), axes, 0)
    return lax.slice_in_dim(whole, 0, len(array)).reshape(array.shape)


def together(arrays, axis):
    line, at, finished = (jnp.concatenate([a.reshape(-1) for a in arrays]), 0, [])
    running = nested_sum(line, axis)
    for a in arrays:
        finished.append(running[at : at + a.size].reshape(a.shape))
        at += a.size
    return tuple(finished)


def pack_slots(stored, rows_shard, capacity, shards):
    owner_shard = stored // rows_shard
    slot_index = stored % rows_shard
    matches = (owner_shard[:, None] == jnp.arange(shards, dtype=jnp.int32)[None, :]).astype(
        jnp.int32
    )
    ranking = jnp.sum(jnp.cumsum(matches, axis=0) * matches, axis=1) - 1
    return (slot_index, owner_shard * capacity + ranking)


def on_device(
    cur_ids, prev_ids, prev_grads, row_place, table, accum, labels, gain, w_gate, w_up, w_out
):
    shards = lax.axis_size("emb")
    replicas = lax.axis_size(DP)
    rows_shard = table.shape[0]
    emb_width = table.shape[1]
    tok_rows = cur_ids.shape[0]
    capacity = min(tok_rows, 2 * tok_rows // shards)
    slot_index, target_pos = pack_slots(row_place[cur_ids], rows_shard, capacity, shards)
    requests = (
        jnp.full((shards * capacity,), -1, jnp.int32)
        .at[target_pos]
        .set(slot_index)
        .reshape(shards, capacity)
    )
    wanted = lax.all_to_all(requests, "emb", split_axis=0, concat_axis=0, tiled=True)
    fetched = table[jnp.maximum(wanted, 0)]
    fetched = jnp.where((wanted >= 0)[..., None], fetched, 0.0).astype(jnp.bfloat16)
    answers = lax.all_to_all(fetched, "emb", split_axis=0, concat_axis=0, tiled=True)
    looked_up = answers.reshape(shards * capacity, emb_width)[target_pos]
    grad_slot, grad_pos = pack_slots(row_place[prev_ids], rows_shard, capacity, shards)
    slot_pack = (
        jnp.full((shards * capacity,), -1, jnp.int32)
        .at[grad_pos]
        .set(grad_slot)
        .reshape(shards, capacity)
    )
    grad_pack = jnp.zeros((shards * capacity, emb_width), jnp.bfloat16).at[grad_pos].set(prev_grads)
    grad_pack = grad_pack.reshape(shards, capacity, emb_width)
    got_rows, got_slots = (
        lax.all_to_all(grad_pack, "emb", split_axis=0, concat_axis=0, tiled=True),
        lax.all_to_all(slot_pack, "emb", split_axis=0, concat_axis=0, tiled=True),
    )
    one_hot = (jnp.arange(rows_shard, dtype=jnp.int32)[:, None] == got_slots.reshape(1, -1)).astype(
        jnp.bfloat16
    )
    table_grad = jnp.dot(
        one_hot, got_rows.reshape(-1, emb_width), preferred_element_type=jnp.float32
    )
    values = looked_up.astype(jnp.float32)
    inverse_rms = lax.rsqrt(jnp.mean(values * values, axis=1, keepdims=True) + norm_eps)
    normed = (values * inverse_rms * gain).astype(jnp.bfloat16)
    gathered = gathered_copies(normed, "emb", 0)
    gate_proj = jnp.dot(gathered, w_gate, preferred_element_type=jnp.float32)
    up_proj = jnp.dot(gathered, w_up, preferred_element_type=jnp.float32)
    sigmoid_gate = jax.nn.sigmoid(gate_proj)
    activated = gate_proj * sigmoid_gate
    hidden = (activated * up_proj).astype(jnp.bfloat16)
    partial_value = jnp.dot(hidden, w_out, preferred_element_type=jnp.float32)
    logits = of_everyone(partial_value, "emb")
    slopes = loss_weight * (jax.nn.sigmoid(logits) - labels)
    back_hidden = slopes[:, None] * w_out.astype(jnp.float32)[None, :]
    back_gate = (
        back_hidden * up_proj * sigmoid_gate * (1.0 + gate_proj * (1.0 - sigmoid_gate))
    ).astype(jnp.bfloat16)
    back_up = (back_hidden * activated).astype(jnp.bfloat16)
    contract = (((0,), (0,)), ((), ()))
    gate_part = lax.dot_general(gathered, back_gate, contract, preferred_element_type=jnp.float32)
    up_part = lax.dot_general(gathered, back_up, contract, preferred_element_type=jnp.float32)
    across = (((1,), (1,)), ((), ()))
    result = lax.dot_general(back_gate, w_gate, across, preferred_element_type=jnp.float32)
    back_normed = sent_and_summed(
        result + lax.dot_general(back_up, w_up, across, preferred_element_type=jnp.float32),
        "emb",
        0,
    )
    scaled = back_normed * gain
    emb_grad = inverse_rms * scaled - values * inverse_rms**3 * jnp.mean(
        values * scaled, axis=1, keepdims=True
    )
    gate_sum, up_sum, total_grad = together(
        (gate_part, up_part, table_grad), (("dp_0", "dp_1", "dp_2"), "dp_3")
    )
    new_accum = accum + total_grad * total_grad
    new_table = table - learn_rate * total_grad * lax.rsqrt(new_accum)
    tower_scale = 1.0 / math.sqrt(tok_rows * shards * replicas)
    return (new_table, new_accum, gate_sum * tower_scale, up_sum * tower_scale, emb_grad)


def solution(mesh):
    torus = Mesh(
        mesh.devices.reshape(4, 4, 2, 2, mesh.shape["emb"]), ("dp_0", "dp_1", "dp_2", "dp_3", "emb")
    )
    return jax.shard_map(
        on_device,
        mesh=torus,
        in_specs=(
            P(DP_EMB),
            P(DP_EMB),
            P(DP_EMB, None),
            P(),
            P("emb", None),
            P("emb", None),
            P(DP),
            P(),
            P(None, "emb"),
            P(None, "emb"),
            P("emb"),
        ),
        out_specs=(P("emb", None), P("emb", None), P(None, "emb"), P(None, "emb"), P(DP_EMB, None)),
        check_vma=False,
    )
```

profile of v0, /device:TPU:1, one launch (start us, length us, event | category | flops | bytes accessed | tf_op | source)
XLA Modules:
  0.0 309.8 jit_solution(17479610885088849231)
XLA Ops:
  0.7 0.7 compare_select_fusion.3
  1.4 2.0 gather_fusion
  4.4 1.4 scatter_custom_fusion
  5.9 22.1 %all_to_all.69 = s32[8,1,64]{2,1,0:T(1,128)S(1)} all-to-all(s32[8,1,64]{2,1,0:T(1,128)S(1)} %all_to_all.44), channel_id=1, replica_groups=mesh['dp_0'=4,'dp_1'=4,'dp_2'=2,'dp_3'=2,'emb'=8] {'emb'}, dimensions={0} | all-to-all | bytes 4096 | tf_op jit(solution)/shard_map/all_to_all | solution.py:110
  28.1 2.2 gather_fusion.1
  30.3 0.8 select_convert_fusion
  31.1 3.4 %all-to-all-start.1 = ((bf16[8,64,128]{2,1,0:T(8,128)(2,1)}), bf16[8,64,128]{2,1,0:T(8,128)(2,1)S(1)}, u32[]{:S(2)}, u32[]{:S(2)}) async-start(bf16[8,64,128]{2,1,0:T(8,128)(2,1)} %select_convert_fusion), calls=%async_computation.1 | async-start | bytes 262144 | tf_op jit(solution)/shard_map/all_to_all | solution.py:113
  34.5 10.2 %all-to-all-done.1 = bf16[8,64,128]{2,1,0:T(8,128)(2,1)S(1)} async-done(((bf16[8,64,128]{2,1,0:T(8,128)(2,1)}), bf16[8,64,128]{2,1,0:T(8,128)(2,1)S(1)}, u32[]{:S(2)}, u32[]{:S(2)}) %all-to-all-start.1) | async-done | bytes 131104 | tf_op jit(solution)/shard_map/all_to_all | solution.py:113
  44.7 0.9 gather_fusion.2
  45.9 0.9 broadcast_in_dim.31
  46.7 5.4 %all-to-all-start.2 = ((bf16[8,256,128]{2,1,0:T(8,128)(2,1)}), bf16[8,256,128]{2,1,0:T(8,128)(2,1)S(1)}, u32[]{:S(2)}, u32[]{:S(2)}) async-start(bf16[8,256,128]{2,1,0:T(8,128)(2,1)} %broadcast_in_dim.31), calls=%async_computation.2 | async-start | bytes 1048576 | tf_op jit(solution)/shard_map/all_to_all | solution.py:20
  52.2 1.7 gather_fusion.3
  55.0 1.4 scatter_custom_fusion.1
  56.4 0.7 all_to_all.49
  57.0 2.1 scatter_custom_fusion.2
  59.1 13.8 %all-to-all-done.2 = bf16[8,256,128]{2,1,0:T(8,128)(2,1)S(1)} async-done(((bf16[8,256,128]{2,1,0:T(8,128)(2,1)}), bf16[8,256,128]{2,1,0:T(8,128)(2,1)S(1)}, u32[]{:S(2)}, u32[]{:S(2)}) %all-to-all-start.2) | async-done | bytes 524320 | tf_op jit(solution)/shard_map/all_to_all | solution.py:20
  72.9 11.5 %all-to-all-start.4 = ((s32[8,1,64]{2,1,0:T(1,128)}), s32[8,1,64]{2,1,0:T(1,128)S(1)}, u32[]{:S(2)}, u32[]{:S(2)}) async-start(s32[8,1,64]{2,1,0:T(1,128)} %all_to_all.49), calls=%async_computation.4 | async-start | bytes 8192 | tf_op jit(solution)/shard_map/all_to_all | solution.py:126
  84.4 2.7 fusion.29
  87.1 2.6 fusion.30
  89.7 3.9 %all-to-all-done.4 = s32[8,1,64]{2,1,0:T(1,128)S(1)} async-done(((s32[8,1,64]{2,1,0:T(1,128)}), s32[8,1,64]{2,1,0:T(1,128)S(1)}, u32[]{:S(2)}, u32[]{:S(2)}) %all-to-all-start.4) | async-done | bytes 2080 | tf_op jit(solution)/shard_map/all_to_all | solution.py:126
  93.6 5.4 %all-to-all-start.5 = ((bf16[8,64,128]{2,1,0:T(8,128)(2,1)}), bf16[8,64,128]{2,1,0:T(8,128)(2,1)S(1)}, u32[]{:S(2)}, u32[]{:S(2)}) async-start(bf16[8,64,128]{2,1,0:T(8,128)(2,1)} %bitcast.21), calls=%async_computation.5 | async-start | bytes 262144 | tf_op jit(solution)/shard_map/all_to_all | solution.py:125
  99.1 4.7 %fusion.5 = f32[1,2048]{1,0:T(1,128)S(1)} fusion(bf16[512,1]{0,1:T(2,128)(2,1)S(1)} %reshape.394, f32[2048,512]{1,0:T(8,128)} %fusion.30, f32[2048,512]{1,0:T(8,128)} %fusion.29), kind=kOutput, calls=%fused_computation.19 | convolution fusion | flops 8388608 | bytes 8397824 | tf_op jit(solution)/shard_map/dot_general | solution.py:143
  103.7 5.6 %all-to-all-done.5 = bf16[8,64,128]{2,1,0:T(8,128)(2,1)S(1)} async-done(((bf16[8,64,128]{2,1,0:T(8,128)(2,1)}), bf16[8,64,128]{2,1,0:T(8,128)(2,1)S(1)}, u32[]{:S(2)}, u32[]{:S(2)}) %all-to-all-start.5) | async-done | bytes 131104 | tf_op jit(solution)/shard_map/all_to_all | solution.py:125
  110.0 5.5 %all-to-all-start.3 = ((f32[8,1,2048]{2,1,0:T(1,128)}), f32[8,1,2048]{2,1,0:T(1,128)S(1)}, u32[]{:S(2)}, u32[]{:S(2)}) async-start(f32[8,1,2048]{2,1,0:T(1,128)} %broadcast_in_dim.32), calls=%async_computation.3 | async-start | bytes 131072 | tf_op jit(solution)/shard_map/all_to_all | solution.py:20
  116.7 1.5 convolution_bitcast_fusion
  118.2 7.0 %all-to-all-done.3 = f32[8,1,2048]{2,1,0:T(1,128)S(1)} async-done(((f32[8,1,2048]{2,1,0:T(1,128)}), f32[8,1,2048]{2,1,0:T(1,128)S(1)}, u32[]{:S(2)}, u32[]{:S(2)}) %all-to-all-start.3) | async-done | bytes 65568 | tf_op jit(solution)/shard_map/all_to_all | solution.py:20
  125.3 4.5 %fusion.2 = (bf16[2048,512]{1,0:T(8,128)(2,1)S(1)}, bf16[2048,512]{1,0:T(8,128)(2,1)S(1)}) fusion(f32[2048,512]{1,0:T(8,128)} %fusion.30, f32[2048,512]{1,0:T(8,128)} %fusion.29, f32[512]{0:T(512)S(1)} %convert_element_type.45, f32[2048]{0:T(1024)S(1)} %subtract_multiply_fusion), kind=kLoop, calls=%fused_computation.12 | loop fusion | flops 14680064 | bytes 12593152 | tf_op jit(solution)/shard_map/convert_element_type | solution.py:149
  131.6 1.8 reshape_reshape.4
  133.4 1.7 copy.29
  135.1 7.0 %all_to_all.70 = f32[2,32,5120]{2,1,0:T(8,128)S(1)} all-to-all(f32[2,32,5120]{2,1,0:T(8,128)S(1)} %copy.29), channel_id=1, replica_groups=mesh['dp_0'=4,'dp_1'=4,'dp_2'=2,'dp_3'=2,'emb'=8] {'dp_3'}, dimensions={0} | all-to-all | bytes 2621440 | tf_op jit(solution)/shard_map/all_to_all | solution.py:47
  142.1 1.0 reduce_sum.76
  143.1 2.4 all_to_all.53
  145.5 12.8 %all-to-all-start.7 = ((f32[32,1,5120]{2,1,0:T(1,128)}), f32[32,1,5120]{2,1,0:T(1,128)S(1)}, u32[]{:S(2)}, u32[]{:S(2)}) async-start(f32[32,1,5120]{2,1,0:T(1,128)} %all_to_all.53), calls=%async_computation.7 | async-start | bytes 1310720 | tf_op jit(solution)/shard_map/all_to_all | solution.py:66
  158.3 2.3 fusion.31
  160.6 1.7 convolution_add_fusion
  162.3 29.6 %all-to-all-done.7 = f32[32,1,5120]{2,1,0:T(1,128)S(1)} async-done(((f32[32,1,5120]{2,1,0:T(1,128)}), f32[32,1,5120]{2,1,0:T(1,128)S(1)}, u32[]{:S(2)}, u32[]{:S(2)}) %all-to-all-start.7) | async-done | bytes 655392 | tf_op jit(solution)/shard_map/all_to_all | solution.py:66
  192.0 11.5 %all-to-all-start.10 = ((f32[8,256,128]{2,1,0:T(8,128)}), f32[8,256,128]{2,1,0:T(8,128)S(1)}, u32[]{:S(2)}, u32[]{:S(2)}) async-start(f32[8,256,128]{2,1,0:T(8,128)} %bitcast.26), calls=%async_computation.10 | async-start | bytes 2097152 | tf_op jit(solution)/shard_map/all_to_all | solution.py:47
  203.8 50.1 %all-to-all-done.10 = f32[8,256,128]{2,1,0:T(8,128)S(1)} async-done(((f32[8,256,128]{2,1,0:T(8,128)}), f32[8,256,128]{2,1,0:T(8,128)S(1)}, u32[]{:S(2)}, u32[]{:S(2)}) %all-to-all-start.10) | async-done | bytes 1048608 | tf_op jit(solution)/shard_map/all_to_all | solution.py:47
  254.0 1.2 broadcast_in_dim.35
  255.2 3.9 %all-to-all-start.8 = ((f32[32,1,5120]{2,1,0:T(1,128)}), f32[32,1,5120]{2,1,0:T(1,128)S(1)}, u32[]{:S(2)}, u32[]{:S(2)}) async-start(f32[32,1,5120]{2,1,0:T(1,128)} %broadcast_in_dim.35), calls=%async_computation.8 | async-start | bytes 1310720 | tf_op jit(solution)/shard_map/all_to_all | solution.py:20
  259.3 0.8 fusion.12
  260.1 27.2 %all-to-all-done.8 = f32[32,1,5120]{2,1,0:T(1,128)S(1)} async-done(((f32[32,1,5120]{2,1,0:T(1,128)}), f32[32,1,5120]{2,1,0:T(1,128)S(1)}, u32[]{:S(2)}, u32[]{:S(2)}) %all-to-all-start.8) | async-done | bytes 655392 | tf_op jit(solution)/shard_map/all_to_all | solution.py:20
  287.5 13.8 %all_to_all.71 = f32[2,32,5120]{2,1,0:T(8,128)S(1)} all-to-all(f32[2,32,5120]{2,1,0:T(8,128)S(1)} %broadcast_in_dim.37), channel_id=1, replica_groups=mesh['dp_0'=4,'dp_1'=4,'dp_2'=2,'dp_3'=2,'emb'=8] {'dp_3'}, dimensions={0} | all-to-all | bytes 2621440 | tf_op jit(solution)/shard_map/all_to_all | solution.py:20
  301.3 1.0 copy.30
  302.3 1.0 slice.32
  303.4 2.1 slice.34
  305.5 1.9 slice_multiply_fusion
  307.4 2.4 multiply_subtract_fusion
  (77 shorter events, 6.9 us)
Async XLA Ops:
  0.6 83.8 %copy-start = (bf16[128,512]{1,0:T(8,128)(2,1)S(1)}, bf16[128,512]{1,0:T(8,128)(2,1)}, u32[]{:S(2)}) copy-start(bf16[128,512]{1,0:T(8,128)(2,1)} %param.19) | copy-start | bytes 393220
  0.6 51.6 %copy-start.1 = (s32[12288]{0:T(1024)S(1)}, s32[12288]{0:T(1024)}, u32[]{:S(2)}) copy-start(s32[12288]{0:T(1024)} %param.14) | copy-start | bytes 147460
  0.7 45.1 %copy-start.10 = (f32[128]{0:T(128)S(1)}, f32[128]{0:T(128)}, u32[]{:S(2)}) copy-start(f32[128]{0:T(128)} %param.18) | copy-start | bytes 1540
  0.7 51.5 %copy-start.11 = (bf16[512]{0:T(512)(128)(2,1)S(1)}, bf16[512]{0:T(512)(128)(2,1)}, u32[]{:S(2)}) copy-start(bf16[512]{0:T(512)(128)(2,1)} %param.21) | copy-start | bytes 3076
  0.7 51.5 %copy-start.12 = (s32[256]{0:T(256)S(1)}, s32[256]{0:T(256)}, u32[]{:S(2)}) copy-start(s32[256]{0:T(256)} %param.12) | copy-start | bytes 3076
  31.1 13.6 %all-to-all-start.1 = ((bf16[8,64,128]{2,1,0:T(8,128)(2,1)}), bf16[8,64,128]{2,1,0:T(8,128)(2,1)S(1)}, u32[]{:S(2)}, u32[]{:S(2)}) async-start(bf16[8,64,128]{2,1,0:T(8,128)(2,1)} %select_convert_fusion), calls=%async_computation.1 | async-start | bytes 262144 | tf_op jit(solution)/shard_map/all_to_all | solution.py:113
  45.6 41.5 %copy-start.4 = (bf16[256,128]{1,0:T(8,128)(2,1)}, bf16[256,128]{1,0:T(8,128)(2,1)S(1)}, u32[]{:S(2)}) copy-start(bf16[256,128]{1,0:T(8,128)(2,1)S(1)} %gather_fusion.2) | copy-start | bytes 196612
  46.7 26.2 %all-to-all-start.2 = ((bf16[8,256,128]{2,1,0:T(8,128)(2,1)}), bf16[8,256,128]{2,1,0:T(8,128)(2,1)S(1)}, u32[]{:S(2)}, u32[]{:S(2)}) async-start(bf16[8,256,128]{2,1,0:T(8,128)(2,1)} %broadcast_in_dim.31), calls=%async_computation.2 | async-start | bytes 1048576 | tf_op jit(solution)/shard_map/all_to_all | solution.py:20
  52.2 34.9 %copy-start.7 = (bf16[128,512]{1,0:T(8,128)(2,1)S(1)}, bf16[128,512]{1,0:T(8,128)(2,1)}, u32[]{:S(2)}) copy-start(bf16[128,512]{1,0:T(8,128)(2,1)} %param.20) | copy-start | bytes 393220
  72.9 20.7 %all-to-all-start.4 = ((s32[8,1,64]{2,1,0:T(1,128)}), s32[8,1,64]{2,1,0:T(1,128)S(1)}, u32[]{:S(2)}, u32[]{:S(2)}) async-start(s32[8,1,64]{2,1,0:T(1,128)} %all_to_all.49), calls=%async_computation.4 | async-start | bytes 8192 | tf_op jit(solution)/shard_map/all_to_all | solution.py:126
  93.6 15.7 %all-to-all-start.5 = ((bf16[8,64,128]{2,1,0:T(8,128)(2,1)}), bf16[8,64,128]{2,1,0:T(8,128)(2,1)S(1)}, u32[]{:S(2)}, u32[]{:S(2)}) async-start(bf16[8,64,128]{2,1,0:T(8,128)(2,1)} %bitcast.21), calls=%async_computation.5 | async-start | bytes 262144 | tf_op jit(solution)/shard_map/all_to_all | solution.py:125
  99.1 26.2 %copy-start.9 = (f32[2048]{0:T(1024)S(1)}, f32[2048]{0:T(1024)}, u32[]{:S(2)}) copy-start(f32[2048]{0:T(1024)} %param.17) | copy-start | bytes 24580
  110.0 15.2 %all-to-all-start.3 = ((f32[8,1,2048]{2,1,0:T(1,128)}), f32[8,1,2048]{2,1,0:T(1,128)S(1)}, u32[]{:S(2)}, u32[]{:S(2)}) async-start(f32[8,1,2048]{2,1,0:T(1,128)} %broadcast_in_dim.32), calls=%async_computation.3 | async-start | bytes 131072 | tf_op jit(solution)/shard_map/all_to_all | solution.py:20
  129.8 1.4 copy-start.2
  129.8 1.7 copy-start.6
  143.1 17.5 %copy-start.8 = (bf16[128,512]{1,0:T(8,128)(2,1)S(1)}, bf16[128,512]{1,0:T(8,128)(2,1)}, u32[]{:S(2)}) copy-start(bf16[128,512]{1,0:T(8,128)(2,1)} %param.20) | copy-start | bytes 393220
  145.5 46.4 %all-to-all-start.7 = ((f32[32,1,5120]{2,1,0:T(1,128)}), f32[32,1,5120]{2,1,0:T(1,128)S(1)}, u32[]{:S(2)}, u32[]{:S(2)}) async-start(f32[32,1,5120]{2,1,0:T(1,128)} %all_to_all.53), calls=%async_computation.7 | async-start | bytes 1310720 | tf_op jit(solution)/shard_map/all_to_all | solution.py:66
  162.3 96.8 %copy-start.5 = (bf16[256,128]{1,0:T(8,128)(2,1)S(1)}, bf16[256,128]{1,0:T(8,128)(2,1)}, u32[]{:S(2)}) copy-start(bf16[256,128]{1,0:T(8,128)(2,1)} %copy-done.4) | copy-start | bytes 196612
  192.0 62.0 %all-to-all-start.10 = ((f32[8,256,128]{2,1,0:T(8,128)}), f32[8,256,128]{2,1,0:T(8,128)S(1)}, u32[]{:S(2)}, u32[]{:S(2)}) async-start(f32[8,256,128]{2,1,0:T(8,128)} %bitcast.26), calls=%async_computation.10 | async-start | bytes 2097152 | tf_op jit(solution)/shard_map/all_to_all | solution.py:47
  255.2 32.1 %all-to-all-start.8 = ((f32[32,1,5120]{2,1,0:T(1,128)}), f32[32,1,5120]{2,1,0:T(1,128)S(1)}, u32[]{:S(2)}, u32[]{:S(2)}) async-start(f32[32,1,5120]{2,1,0:T(1,128)} %broadcast_in_dim.35), calls=%async_computation.8 | async-start | bytes 1310720 | tf_op jit(solution)/shard_map/all_to_all | solution.py:20
  302.3 5.1 %copy-start.3 = (f32[1536,128]{1,0:T(8,128)S(1)}, f32[1536,128]{1,0:T(8,128)}, u32[]{:S(2)}) copy-start(f32[1536,128]{1,0:T(8,128)} %param.15) | copy-start | bytes 2359300
where the time goes:
time: 313 us; the launch traced here: 310 us
  waiting for transfers between devices  147 us (47%)
  starting transfers between devices  59.4 us (19%)
  blocking collectives  42.9 us (14%)
  local copies, waits for them, and re-layouts  27.3 us (9%)
  matrix products  16.4 us (5%)
  other arithmetic  15.2 us (5%)
    all_to_all x1, waiting for transfers between devices, sent_and_summed(): lax.all_to_all(pieces, axis, split_axis=0, concat_axis=0, tiled=True)  50.1 us
    all_to_all x3, waiting for transfers between devices, from_everyone(): lax.all_to_all(jnp.broadcast_to(array[None], (length, *array.shape)), axi...  48 us
    all_to_all x1, waiting for transfers between devices, sum_in_two_steps(): return jnp.sum(lax.all_to_all(own, far, 0, 0, tiled=True), axis=0)  29.6 us
    all_to_all x1, blocking collectives, on_device(): lax.all_to_all(requests, 'emb', split_axis=0, concat_axis=0, tiled=True)  22.1 us
    all_to_all x3, starting transfers between devices, from_everyone(): lax.all_to_all(jnp.broadcast_to(array[None], (length, *array.shape)), axi...  14.8 us
    all_to_all x1, blocking collectives, from_everyone(): lax.all_to_all(jnp.broadcast_to(array[None], (length, *array.shape)), axi...  13.8 us
    all_to_all x1, starting transfers between devices, sum_in_two_steps(): return jnp.sum(lax.all_to_all(own, far, 0, 0, tiled=True), axis=0)  12.8 us
    all_to_all x1, starting transfers between devices, on_device(): lax.all_to_all(slot_pack, 'emb', split_axis=0, concat_axis=0, tiled=True)  11.5 us
  transfers between devices with their start and end apart: 8, of which 8 were waited for; matrix products, arithmetic and copies ran while one was open for 8% of the time, Pallas kernels for 0%

commit v1 on v0

v1 whole, which is shorter than its diff:
```python
import math

import jax
import jax.numpy as jnp
from jax import lax
from jax.experimental import pallas as pl
from jax.experimental.pallas import tpu as pltpu
from jax.sharding import Mesh
from jax.sharding import PartitionSpec as P

DP = ("x", "y", "zh", "core")
DP_EMB = ("x", "y", "zh", "core", "emb")
XY = ("x", "y")
ZZ = ("zh", "emb")

loss_weight = 64.0
learn_rate = 0.1
norm_eps = 1e-06

bf16 = jnp.bfloat16
f32 = jnp.float32


def exchange(pieces, axis):
    return lax.all_to_all(pieces, axis, 0, 0, tiled=True)


def to_all(array, axis):
    return exchange(jnp.broadcast_to(array[None], (lax.axis_size(axis), *array.shape)), axis)


def dot32(a, b):
    return jnp.dot(a, b, preferred_element_type=f32)


def placed(ids, row_place):
    lanes = 128
    grid = row_place.reshape(-1, lanes)
    parts = jnp.concatenate([grid // lanes, grid % lanes], axis=1).astype(bf16)
    pick = (ids[:, None] // lanes == jnp.arange(grid.shape[0], dtype=jnp.int32)[None, :]).astype(bf16)
    lines = dot32(pick, parts)
    lane = ids[:, None] % lanes == jnp.arange(lanes, dtype=jnp.int32)[None, :]
    high = jnp.sum(jnp.where(lane, lines[:, :lanes], 0.0), axis=1)
    low = jnp.sum(jnp.where(lane, lines[:, lanes:], 0.0), axis=1)
    return high.astype(jnp.int32) * lanes + low.astype(jnp.int32)


def slots_of(place, rows_shard, capacity, shards):
    owner = place // rows_shard
    slot = place % rows_shard
    match = owner[:, None] == jnp.arange(shards, dtype=jnp.int32)[None, :]
    n = place.shape[0]
    before = (
        jnp.arange(n, dtype=jnp.int32)[:, None] >= jnp.arange(n, dtype=jnp.int32)[None, :]
    ).astype(bf16)
    counts = dot32(before, match.astype(bf16))
    rank = jnp.sum(jnp.where(match, counts, 0.0), axis=1).astype(jnp.int32) - 1
    return slot, owner * capacity + rank


def coded(slot):
    return jnp.stack([slot // 128 + 1, slot % 128], axis=1).astype(bf16)


def code_line(packed, shards, capacity):
    return packed.astype(bf16).reshape(shards, capacity, 2).swapaxes(1, 2).reshape(shards, 1, -1)


def decoded(line, capacity):
    values = line.astype(jnp.int32)
    return ((values[..., :capacity] - 1) * 128 + values[..., capacity:]).reshape(-1)


def tower_kernel(
    answers_ref, target_ref, weights_ref, w_out_ref, gain_ref, labels_ref,
    emb_grad_ref, grads_ref, gate_s, up_s, sig_s,
):
    tok = target_ref.shape[0]
    width = answers_ref.shape[1]
    shards = w_out_ref.shape[0]
    slot_lane = lax.broadcasted_iota(jnp.int32, (tok, answers_ref.shape[0]), 1)
    pick = jnp.where(target_ref[...] == slot_lane, 1.0, 0.0).astype(bf16)
    values = dot32(pick, answers_ref[...])
    inverse_rms = lax.rsqrt(jnp.mean(values * values, axis=1, keepdims=True) + norm_eps)
    gain = gain_ref[...]
    normed = (values * inverse_rms * gain).astype(bf16)
    normed_t = (values * inverse_rms * gain).T.astype(bf16)

    def block(shard, half, side):
        tiles = []
        for tile in (2 * half, 2 * half + 1):
            quarters = [
                weights_ref[side, pl.ds((tile * 4 + k) * shards * 32 + shard * 32, 32), :]
                for k in range(4)
            ]
            tiles.append(jnp.concatenate(quarters, axis=0))
        return jnp.concatenate(tiles, axis=1)

    def forward(shard, total):
        for half in range(2):
            at = shard * 2 + half
            gate = dot32(normed, block(shard, half, 0))
            up = dot32(normed, block(shard, half, 1))
            sig = jax.nn.sigmoid(gate)
            gate_s[at] = gate
            up_s[at] = up
            sig_s[at] = sig
            hidden = (gate * sig * up).astype(bf16).astype(f32)
            for j in range(2):
                out = w_out_ref[shard, pl.ds(2 * half + j, 1), :].astype(f32)
                total = total + hidden[:, j * 128 : (j + 1) * 128] * out
        return total

    total = lax.fori_loop(0, shards, forward, jnp.zeros((tok, 128), f32))
    logits = jnp.sum(total, axis=1, keepdims=True)
    slopes = loss_weight * (jax.nn.sigmoid(logits) - labels_ref[...])

    across = (((1,), (1,)), ((), ()))

    def backward(shard, back):
        for half in range(2):
            at = shard * 2 + half
            gate = gate_s[at]
            up = up_s[at]
            sig = sig_s[at]
            out = jnp.concatenate(
                [w_out_ref[shard, pl.ds(2 * half + j, 1), :].astype(f32) for j in range(2)], axis=1
            )
            back_hidden = slopes * out
            back_gate = (back_hidden * up * sig * (1.0 + gate * (1.0 - sig))).astype(bf16)
            back_up = (back_hidden * (gate * sig)).astype(bf16)
            for side, part in ((0, back_gate), (1, back_up)):
                back = back + lax.dot_general(
                    part, block(shard, half, side), across, preferred_element_type=f32
                )
                grad = dot32(normed_t, part).astype(bf16)
                for j in range(2):
                    tile = 2 * half + j
                    for k in range(4):
                        grads_ref[
                            side, pl.ds((tile * 4 + k) * shards * 32 + shard * 32, 32), :
                        ] = grad[k * 32 : (k + 1) * 32, j * 128 : (j + 1) * 128]
        return back

    back = lax.fori_loop(0, shards, backward, jnp.zeros((tok, width), f32))
    scaled = back * gain
    emb_grad_ref[...] = inverse_rms * scaled - values * (
        inverse_rms * inverse_rms * inverse_rms
    ) * jnp.mean(values * scaled, axis=1, keepdims=True)


def tower(answers, target, weights, w_out, gain, labels):
    tok = target.shape[0]
    width = answers.shape[1]
    shards = w_out.shape[0]
    vmem = pl.BlockSpec(memory_space=pltpu.VMEM)
    return pl.pallas_call(
        tower_kernel,
        out_shape=(
            jax.ShapeDtypeStruct((tok, width), f32),
            jax.ShapeDtypeStruct((2, shards * 512, width), bf16),
        ),
        in_specs=[vmem] * 6,
        out_specs=(vmem, vmem),
        scratch_shapes=[pltpu.VMEM((2 * shards, tok, 256), f32)] * 3,
        compiler_params=pltpu.CompilerParams(vmem_limit_bytes=40 * 1024 * 1024),
        cost_estimate=pl.CostEstimate(
            flops=6 * 2 * tok * width * 4096, bytes_accessed=5 << 20, transcendentals=2 << 20
        ),
        name="tower",
    )(answers, target.reshape(-1, 1), weights, w_out, gain.reshape(1, -1), labels.reshape(-1, 1))


def on_device(
    cur_ids, prev_ids, prev_grads, row_place, table, accum, labels, gain, w_gate, w_up, w_out
):
    shards = lax.axis_size("emb")
    plane = lax.axis_size(XY)
    rows_shard, width = table.shape
    tok = cur_ids.shape[0]
    capacity = min(tok, 2 * tok // shards)
    slots = shards * capacity

    place = placed(jnp.concatenate([cur_ids, prev_ids]), row_place)
    cur_slot, cur_pos = slots_of(place[:tok], rows_shard, capacity, shards)
    prev_slot, prev_pos = slots_of(place[tok:], rows_shard, capacity, shards)
    slot_ids = jnp.arange(slots, dtype=jnp.int32)[:, None]
    cur_pack = (slot_ids == cur_pos[None, :]).astype(bf16)
    prev_pack = (slot_ids == prev_pos[None, :]).astype(bf16)
    cur_codes = code_line(dot32(cur_pack, coded(cur_slot)), shards, capacity)
    prev_codes = code_line(dot32(prev_pack, coded(prev_slot)), shards, capacity)
    prev_rows = dot32(prev_pack, prev_grads).astype(bf16).reshape(shards, capacity, width)

    at = lax.axis_index(XY)
    own_side = jnp.where(lax.axis_index("core") == 0, w_gate, w_up)
    own_slice = lax.dynamic_slice(own_side, ((at % 4) * 32, (at // 4) * 128), (32, 128))
    shared = jnp.concatenate(
        [own_slice, w_out.reshape(4, 128), jnp.zeros((10, 128), bf16)], axis=0
    )
    first = exchange(
        jnp.concatenate(
            [
                prev_rows,
                jnp.broadcast_to(shared[None], (shards, *shared.shape)),
                cur_codes,
                prev_codes,
            ],
            axis=1,
        ),
        "emb",
    )
    got_rows = first[:, :capacity].reshape(slots, width)
    got_slice = first[:, capacity : capacity + 32].reshape(shards * 32, 128)
    all_out = first[:, capacity + 32 : capacity + 36]
    wanted = decoded(first[:, capacity + 46], capacity)
    got_slots = decoded(first[:, capacity + 47], capacity)

    row_ids = jnp.arange(rows_shard, dtype=jnp.int32)
    fetched = dot32(
        (wanted[:, None] == row_ids[None, :]).astype(bf16), table.astype(bf16)
    ).astype(bf16)
    table_grad = dot32((row_ids[:, None] == got_slots[None, :]).astype(bf16), got_rows)

    grad_piece = rows_shard // plane
    second = exchange(
        jnp.concatenate(
            [
                jnp.broadcast_to(got_slice[None], (plane, *got_slice.shape)),
                table_grad.astype(bf16).reshape(plane, grad_piece, width),
            ],
            axis=1,
        ),
        XY,
    )
    answers = exchange(fetched.reshape(shards, capacity, width), "emb").reshape(slots, width)

    lines = plane * shards * 32
    own_weights = second[:, : shards * 32].reshape(lines, 128)
    plane_grad = second[:, shards * 32 :].astype(f32).sum(axis=0).astype(bf16)
    third = exchange(
        jnp.concatenate(
            [
                jnp.broadcast_to(own_weights[None], (2, lines, 128)),
                plane_grad.reshape(2, grad_piece // 2, width),
            ],
            axis=1,
        ),
        "core",
    )
    my_labels = lax.dynamic_slice(labels, (lax.axis_index("emb") * tok,), (tok,))
    emb_grad, tower_grads = tower(answers, cur_pos, third, all_out, gain, my_labels)

    half_grad = third[:, lines:].astype(f32).sum(axis=0)
    half_grad = half_grad + lax.ppermute(half_grad, "zh", [(0, 1), (1, 0)])

    core_sum = exchange(tower_grads, "core").astype(f32).sum(axis=0).astype(bf16)
    fourth = exchange(
        jnp.concatenate(
            [
                core_sum.reshape(plane, shards * 32, 128),
                jnp.broadcast_to(half_grad.astype(bf16)[None], (plane, *half_grad.shape)),
            ],
            axis=1,
        ),
        XY,
    )
    plane_sum = fourth[:, : shards * 32].astype(f32).sum(axis=0).astype(bf16)
    got_grad = fourth[:, shards * 32 :].reshape(rows_shard // 2, width)
    for_z = jnp.broadcast_to(plane_sum.reshape(1, shards, 32, 128), (2, shards, 32, 128))
    tower_sum = exchange(for_z.reshape(2 * shards, 32, 128), ZZ).astype(f32).sum(axis=0)
    side = to_all(tower_sum.astype(bf16), XY).reshape(plane * 32, 128)
    last = to_all(jnp.concatenate([side, got_grad], axis=0), "core")

    tower_scale = 1.0 / math.sqrt(tok * shards * lax.axis_size(DP))
    both = last[:, : plane * 32].astype(f32) * tower_scale
    both = both.reshape(2, 4, 128, 128).swapaxes(1, 2).reshape(2, 128, 512)
    total_grad = (
        last[:, plane * 32 :]
        .reshape(2, plane, grad_piece // 2, width)
        .swapaxes(0, 1)
        .reshape(rows_shard, width)
        .astype(f32)
    )
    new_accum = accum + total_grad * total_grad
    new_table = table - learn_rate * total_grad * lax.rsqrt(new_accum)
    return (new_table, new_accum, both[0], both[1], emb_grad)


def solution(mesh):
    torus = Mesh(mesh.devices.reshape(4, 4, 2, 2, mesh.shape["emb"]), DP_EMB)
    return jax.shard_map(
        on_device,
        mesh=torus,
        in_specs=(
            P(DP_EMB),
            P(DP_EMB),
            P(DP_EMB, None),
            P(),
            P("emb", None),
            P("emb", None),
            P(DP),
            P(),
            P(None, "emb"),
            P(None, "emb"),
            P("emb"),
        ),
        out_specs=(P("emb", None), P("emb", None), P(None, "emb"), P(None, "emb"), P(DP_EMB, None)),
        check_vma=False,
    )
```

time: 313 us -> 170 us (0.54)
  waiting for transfers between devices: 147 us -> 23.7 us
  blocking collectives: 42.9 us -> 92.6 us
  starting transfers between devices: 59.4 us -> 26.9 us
  local copies, waits for them, and re-layouts: 27.3 us -> 7.51 us
  matrix products: 16.4 us -> 3.34 us
  other arithmetic: 15.2 us -> 6.9 us
  Pallas kernels: 0 us -> 7.42 us
    all_to_all x8 -> x3, waiting for transfers between devices: 147 us -> 23.7 us  [exchange(): return lax.all_to_all(pieces, axis, 0, 0, tiled=True)]
    all_to_all x3 -> x6, blocking collectives: 42.9 us -> 92.6 us  [exchange(): return lax.all_to_all(pieces, axis, 0, 0, tiled=True)]
    all_to_all x8 -> x3, starting transfers between devices: 59.4 us -> 18.9 us  [exchange(): return lax.all_to_all(pieces, axis, 0, 0, tiled=True)]
    dot_general x8, matrix products: 16.4 us -> 3.34 us  [dot32(): return jnp.dot(a, b, preferred_element_type=f32)]
    ppermute x0 -> x1, starting transfers between devices: none -> 7.95 us  [on_device(): half_grad = half_grad + lax.ppermute(half_grad, 'zh', [(0, 1), (1, 0)])]
    pallas_call x0 -> x1, Pallas kernels: none -> 7.42 us  [tower(): pl.pallas_call(tower_kernel, out_shape=(jax.ShapeDtypeStruct((tok, width)...]
    gather x4 -> x0, local copies, waits for them, and re-layouts: 6.79 us -> none  [the longest x1 2.18 us: on_device(): fetched = table[jnp.maximum(wanted, 0)]]
    convert_element_type x6 -> x2, other arithmetic: 5.41 us -> 0.01 us  [the longest x1 0.01 us: on_device(): half_grad.astype(bf16)[None]]
  transfers between devices with their start and end apart: 8 -> 4, of which waited for: 8 -> 3; matrix products, arithmetic and copies ran while one was open for 8% -> 2% of each run, Pallas kernels for 0% -> 4%
where the time goes in v1:
time: 170 us; the launch traced here: 169 us
  blocking collectives  92.6 us (54%)
  starting transfers between devices  26.9 us (16%)
  waiting for transfers between devices  23.7 us (14%)
  local copies, waits for them, and re-layouts  7.51 us (4%)
  Pallas kernels  7.42 us (4%)
  other arithmetic  6.9 us (4%)
  matrix products  3.34 us (2%)
    all_to_all x6, blocking collectives, exchange(): return lax.all_to_all(pieces, axis, 0, 0, tiled=True)  92.6 us
    all_to_all x3, waiting for transfers between devices, exchange(): return lax.all_to_all(pieces, axis, 0, 0, tiled=True)  23.7 us
    all_to_all x3, starting transfers between devices, exchange(): return lax.all_to_all(pieces, axis, 0, 0, tiled=True)  18.9 us
    ppermute x1, starting transfers between devices, on_device(): half_grad = half_grad + lax.ppermute(half_grad, 'zh', [(0, 1), (1, 0)])  7.95 us
    pallas_call x1, Pallas kernels, tower(): pl.pallas_call(tower_kernel, out_shape=(jax.ShapeDtypeStruct((tok, width)...  7.42 us
    unnamed x13, local copies, waits for them, and re-layouts  3.49 us
  transfers between devices with their start and end apart: 4, of which 3 were waited for; matrix products, arithmetic and copies ran while one was open for 2% of the time, Pallas kernels for 4%

profile of v1, /device:TPU:1, one launch (start us, length us, event | category | flops | bytes accessed | tf_op | source)
XLA Modules:
  0.0 169.4 jit_solution(1035533189530579867)
XLA Ops:
  0.7 0.7 constant_dynamic-update-slice_fusion.1
  1.4 0.7 constant_dynamic-update-slice_fusion
  2.1 0.9 fusion.17
  3.0 0.3 fusion.15
  3.5 0.2 fusion.7
  3.7 0.2 fusion.6
  3.9 0.2 convolution_convert_fusion.1
  4.2 0.1 reshape.264
  4.3 0.2 convolution_convert_fusion.2
  4.6 0.1 reshape.263
  4.7 0.2 convolution_convert_fusion
  5.0 0.7 dynamic-slice_select_fusion
  5.8 0.8 maximum_maximum_fusion
  6.6 24.5 %all_to_all.45 = bf16[8,112,128]{2,1,0:T(8,128)(2,1)S(1)} all-to-all(bf16[8,112,128]{2,1,0:T(8,128)(2,1)S(1)} %pad_maximum_fusion.4), channel_id=1, replica_groups=mesh['x'=4,'y'=4,'zh'=2,'core'=2,'emb'=8] {'emb'}, dimensions={0} | all-to-all | bytes 458752 | tf_op jit(solution)/shard_map/all_to_all | solution.py:25
  31.3 0.6 fusion.2
  31.9 0.2 broadcast_in_dim.37
  32.1 1.2 pad_maximum_fusion.1
  33.3 6.9 %all-to-all-start.2 = ((bf16[16,352,128]{2,1,0:T(8,128)(2,1)}), bf16[16,352,128]{2,1,0:T(8,128)(2,1)S(1)}, u32[]{:S(2)}, u32[]{:S(2)}) async-start(bf16[16,352,128]{2,1,0:T(8,128)(2,1)} %pad_maximum_fusion.1), calls=%async_computation.2 | async-start | bytes 2883584 | tf_op jit(solution)/shard_map/all_to_all | solution.py:25
  40.4 1.3 fusion.5
  41.7 15.7 %all-to-all-done.2 = bf16[16,352,128]{2,1,0:T(8,128)(2,1)S(1)} async-done(((bf16[16,352,128]{2,1,0:T(8,128)(2,1)}), bf16[16,352,128]{2,1,0:T(8,128)(2,1)S(1)}, u32[]{:S(2)}, u32[]{:S(2)}) %all-to-all-start.2) | async-done | bytes 1441824 | tf_op jit(solution)/shard_map/all_to_all | solution.py:25
  57.5 0.1 slice.96
  57.6 0.1 broadcast_in_dim.39
  57.8 0.1 pad_maximum_fusion
  57.9 11.0 %all_to_all.46.weights_ref = bf16[2,4144,128]{2,1,0:T(8,128)(2,1)S(1)} all-to-all(bf16[2,4144,128]{2,1,0:T(8,128)(2,1)S(1)} %pad_maximum_fusion), channel_id=1, replica_groups=mesh['x'=4,'y'=4,'zh'=2,'core'=2,'emb'=8] {'core'}, dimensions={0} | all-to-all | bytes 4243456 | tf_op jit(solution)/shard_map/all_to_all | solution.py:25
  69.0 8.4 %all-to-all-start.1 = ((bf16[8,64,128]{2,1,0:T(8,128)(2,1)}), bf16[8,64,128]{2,1,0:T(8,128)(2,1)S(1)}, u32[]{:S(2)}, u32[]{:S(2)}) async-start(bf16[8,64,128]{2,1,0:T(8,128)(2,1)} %bitcast.7), calls=%async_computation.1 | async-start | bytes 262144 | tf_op jit(solution)/shard_map/all_to_all | solution.py:25
  77.3 0.8 dynamic_slice.7
  78.1 0.1 copy.45.labels_ref
  78.3 0.1 copy.44.target_ref
  78.4 7.9 %collective-permute-start = (f32[48,128]{1,0:T(8,128)S(1)}, f32[48,128]{1,0:T(8,128)S(1)}, u32[]{:S(2)}, u32[]{:S(2)}) collective-permute-start(f32[48,128]{1,0:T(8,128)S(1)} %convert_reduce_fusion), channel_id=1, source_target_pairs={{0,16},{16,0},{1,17},{17,1},{2,18},{18,2},{3,19},{19,3},{4,20},{20... | collective-permute-start | bytes 73736 | tf_op jit(solution)/shard_map/ppermute | solution.py:254
  86.4 1.3 all-to-all-done.1
  87.7 7.4 %tower.1 = (f32[256,128]{1,0:T(8,128)}, bf16[2,4096,128]{2,1,0:T(8,128)(2,1)S(1)}) custom-call(bf16[512,128]{1,0:T(8,128)(2,1)S(1)} %bitcast.79, s32[256,1]{1,0:T(8,128)S(1)} %copy.44.target_ref, bf16[2,4144,128]{2,1,0:T(8,128)(2,1)S(1)} %all_to_all.46.weights_ref, bf16[8,4,128]{2,1,0:T(4,128)(2,1)S(1)} %slice.98.w_out_ref, f32[1,128]{1,0:T(1,128)S(1)} %bitcast.80, ...), custom_call_target="tpu_custom_call" | custom-call | flops 1610612736 | bytes 5242880 | tf_op jit(solution)/shard_map/tower/pallas_call | solution.py:157
  95.1 7.6 %all_to_all.47 = bf16[2,4096,128]{2,1,0:T(8,128)(2,1)S(1)} all-to-all(bf16[2,4096,128]{2,1,0:T(8,128)(2,1)S(1)} %get-tuple-element.7), channel_id=1, replica_groups=mesh['x'=4,'y'=4,'zh'=2,'core'=2,'emb'=8] {'core'}, dimensions={0} | all-to-all | bytes 4194304 | tf_op jit(solution)/shard_map/all_to_all | solution.py:25
  102.7 1.1 reduce_sum.98
  104.0 21.0 %all_to_all.48 = bf16[16,304,128]{2,1,0:T(8,128)(2,1)S(1)} all-to-all(bf16[16,304,128]{2,1,0:T(8,128)(2,1)S(1)} %pad_maximum_fusion.2), channel_id=1, replica_groups=mesh['x'=4,'y'=4,'zh'=2,'core'=2,'emb'=8] {'x','y'}, dimensions={0} | all-to-all | bytes 2490368 | tf_op jit(solution)/shard_map/all_to_all | solution.py:25
  125.0 0.1 slice_reduce_fusion
  125.2 19.2 %all_to_all.49 = bf16[16,32,128]{2,1,0:T(8,128)(2,1)S(1)} all-to-all(bf16[16,32,128]{2,1,0:T(8,128)(2,1)S(1)} %bitcast.90), channel_id=1, replica_groups=mesh['x'=4,'y'=4,'zh'=2,'core'=2,'emb'=8] {'zh','emb'}, dimensions={0} | all-to-all | bytes 262144 | tf_op jit(solution)/shard_map/all_to_all | solution.py:25
  144.4 0.7 broadcast_in_dim.43
  145.1 3.7 %all-to-all-start.7 = ((bf16[16,32,128]{2,1,0:T(8,128)(2,1)}), bf16[16,32,128]{2,1,0:T(8,128)(2,1)S(1)}, u32[]{:S(2)}, u32[]{:S(2)}) async-start(bf16[16,32,128]{2,1,0:T(8,128)(2,1)} %broadcast_in_dim.43), calls=%async_computation.7 | async-start | bytes 262144 | tf_op jit(solution)/shard_map/all_to_all | solution.py:25
  148.8 6.7 %all-to-all-done.7 = bf16[16,32,128]{2,1,0:T(8,128)(2,1)S(1)} async-done(((bf16[16,32,128]{2,1,0:T(8,128)(2,1)}), bf16[16,32,128]{2,1,0:T(8,128)(2,1)S(1)}, u32[]{:S(2)}, u32[]{:S(2)}) %all-to-all-start.7) | async-done | bytes 131104 | tf_op jit(solution)/shard_map/all_to_all | solution.py:25
  155.5 9.2 %all_to_all.50 = bf16[2,1280,128]{2,1,0:T(8,128)(2,1)S(1)} all-to-all(bf16[2,1280,128]{2,1,0:T(8,128)(2,1)S(1)} %broadcast_in_dim.44), channel_id=1, replica_groups=mesh['x'=4,'y'=4,'zh'=2,'core'=2,'emb'=8] {'core'}, dimensions={0} | all-to-all | bytes 1310720 | tf_op jit(solution)/shard_map/all_to_all | solution.py:25
  164.8 0.1 copy.49
  165.0 0.8 copy.51
  165.8 0.1 copy.48
  165.9 0.8 copy.50
  166.8 0.1 convert_multiply_fusion
  167.0 0.9 copy-done.3
  167.9 0.2 copy-done.4
  168.1 1.3 fusion.8
  (51 shorter events, 1.4 us)
Async XLA Ops:
  0.6 4.1 %copy-start = (bf16[256,128]{1,0:T(8,128)(2,1)S(1)}, bf16[256,128]{1,0:T(8,128)(2,1)}, u32[]{:S(2)}) copy-start(bf16[256,128]{1,0:T(8,128)(2,1)} %param.13) | copy-start | bytes 196612
  33.3 7.1 %copy-start.2 = (f32[1536,128]{1,0:T(8,128)S(1)}, f32[1536,128]{1,0:T(8,128)}, u32[]{:S(2)}) copy-start(f32[1536,128]{1,0:T(8,128)} %param.15) | copy-start | bytes 2359300
  33.3 24.1 %all-to-all-start.2 = ((bf16[16,352,128]{2,1,0:T(8,128)(2,1)}), bf16[16,352,128]{2,1,0:T(8,128)(2,1)S(1)}, u32[]{:S(2)}, u32[]{:S(2)}) async-start(bf16[16,352,128]{2,1,0:T(8,128)(2,1)} %pad_maximum_fusion.1), calls=%async_computation.2 | async-start | bytes 2883584 | tf_op jit(solution)/shard_map/all_to_all | solution.py:25
  57.9 29.8 %copy-start.1 = (f32[128]{0:T(128)S(1)}, f32[128]{0:T(128)}, u32[]{:S(2)}) copy-start(f32[128]{0:T(128)} %param.18) | copy-start | bytes 1540
  69.0 18.7 %all-to-all-start.1 = ((bf16[8,64,128]{2,1,0:T(8,128)(2,1)}), bf16[8,64,128]{2,1,0:T(8,128)(2,1)S(1)}, u32[]{:S(2)}, u32[]{:S(2)}) async-start(bf16[8,64,128]{2,1,0:T(8,128)(2,1)} %bitcast.7), calls=%async_computation.1 | async-start | bytes 262144 | tf_op jit(solution)/shard_map/all_to_all | solution.py:25
  78.4 25.4 %collective-permute-start = (f32[48,128]{1,0:T(8,128)S(1)}, f32[48,128]{1,0:T(8,128)S(1)}, u32[]{:S(2)}, u32[]{:S(2)}) collective-permute-start(f32[48,128]{1,0:T(8,128)S(1)} %convert_reduce_fusion), channel_id=1, source_target_pairs={{0,16},{16,0},{1,17},{17,1},{2,18},{18,2},{3,19},{19,3},{4,20},{20... | collective-permute-start | bytes 73736 | tf_op jit(solution)/shard_map/ppermute | solution.py:254
  145.1 10.4 %all-to-all-start.7 = ((bf16[16,32,128]{2,1,0:T(8,128)(2,1)}), bf16[16,32,128]{2,1,0:T(8,128)(2,1)S(1)}, u32[]{:S(2)}, u32[]{:S(2)}) async-start(bf16[16,32,128]{2,1,0:T(8,128)(2,1)} %broadcast_in_dim.43), calls=%async_computation.7 | async-start | bytes 262144 | tf_op jit(solution)/shard_map/all_to_all | solution.py:25
  166.8 1.1 copy-start.3
  166.8 1.4 copy-start.4

commit v2 on v1

v2 whole, which is shorter than its diff:
```python
import math

import jax
import jax.numpy as jnp
from jax import lax
from jax.experimental import pallas as pl
from jax.experimental.pallas import tpu as pltpu
from jax.sharding import Mesh
from jax.sharding import PartitionSpec as P


DP = ("x", "y", "zh", "core")
DP_EMB = ("x", "y", "zh", "core", "emb")
XY = ("x", "y")
ZZ = ("zh", "emb")

loss_weight = 64.0
learn_rate = 0.1
norm_eps = 1e-06

bf16 = jnp.bfloat16
f32 = jnp.float32


def exchange(pieces, axis):
    return lax.all_to_all(pieces, axis, 0, 0, tiled=True)


def to_all(array, axis):
    return exchange(jnp.broadcast_to(array[None], (lax.axis_size(axis), *array.shape)), axis)


def dot32(a, b):
    return jnp.dot(a, b, preferred_element_type=f32)


def placed(ids, row_place):
    lanes = 128
    grid = row_place.reshape(-1, lanes)
    parts = jnp.concatenate([grid // lanes, grid % lanes], axis=1).astype(bf16)
    pick = (ids[:, None] // lanes == jnp.arange(grid.shape[0], dtype=jnp.int32)[None, :]).astype(bf16)
    lines = dot32(pick, parts)
    lane = ids[:, None] % lanes == jnp.arange(lanes, dtype=jnp.int32)[None, :]
    high = jnp.sum(jnp.where(lane, lines[:, :lanes], 0.0), axis=1)
    low = jnp.sum(jnp.where(lane, lines[:, lanes:], 0.0), axis=1)
    return high.astype(jnp.int32) * lanes + low.astype(jnp.int32)


def slots_of(place, rows_shard, capacity, shards):
    owner = place // rows_shard
    slot = place % rows_shard
    match = owner[:, None] == jnp.arange(shards, dtype=jnp.int32)[None, :]
    n = place.shape[0]
    before = (
        jnp.arange(n, dtype=jnp.int32)[:, None] >= jnp.arange(n, dtype=jnp.int32)[None, :]
    ).astype(bf16)
    counts = dot32(before, match.astype(bf16))
    rank = jnp.sum(jnp.where(match, counts, 0.0), axis=1).astype(jnp.int32) - 1
    return slot, owner * capacity + rank


def coded(slot):
    return jnp.stack([slot // 128 + 1, slot % 128], axis=1).astype(bf16)


def code_line(packed, shards, capacity):
    return packed.astype(bf16).reshape(shards, capacity, 2).swapaxes(1, 2).reshape(shards, 1, -1)


def decoded(line, capacity):
    values = line.astype(jnp.int32)
    return ((values[..., :capacity] - 1) * 128 + values[..., capacity:]).reshape(-1)


def tower_kernel(
    here_ref, answers_ref, target_ref, own_ref, other_ref, w_gate_ref, w_up_ref, w_out_ref,
    gain_ref, labels_ref, emb_grad_ref, grads_ref, weights_s, gate_s, up_s, sig_s,
):
    tok = target_ref.shape[0]
    width = answers_ref.shape[1]
    shards = w_out_ref.shape[0]
    core = here_ref[0]
    home = here_ref[1]
    weights_s[core] = own_ref[...]
    weights_s[1 - core] = other_ref[...]
    slot_lane = lax.broadcasted_iota(jnp.int32, (tok, answers_ref.shape[0]), 1)
    pick = jnp.where(target_ref[...] == slot_lane, 1.0, 0.0).astype(bf16)
    values = dot32(pick, answers_ref[...])
    inverse_rms = lax.rsqrt(jnp.mean(values * values, axis=1, keepdims=True) + norm_eps)
    gain = gain_ref[...]
    normed_wide = values * inverse_rms * gain
    normed = normed_wide.astype(bf16)
    normed_t = normed_wide.T.astype(bf16)

    def far_block(hop, half, side):
        tiles = []
        for tile in (2 * half, 2 * half + 1):
            quarters = [
                weights_s[side, pl.ds((tile * 4 + k) * (shards - 1) * 32 + hop * 32, 32), :]
                for k in range(4)
            ]
            tiles.append(jnp.concatenate(quarters, axis=0))
        return jnp.concatenate(tiles, axis=1)

    def home_block(hop, half, side):
        return (w_gate_ref, w_up_ref)[side][:, half * 256 : (half + 1) * 256]

    def out_row(shard, half, j):
        return w_out_ref[shard, pl.ds(2 * half + j, 1), :].astype(f32)

    def forward(hop, total, block):
        shard = (home + 1 + hop) % shards
        for half in range(2):
            at = hop * 2 + half
            gate = dot32(normed, block(hop, half, 0))
            up = dot32(normed, block(hop, half, 1))
            sig = jax.nn.sigmoid(gate)
            gate_s[at] = gate
            up_s[at] = up
            sig_s[at] = sig
            hidden = (gate * sig * up).astype(bf16).astype(f32)
            for j in range(2):
                total = total + hidden[:, j * 128 : (j + 1) * 128] * out_row(shard, half, j)
        return total

    total = forward(shards - 1, jnp.zeros((tok, 128), f32), home_block)
    total = lax.fori_loop(0, shards - 1, lambda hop, t: forward(hop, t, far_block), total)
    logits = jnp.sum(total, axis=1, keepdims=True)
    slopes = loss_weight * (jax.nn.sigmoid(logits) - labels_ref[...])

    across = (((1,), (1,)), ((), ()))

    def backward(hop, back, block):
        shard = (home + 1 + hop) % shards
        for half in range(2):
            at = hop * 2 + half
            gate = gate_s[at]
            up = up_s[at]
            sig = sig_s[at]
            out = jnp.concatenate([out_row(shard, half, j) for j in range(2)], axis=1)
            back_hidden = slopes * out
            back_gate = (back_hidden * up * sig * (1.0 + gate * (1.0 - sig))).astype(bf16)
            back_up = (back_hidden * (gate * sig)).astype(bf16)
            for side, part in ((0, back_gate), (1, back_up)):
                back = back + lax.dot_general(
                    part, block(hop, half, side), across, preferred_element_type=f32
                )
                grad = dot32(normed_t, part).astype(bf16)
                place = core if side == 0 else 1 - core
                for j in range(2):
                    tile = 2 * half + j
                    for k in range(4):
                        grads_ref[
                            place, pl.ds((tile * 4 + k) * shards * 32 + shard * 32, 32), :
                        ] = grad[k * 32 : (k + 1) * 32, j * 128 : (j + 1) * 128]
        return back

    back = backward(shards - 1, jnp.zeros((tok, width), f32), home_block)
    back = lax.fori_loop(0, shards - 1, lambda hop, b: backward(hop, b, far_block), back)
    scaled = back * gain
    emb_grad_ref[...] = inverse_rms * scaled - values * (
        inverse_rms * inverse_rms * inverse_rms
    ) * jnp.mean(values * scaled, axis=1, keepdims=True)


def tower(here, answers, target, own, other, w_gate, w_up, w_out, gain, labels):
    tok = target.shape[0]
    width = answers.shape[1]
    shards = w_out.shape[0]
    vmem = pl.BlockSpec(memory_space=pltpu.VMEM)
    return pl.pallas_call(
        tower_kernel,
        out_shape=(
            jax.ShapeDtypeStruct((tok, width), f32),
            jax.ShapeDtypeStruct((2, shards * 512, width), bf16),
        ),
        in_specs=[pl.BlockSpec(memory_space=pltpu.SMEM)] + [vmem] * 9,
        out_specs=(vmem, vmem),
        scratch_shapes=[pltpu.VMEM((2, *own.shape), bf16)]
        + [pltpu.VMEM((2 * shards, tok, 256), f32)] * 3,
        compiler_params=pltpu.CompilerParams(vmem_limit_bytes=24 * 1024 * 1024),
        cost_estimate=pl.CostEstimate(
            flops=6 * 2 * tok * width * 4096, bytes_accessed=5 << 20, transcendentals=2 << 20
        ),
        name="tower",
    )(
        here, answers, target.reshape(-1, 1), own, other, w_gate, w_up, w_out,
        gain.reshape(1, -1), labels.reshape(-1, 1),
    )


def update_kernel(
    here_ref, own_ref, other_ref, table_ref, accum_ref,
    new_table_ref, new_accum_ref, gate_ref, up_ref, both_s, *, scale,
):
    core = here_ref[0]
    both_s[core] = own_ref[...]
    both_s[1 - core] = other_ref[...]
    plane, lines = own_ref.shape[:2]
    span = lines - 32
    for side, out_ref in ((0, gate_ref), (1, up_ref)):
        for q in range(plane):
            tile, k = q // 4, q % 4
            out_ref[k * 32 : (k + 1) * 32, tile * 128 : (tile + 1) * 128] = (
                both_s[side, q, :32, :].astype(f32) * scale
            )
            rows = pl.ds((2 * q + side) * span, span)
            grad = both_s[side, q, 32:, :].astype(f32)
            total = accum_ref[rows, :] + grad * grad
            new_accum_ref[rows, :] = total
            new_table_ref[rows, :] = table_ref[rows, :] - learn_rate * grad * lax.rsqrt(total)


def update(here, own, other, table, accum, scale):
    vmem = pl.BlockSpec(memory_space=pltpu.VMEM)
    part = jax.ShapeDtypeStruct((128, 512), f32)
    return pl.pallas_call(
        lambda *refs: update_kernel(*refs, scale=scale),
        out_shape=(
            jax.ShapeDtypeStruct(table.shape, f32),
            jax.ShapeDtypeStruct(table.shape, f32),
            part,
            part,
        ),
        in_specs=[pl.BlockSpec(memory_space=pltpu.SMEM)] + [vmem] * 4,
        out_specs=(vmem,) * 4,
        scratch_shapes=[pltpu.VMEM((2, *own.shape), bf16)],
        compiler_params=pltpu.CompilerParams(vmem_limit_bytes=12 * 1024 * 1024),
        name="update",
    )(here, own, other, table, accum)


def swapped(array, axis):
    return lax.ppermute(array, axis, [(0, 1), (1, 0)])


def step(
    cur_ids, prev_ids, prev_grads, row_place, table, accum, labels, gain, w_gate, w_up, w_out
):
    shards = lax.axis_size("emb")
    plane = lax.axis_size(XY)
    rows_shard, width = table.shape
    tok = cur_ids.shape[0]
    capacity = min(tok, 2 * tok // shards)
    slots = shards * capacity
    core = lax.axis_index("core")
    home = lax.axis_index("emb")
    here = jnp.stack([core, home]).astype(jnp.int32)

    cur_slot, cur_pos = slots_of(placed(cur_ids, row_place), rows_shard, capacity, shards)
    prev_slot, prev_pos = slots_of(placed(prev_ids, row_place), rows_shard, capacity, shards)
    slot_ids = jnp.arange(slots, dtype=jnp.int32)[:, None]
    cur_pack = (slot_ids == cur_pos[None, :]).astype(bf16)
    prev_pack = (slot_ids == prev_pos[None, :]).astype(bf16)
    cur_codes = code_line(dot32(cur_pack, coded(cur_slot)), shards, capacity)
    prev_codes = code_line(dot32(prev_pack, coded(prev_slot)), shards, capacity)
    prev_rows = dot32(prev_pack, prev_grads).astype(bf16).reshape(shards, capacity, width)

    at = lax.axis_index(XY)
    own_side = jnp.where(core == 0, w_gate, w_up)
    own_slice = lax.dynamic_slice(own_side, ((at % 4) * 32, (at // 4) * 128), (32, 128))
    shared = jnp.concatenate(
        [own_slice, w_out.reshape(4, 128), jnp.zeros((10, 128), bf16)], axis=0
    )
    first = exchange(
        jnp.concatenate(
            [
                prev_rows,
                jnp.broadcast_to(shared[None], (shards, *shared.shape)),
                cur_codes,
                prev_codes,
            ],
            axis=1,
        ),
        "emb",
    )
    got_rows = first[:, :capacity].reshape(slots, width)
    slices = first[:, capacity : capacity + 32]
    all_out = first[:, capacity + 32 : capacity + 36]
    wanted = decoded(first[:, capacity + 46], capacity)
    got_slots = decoded(first[:, capacity + 47], capacity)

    row_ids = jnp.arange(rows_shard, dtype=jnp.int32)
    fetched = dot32(
        (wanted[:, None] == row_ids[None, :]).astype(bf16), table.astype(bf16)
    ).astype(bf16)
    answers = exchange(fetched.reshape(shards, capacity, width), "emb").reshape(slots, width)

    foreign = lax.dynamic_slice(
        jnp.concatenate([slices, slices], axis=0), (home + 1, 0, 0), (shards - 1, 32, 128)
    ).reshape((shards - 1) * 32, 128)
    own_weights = lax.all_gather(foreign, XY, axis=0, tiled=True)
    other_weights = swapped(own_weights, "core")

    table_grad = dot32((row_ids[:, None] == got_slots[None, :]).astype(bf16), got_rows)
    span = rows_shard // plane // 2
    pieces = table_grad.reshape(plane, 2, span, width)
    mine = lax.dynamic_index_in_dim(pieces, core, 1, keepdims=False)
    theirs = lax.dynamic_index_in_dim(pieces, 1 - core, 1, keepdims=False)
    pair_grad = (mine + swapped(theirs, "core")).astype(bf16)

    answers, pair_grad = lax.optimization_barrier((answers, pair_grad))
    my_labels = lax.dynamic_slice(labels, (home * tok,), (tok,))
    emb_grad, tower_grads = tower(
        here, answers, cur_pos, own_weights, other_weights, w_gate, w_up, all_out, gain, my_labels
    )

    received = swapped(tower_grads[1], "core")
    core_sum = (tower_grads[0].astype(f32) + received.astype(f32)).astype(bf16)
    second = exchange(
        jnp.concatenate([core_sum.reshape(plane, shards * 32, 128), pair_grad], axis=1), XY
    )
    plane_sum = second[:, : shards * 32].astype(f32).sum(axis=0).astype(bf16)
    half_grad = second[:, shards * 32 :].astype(f32).sum(axis=0)
    for_z = jnp.broadcast_to(plane_sum.reshape(1, shards, 32, 128), (2, shards, 32, 128))
    third = exchange(for_z.reshape(2 * shards, 32, 128), ZZ)
    tower_sum = third.astype(f32).sum(axis=0).astype(bf16)
    total_grad = (half_grad + swapped(half_grad, "zh")).astype(bf16)
    own = to_all(jnp.concatenate([tower_sum, total_grad], axis=0), XY)
    other = swapped(own, "core")

    tower_scale = 1.0 / math.sqrt(tok * shards * lax.axis_size(DP))
    new_table, new_accum, gate_sum, up_sum = update(here, own, other, table, accum, tower_scale)
    return (new_table, new_accum, gate_sum, up_sum, emb_grad)


def solution(mesh):
    torus = Mesh(mesh.devices.reshape(4, 4, 2, 2, mesh.shape["emb"]), DP_EMB)
    return jax.shard_map(
        step,
        mesh=torus,
        in_specs=(
            P(DP_EMB),
            P(DP_EMB),
            P(DP_EMB, None),
            P(),
            P("emb", None),
            P("emb", None),
            P(DP),
            P(),
            P(None, "emb"),
            P(None, "emb"),
            P("emb"),
        ),
        out_specs=(P("emb", None), P("emb", None), P(None, "emb"), P(None, "emb"), P(DP_EMB, None)),
        check_vma=False,
    )
```

time: 170 us -> 168 us (0.988)
  blocking collectives: 92.6 us -> 53.9 us
  starting transfers between devices: 26.9 us -> 59.3 us
  waiting for transfers between devices: 23.7 us -> 27.7 us
  Pallas kernels: 7.42 us -> 9.53 us
  local copies, waits for them, and re-layouts: 7.51 us -> 5.71 us
    all_to_all x6 -> x2, blocking collectives: 92.6 us -> 33.6 us  [exchange(): return lax.all_to_all(pieces, axis, 0, 0, tiled=True)]
    ppermute x1 -> x5, starting transfers between devices: 7.95 us -> 33.6 us  [swapped(): return lax.ppermute(array, axis, [(0, 1), (1, 0)])]
    all_gather x0 -> x1, blocking collectives: none -> 20.3 us  [step(): own_weights = lax.all_gather(foreign, XY, axis=0, tiled=True)]
    ppermute x1 -> x5, waiting for transfers between devices: 0.01 us -> 8.58 us  [swapped(): return lax.ppermute(array, axis, [(0, 1), (1, 0)])]
    all_to_all x3, starting transfers between devices: 18.9 us -> 25.7 us  [exchange(): return lax.all_to_all(pieces, axis, 0, 0, tiled=True)]
    all_to_all x3, waiting for transfers between devices: 23.7 us -> 19.1 us  [exchange(): return lax.all_to_all(pieces, axis, 0, 0, tiled=True)]
    unnamed x13 -> x16, local copies, waits for them, and re-layouts: 3.49 us -> 0.04 us
    pallas_call x0 -> x1, Pallas kernels: none -> 2.05 us  [update(): pl.pallas_call(lambda *refs: update_kernel(*refs, scale=scale), out_shape...]
  transfers between devices with their start and end apart: 4 -> 8, of which waited for: 3 -> 5; matrix products, arithmetic and copies ran while one was open for 2% -> 5% of each run, Pallas kernels for 4% -> 0%
where the time goes in v2:
time: 168 us; the launch traced here: 167 us
  starting transfers between devices  59.3 us (35%)
  blocking collectives  53.9 us (32%)
  waiting for transfers between devices  27.7 us (16%)
  Pallas kernels  9.53 us (6%)
  local copies, waits for them, and re-layouts  5.71 us (3%)
  other arithmetic  5.6 us (3%)
  matrix products  4.46 us (3%)
    ppermute x5, starting transfers between devices, swapped(): return lax.ppermute(array, axis, [(0, 1), (1, 0)])  33.6 us
    all_to_all x2, blocking collectives, exchange(): return lax.all_to_all(pieces, axis, 0, 0, tiled=True)  33.6 us
    all_to_all x3, starting transfers between devices, exchange(): return lax.all_to_all(pieces, axis, 0, 0, tiled=True)  25.7 us
    all_gather x1, blocking collectives, step(): own_weights = lax.all_gather(foreign, XY, axis=0, tiled=True)  20.3 us
    all_to_all x3, waiting for transfers between devices, exchange(): return lax.all_to_all(pieces, axis, 0, 0, tiled=True)  19.1 us
    ppermute x5, waiting for transfers between devices, swapped(): return lax.ppermute(array, axis, [(0, 1), (1, 0)])  8.58 us
    pallas_call x1, Pallas kernels, tower(): pl.pallas_call(tower_kernel, out_shape=(jax.ShapeDtypeStruct((tok, width)...  7.48 us
    dot_general x9, matrix products, dot32(): return jnp.dot(a, b, preferred_element_type=f32)  4.46 us
  transfers between devices with their start and end apart: 8, of which 5 were waited for; matrix products, arithmetic and copies ran while one was open for 5% of the time, Pallas kernels for 0%

profile of v2, /device:TPU:1, one launch (start us, length us, event | category | flops | bytes accessed | tf_op | source)
XLA Modules:
  0.0 167.2 jit_solution(6570418057185215806)
XLA Ops:
  0.7 0.7 and_select_fusion.2
  1.4 0.9 fusion.31
  2.3 0.3 fusion.24
  2.6 0.7 and_select_fusion
  3.3 0.2 fusion.9
  3.5 0.1 copy.102
  3.7 0.1 copy.99
  3.8 0.1 copy.81
  3.9 0.2 fusion.18
  4.3 0.2 convolution_convert_fusion.2
  4.5 0.1 reshape.493
  4.6 0.1 reshape.511
  4.7 0.3 fusion.23
  5.1 0.2 fusion.8
  5.3 0.1 copy.88
  5.4 0.1 fusion.16
  5.7 0.2 convolution_convert_fusion
  6.0 0.2 convolution_convert_fusion.1
  6.2 0.1 reshape.495
  6.6 0.7 pad_maximum_fusion.1
  7.3 13.1 %all-to-all-start = ((bf16[8,112,128]{2,1,0:T(8,128)(2,1)}), bf16[8,112,128]{2,1,0:T(8,128)(2,1)S(1)}, u32[]{:S(2)}, u32[]{:S(2)}) async-start(bf16[8,112,128]{2,1,0:T(8,128)(2,1)} %pad_maximum_fusion.1), calls=%async_computation | async-start | bytes 458752 | tf_op jit(solution)/shard_map/all_to_all | solution.py:26
  20.4 11.6 %all-to-all-done = bf16[8,112,128]{2,1,0:T(8,128)(2,1)S(1)} async-done(((bf16[8,112,128]{2,1,0:T(8,128)(2,1)}), bf16[8,112,128]{2,1,0:T(8,128)(2,1)S(1)}, u32[]{:S(2)}, u32[]{:S(2)}) %all-to-all-start) | async-done | bytes 229408 | tf_op jit(solution)/shard_map/all_to_all | solution.py:26
  32.3 20.3 %all_gather.3.own_ref = bf16[3584,128]{1,0:T(8,128)(2,1)S(1)} all-gather(bf16[224,128]{1,0:T(8,128)(2,1)S(1)} %bitcast.80), channel_id=1, replica_groups=mesh['x'=4,'y'=4,'zh'=2,'core'=2,'emb'=8] {'x','y'}, dimensions={0}, use_global_device_ids=true | all-gather | bytes 974848 | tf_op jit(solution)/shard_map/all_gather | solution.py:292
  52.6 10.6 %collective-permute-start.1 = (bf16[3584,128]{1,0:T(8,128)(2,1)S(1)}, bf16[3584,128]{1,0:T(8,128)(2,1)S(1)}, u32[]{:S(2)}, u32[]{:S(2)}) collective-permute-start(bf16[3584,128]{1,0:T(8,128)(2,1)S(1)} %all_gather.3.own_ref), channel_id=1, source_target_pairs={{0,8},{8,0},{1,9},{9,1},{2,10},{10,2},{3,11},{11,3},{4,12},{12,4},... | collective-permute-start | bytes 2752520 | tf_op jit(solution)/shard_map/ppermute | solution.py:234
  63.3 1.5 fusion.1
  65.0 1.8 %dynamic-slice_bitcast_fusion = f32[16,48,128]{2,1,0:T(8,128)} fusion(f32[16,2,48,128]{3,2,1,0:T(8,128)} %fusion.1, s32[]{:T(128)S(6)} %select_n.227), kind=kLoop, calls=%fused_computation.25 | loop fusion | bytes 786436 | tf_op jit(solution)/shard_map/jit(dynamic_index_in_dim)/squeeze | solution.py:299
  66.8 1.9 %collective-permute-start = (f32[16,48,128]{2,1,0:T(8,128)}, f32[16,48,128]{2,1,0:T(8,128)}, u32[]{:S(2)}, u32[]{:S(2)}) collective-permute-start(f32[16,48,128]{2,1,0:T(8,128)} %dynamic-slice_bitcast_fusion), channel_id=1, source_target_pairs={{0,8},{8,0},{1,9},{9,1},{2,10},{10,2},{3,11},{11,3},{4,12},{12,4},... | collective-permute-start | bytes 1179656 | tf_op jit(solution)/shard_map/ppermute | solution.py:234
  68.7 1.3 fusion.7
  70.0 5.2 %all-to-all-start.1 = ((bf16[8,64,128]{2,1,0:T(8,128)(2,1)}), bf16[8,64,128]{2,1,0:T(8,128)(2,1)S(1)}, u32[]{:S(2)}, u32[]{:S(2)}) async-start(bf16[8,64,128]{2,1,0:T(8,128)(2,1)} %bitcast.11), calls=%async_computation.1 | async-start | bytes 262144 | tf_op jit(solution)/shard_map/all_to_all | solution.py:26
  75.2 0.8 dynamic_slice.20
  76.0 0.1 copy.103.labels_ref
  76.2 0.7 slice.76.w_out_ref
  76.9 1.2 fusion.10
  78.1 7.5 %all-to-all-done.1 = bf16[8,64,128]{2,1,0:T(8,128)(2,1)S(1)} async-done(((bf16[8,64,128]{2,1,0:T(8,128)(2,1)}), bf16[8,64,128]{2,1,0:T(8,128)(2,1)S(1)}, u32[]{:S(2)}, u32[]{:S(2)}) %all-to-all-start.1) | async-done | bytes 131104 | tf_op jit(solution)/shard_map/all_to_all | solution.py:26
  85.6 7.5 %tower.1 = (f32[256,128]{1,0:T(8,128)}, bf16[2,4096,128]{2,1,0:T(8,128)(2,1)S(1)}) custom-call(s32[2]{0:T(128)S(1)} %pad_add_fusion.here_ref.refs_0_, bf16[512,128]{1,0:T(8,128)(2,1)S(1)} %bitcast.76, s32[256,1]{1,0:T(8,128)S(1)} %get-tuple-element.32.target_ref, bf16[3584,128]{1,0:T(8,128)(2,1)S(1)} %all_gather.3.own_ref, ...), custom_call_target="tpu_custom_call" | custom-call | flops 1610612736 | bytes 5242880 | tf_op jit(solution)/shard_map/tower/pallas_call | solution.py:171
  93.1 4.5 %collective-permute-start.2 = (bf16[4096,128]{1,0:T(8,128)(2,1)S(1)}, bf16[4096,128]{1,0:T(8,128)(2,1)S(1)}, u32[]{:S(2)}, u32[]{:S(2)}) collective-permute-start(bf16[4096,128]{1,0:T(8,128)(2,1)S(1)} %slice_bitcast_fusion), channel_id=1, source_target_pairs={{0,8},{8,0},{1,9},{9,1},{2,10},{10,2},{3,11},{11,3},{4,12},{12,4},... | collective-permute-start | bytes 3145736 | tf_op jit(solution)/shard_map/ppermute | solution.py:234
  97.6 2.3 %collective-permute-done.2 = bf16[4096,128]{1,0:T(8,128)(2,1)S(1)} collective-permute-done((bf16[4096,128]{1,0:T(8,128)(2,1)S(1)}, bf16[4096,128]{1,0:T(8,128)(2,1)S(1)}, u32[]{:S(2)}, u32[]{:S(2)}) %collective-permute-start.2) | collective-permute-done | bytes 1048608 | tf_op jit(solution)/shard_map/ppermute | solution.py:234
  99.9 0.3 fusion.3
  100.2 22.4 %all_to_all.25 = bf16[16,304,128]{2,1,0:T(8,128)(2,1)S(1)} all-to-all(bf16[16,304,128]{2,1,0:T(8,128)(2,1)S(1)} %pad_maximum_fusion), channel_id=1, replica_groups=mesh['x'=4,'y'=4,'zh'=2,'core'=2,'emb'=8] {'x','y'}, dimensions={0} | all-to-all | bytes 2490368 | tf_op jit(solution)/shard_map/all_to_all | solution.py:26
  122.7 0.1 slice_reduce_fusion
  122.8 0.7 broadcast_in_dim.27
  123.5 7.4 %all-to-all-start.3 = ((bf16[16,32,128]{2,1,0:T(8,128)(2,1)}), bf16[16,32,128]{2,1,0:T(8,128)(2,1)S(1)}, u32[]{:S(2)}, u32[]{:S(2)}) async-start(bf16[16,32,128]{2,1,0:T(8,128)(2,1)} %bitcast.28), calls=%async_computation.3 | async-start | bytes 262144 | tf_op jit(solution)/shard_map/all_to_all | solution.py:26
  131.0 12.0 %collective-permute-start.3 = (f32[48,128]{1,0:T(8,128)S(1)}, f32[48,128]{1,0:T(8,128)S(1)}, u32[]{:S(2)}, u32[]{:S(2)}) collective-permute-start(f32[48,128]{1,0:T(8,128)S(1)} %convert_reduce_fusion), channel_id=1, source_target_pairs={{0,16},{16,0},{1,17},{17,1},{2,18},{18,2},{3,19},{19,3},{4,20},{20... | collective-permute-start | bytes 73736 | tf_op jit(solution)/shard_map/ppermute | solution.py:234
  143.0 5.1 %collective-permute-done.3 = f32[48,128]{1,0:T(8,128)S(1)} collective-permute-done((f32[48,128]{1,0:T(8,128)S(1)}, f32[48,128]{1,0:T(8,128)S(1)}, u32[]{:S(2)}, u32[]{:S(2)}) %collective-permute-start.3) | collective-permute-done | bytes 24608 | tf_op jit(solution)/shard_map/ppermute | solution.py:234
  148.1 11.1 %all_to_all.26.refs_1_ = bf16[16,80,128]{2,1,0:T(8,128)(2,1)S(1)} all-to-all(bf16[16,80,128]{2,1,0:T(8,128)(2,1)S(1)} %broadcast_in_dim.28), channel_id=1, replica_groups=mesh['x'=4,'y'=4,'zh'=2,'core'=2,'emb'=8] {'x','y'}, dimensions={0} | all-to-all | bytes 655360 | tf_op jit(solution)/shard_map/all_to_all | solution.py:26
  159.3 4.6 %collective-permute-start.4 = (bf16[16,80,128]{2,1,0:T(8,128)(2,1)S(1)}, bf16[16,80,128]{2,1,0:T(8,128)(2,1)S(1)}, u32[]{:S(2)}, u32[]{:S(2)}) collective-permute-start(bf16[16,80,128]{2,1,0:T(8,128)(2,1)S(1)} %all_to_all.26.refs_1_), channel_id=1, source_target_pairs={{0,8},{8,0},{1,9},{9,1},{2,10},{10,2},{3,11},{11,3},{4,12},{12,4},... | collective-permute-start | bytes 983048 | tf_op jit(solution)/shard_map/ppermute | solution.py:234
  163.9 1.2 collective-permute-done.4.refs_2_
  165.1 2.0 %update.1 = (f32[1536,128]{1,0:T(8,128)}, f32[1536,128]{1,0:T(8,128)}, f32[128,512]{1,0:T(8,128)}, f32[128,512]{1,0:T(8,128)}) custom-call(s32[2]{0:T(128)S(1)} %pad_add_fusion.here_ref.refs_0_, bf16[16,80,128]{2,1,0:T(8,128)(2,1)S(1)} %all_to_all.26.refs_1_, bf16[16,80,128]{2,1,0:T(8,128)(2,1)S(1)} %collective-permute-done.4.refs_2_, ...), custom_call_target="tpu_custom_call" | custom-call | tf_op jit(solution)/shard_map/update/pallas_call | solution.py:217
  (59 shorter events, 1.6 us)
Async XLA Ops:
  0.6 5.1 %copy-start = (bf16[256,128]{1,0:T(8,128)(2,1)S(1)}, bf16[256,128]{1,0:T(8,128)(2,1)}, u32[]{:S(2)}) copy-start(bf16[256,128]{1,0:T(8,128)(2,1)} %param.13) | copy-start | bytes 196612
  2.2 4.2 %copy-start.3 = (bf16[128,512]{1,0:T(8,128)(2,1)S(1)}, bf16[128,512]{1,0:T(8,128)(2,1)}, u32[]{:S(2)}) copy-start(bf16[128,512]{1,0:T(8,128)(2,1)} %w_up_ref.1) | copy-start | bytes 393220
  2.2 4.2 %copy-start.4 = (bf16[128,512]{1,0:T(8,128)(2,1)S(1)}, bf16[128,512]{1,0:T(8,128)(2,1)}, u32[]{:S(2)}) copy-start(bf16[128,512]{1,0:T(8,128)(2,1)} %w_gate_ref.1) | copy-start | bytes 393220
  2.2 4.2 %copy-start.7 = (bf16[512]{0:T(512)(128)(2,1)S(1)}, bf16[512]{0:T(512)(128)(2,1)}, u32[]{:S(2)}) copy-start(bf16[512]{0:T(512)(128)(2,1)} %param.21) | copy-start | bytes 3076
  7.3 24.7 %all-to-all-start = ((bf16[8,112,128]{2,1,0:T(8,128)(2,1)}), bf16[8,112,128]{2,1,0:T(8,128)(2,1)S(1)}, u32[]{:S(2)}, u32[]{:S(2)}) async-start(bf16[8,112,128]{2,1,0:T(8,128)(2,1)} %pad_maximum_fusion.1), calls=%async_computation | async-start | bytes 458752 | tf_op jit(solution)/shard_map/all_to_all | solution.py:26
  20.4 48.3 %copy-start.1 = (f32[1536,128]{1,0:T(8,128)S(1)}, f32[1536,128]{1,0:T(8,128)}, u32[]{:S(2)}) copy-start(f32[1536,128]{1,0:T(8,128)} %refs_3_.1) | copy-start | bytes 2359300
  32.1 31.2 %copy-start.6 = (bf16[8,112,128]{2,1,0:T(8,128)(2,1)}, bf16[8,112,128]{2,1,0:T(8,128)(2,1)S(1)}, u32[]{:S(2)}) copy-start(bf16[8,112,128]{2,1,0:T(8,128)(2,1)S(1)} %all-to-all-done) | copy-start | bytes 688132
  52.6 33.0 %collective-permute-start.1 = (bf16[3584,128]{1,0:T(8,128)(2,1)S(1)}, bf16[3584,128]{1,0:T(8,128)(2,1)S(1)}, u32[]{:S(2)}, u32[]{:S(2)}) collective-permute-start(bf16[3584,128]{1,0:T(8,128)(2,1)S(1)} %all_gather.3.own_ref), channel_id=1, source_target_pairs={{0,8},{8,0},{1,9},{9,1},{2,10},{10,2},{3,11},{11,3},{4,12},{12,4},... | collective-permute-start | bytes 2752520 | tf_op jit(solution)/shard_map/ppermute | solution.py:234
  64.8 20.8 %copy-start.5 = (f32[128]{0:T(128)S(1)}, f32[128]{0:T(128)}, u32[]{:S(2)}) copy-start(f32[128]{0:T(128)} %param.18) | copy-start | bytes 1540
  66.8 10.2 %collective-permute-start = (f32[16,48,128]{2,1,0:T(8,128)}, f32[16,48,128]{2,1,0:T(8,128)}, u32[]{:S(2)}, u32[]{:S(2)}) collective-permute-start(f32[16,48,128]{2,1,0:T(8,128)} %dynamic-slice_bitcast_fusion), channel_id=1, source_target_pairs={{0,8},{8,0},{1,9},{9,1},{2,10},{10,2},{3,11},{11,3},{4,12},{12,4},... | collective-permute-start | bytes 1179656 | tf_op jit(solution)/shard_map/ppermute | solution.py:234
  70.0 15.6 %all-to-all-start.1 = ((bf16[8,64,128]{2,1,0:T(8,128)(2,1)}), bf16[8,64,128]{2,1,0:T(8,128)(2,1)S(1)}, u32[]{:S(2)}, u32[]{:S(2)}) async-start(bf16[8,64,128]{2,1,0:T(8,128)(2,1)} %bitcast.11), calls=%async_computation.1 | async-start | bytes 262144 | tf_op jit(solution)/shard_map/all_to_all | solution.py:26
  93.1 6.7 %collective-permute-start.2 = (bf16[4096,128]{1,0:T(8,128)(2,1)S(1)}, bf16[4096,128]{1,0:T(8,128)(2,1)S(1)}, u32[]{:S(2)}, u32[]{:S(2)}) collective-permute-start(bf16[4096,128]{1,0:T(8,128)(2,1)S(1)} %slice_bitcast_fusion), channel_id=1, source_target_pairs={{0,8},{8,0},{1,9},{9,1},{2,10},{10,2},{3,11},{11,3},{4,12},{12,4},... | collective-permute-start | bytes 3145736 | tf_op jit(solution)/shard_map/ppermute | solution.py:234
  122.7 42.4 %copy-start.2 = (f32[1536,128]{1,0:T(8,128)S(1)}, f32[1536,128]{1,0:T(8,128)}, u32[]{:S(2)}) copy-start(f32[1536,128]{1,0:T(8,128)} %refs_4_.1) | copy-start | bytes 2359300
  123.5 24.5 %all-to-all-start.3 = ((bf16[16,32,128]{2,1,0:T(8,128)(2,1)}), bf16[16,32,128]{2,1,0:T(8,128)(2,1)S(1)}, u32[]{:S(2)}, u32[]{:S(2)}) async-start(bf16[16,32,128]{2,1,0:T(8,128)(2,1)} %bitcast.28), calls=%async_computation.3 | async-start | bytes 262144 | tf_op jit(solution)/shard_map/all_to_all | solution.py:26
  131.0 17.1 %collective-permute-start.3 = (f32[48,128]{1,0:T(8,128)S(1)}, f32[48,128]{1,0:T(8,128)S(1)}, u32[]{:S(2)}, u32[]{:S(2)}) collective-permute-start(f32[48,128]{1,0:T(8,128)S(1)} %convert_reduce_fusion), channel_id=1, source_target_pairs={{0,16},{16,0},{1,17},{17,1},{2,18},{18,2},{3,19},{19,3},{4,20},{20... | collective-permute-start | bytes 73736 | tf_op jit(solution)/shard_map/ppermute | solution.py:234
  159.3 5.8 %collective-permute-start.4 = (bf16[16,80,128]{2,1,0:T(8,128)(2,1)S(1)}, bf16[16,80,128]{2,1,0:T(8,128)(2,1)S(1)}, u32[]{:S(2)}, u32[]{:S(2)}) collective-permute-start(bf16[16,80,128]{2,1,0:T(8,128)(2,1)S(1)} %all_to_all.26.refs_1_), channel_id=1, source_target_pairs={{0,8},{8,0},{1,9},{9,1},{2,10},{10,2},{3,11},{11,3},{4,12},{12,4},... | collective-permute-start | bytes 983048 | tf_op jit(solution)/shard_map/ppermute | solution.py:234

commit v3 on v2

--- a/solution.py
+++ b/solution.py
@@ -34,37 +34,101 @@
     return jnp.dot(a, b, preferred_element_type=f32)
 
 
-def placed(ids, row_place):
-    lanes = 128
-    grid = row_place.reshape(-1, lanes)
-    parts = jnp.concatenate([grid // lanes, grid % lanes], axis=1).astype(bf16)
-    pick = (ids[:, None] // lanes == jnp.arange(grid.shape[0], dtype=jnp.int32)[None, :]).astype(bf16)
-    lines = dot32(pick, parts)
-    lane = ids[:, None] % lanes == jnp.arange(lanes, dtype=jnp.int32)[None, :]
-    high = jnp.sum(jnp.where(lane, lines[:, :lanes], 0.0), axis=1)
-    low = jnp.sum(jnp.where(lane, lines[:, lanes:], 0.0), axis=1)
-    return high.astype(jnp.int32) * lanes + low.astype(jnp.int32)
-
-
-def slots_of(place, rows_shard, capacity, shards):
-    owner = place // rows_shard
-    slot = place % rows_shard
-    match = owner[:, None] == jnp.arange(shards, dtype=jnp.int32)[None, :]
-    n = place.shape[0]
-    before = (
-        jnp.arange(n, dtype=jnp.int32)[:, None] >= jnp.arange(n, dtype=jnp.int32)[None, :]
+def packed(ids, parts, capacity, shards, rows_shard):
+    tok = ids.shape[1]
+    lines = parts.shape[0]
+    row = lax.broadcasted_iota(jnp.int32, (lines, tok), 0)
+    pick = jnp.where(ids // 128 == row, 1.0, 0.0).astype(bf16)
+    found = lax.dot_general(parts, pick, (((0,), (0,)), ((), ())), preferred_element_type=f32)
+    lane = lax.broadcasted_iota(jnp.int32, (128, tok), 0) == ids % 128
+    high = jnp.sum(jnp.where(lane, found[:128], 0.0), axis=0, keepdims=True)
+    low = jnp.sum(jnp.where(lane, found[128:], 0.0), axis=0, keepdims=True)
+    place = (high * 128.0 + low).astype(jnp.int32)
+    shard = lax.broadcasted_iota(jnp.int32, (shards, tok), 0)
+    match = (place >= shard * rows_shard) & (place < (shard + 1) * rows_shard)
+    matched = jnp.where(match, 1.0, 0.0)
+    owner = jnp.sum(jnp.where(match, shard, 0), axis=0, keepdims=True)
+    slot = place - owner * rows_shard
+    earlier = lax.broadcasted_iota(jnp.int32, (tok, tok), 0) <= lax.broadcasted_iota(
+        jnp.int32, (tok, tok), 1
+    )
+    counts = dot32(matched.astype(bf16), jnp.where(earlier, 1.0, 0.0).astype(bf16))
+    rank = jnp.sum(matched * counts, axis=0, keepdims=True).astype(jnp.int32) - 1
+    line = lax.broadcasted_iota(jnp.int32, (128, tok), 0)
+    spread = jnp.where(line % capacity == rank, 1.0, 0.0).astype(bf16)
+    both = (((1,), (1,)), ((), ()))
+    codes = [
+        lax.dot_general(
+            (matched * part.astype(f32)).astype(bf16), spread, both, preferred_element_type=f32
+        )
+        for part in (slot // 128 + 1, slot % 128)
+    ]
+    first_half = lax.broadcasted_iota(jnp.int32, (shards, 128), 1) < capacity
+    code = jnp.where(first_half, codes[0], codes[1])
+    return code, owner * capacity + rank
+
+
+def pack_kernel(
+    here_ref, *refs, capacity, rows_shard
+):
+    sources, (out_ref, pos_ref), buffers, sems = refs[:7], refs[7:9], refs[9:16], refs[16]
+    copies = [
+        pltpu.make_async_copy(source, buffer, sems.at[i])
+        for i, (source, buffer) in enumerate(zip(sources, buffers, strict=True))
+    ]
+    for copy in copies:
+        copy.start()
+    for copy in copies:
+        copy.wait()
+    cur_ref, prev_ref, grads_ref, places_ref, w_gate_ref, w_up_ref, w_out_ref = buffers
+    shards = out_ref.shape[0]
+    places = places_ref[...]
+    parts = jnp.concatenate(
+        [(places // 128).astype(f32), (places % 128).astype(f32)], axis=1
     ).astype(bf16)
-    counts = dot32(before, match.astype(bf16))
-    rank = jnp.sum(jnp.where(match, counts, 0.0), axis=1).astype(jnp.int32) - 1
-    return slot, owner * capacity + rank
-
-
-def coded(slot):
-    return jnp.stack([slot // 128 + 1, slot % 128], axis=1).astype(bf16)
-
-
-def code_line(packed, shards, capacity):
-    return packed.astype(bf16).reshape(shards, capacity, 2).swapaxes(1, 2).reshape(shards, 1, -1)
+    cur_code, cur_pos = packed(cur_ref[...], parts, capacity, shards, rows_shard)
+    prev_code, prev_pos = packed(prev_ref[...], parts, capacity, shards, rows_shard)
+    pos_ref[...] = cur_pos
+    slots = shards * capacity
+    slot_row = lax.broadcasted_iota(jnp.int32, (slots, prev_pos.shape[1]), 0)
+    pack = jnp.where(slot_row == prev_pos, 1.0, 0.0).astype(bf16)
+    rows = dot32(pack, grads_ref[...]).astype(bf16)
+    at = here_ref[2]
+    cut = (pl.ds(pl.multiple_of((at % 4) * 32, 32), 32), pl.ds(pl.multiple_of((at // 4) * 128, 128), 128))
+    gate_slice = w_gate_ref[cut].astype(f32)
+    up_slice = w_up_ref[cut].astype(f32)
+    own = jnp.where(here_ref[0] == 0, gate_slice, up_slice).astype(bf16)
+    out = jnp.concatenate([w_out_ref[...].astype(f32), jnp.zeros((12, 128), f32)], axis=0)
+    tail_row = lax.broadcasted_iota(jnp.int32, (16, 128), 0)
+    for shard in range(shards):
+        out_ref[shard, :capacity, :] = rows[shard * capacity : (shard + 1) * capacity]
+        out_ref[shard, capacity : capacity + 32, :] = own
+        tail = jnp.where(tail_row == 14, cur_code[shard : shard + 1], out)
+        tail = jnp.where(tail_row == 15, prev_code[shard : shard + 1], tail)
+        out_ref[shard, capacity + 32 : capacity + 48, :] = tail.astype(bf16)
+
+
+def pack(here, cur_ids, prev_ids, prev_grads, row_place, w_gate, w_up, w_out, shards, capacity, rows_shard):
+    vmem = pl.BlockSpec(memory_space=pltpu.VMEM)
+    tok = cur_ids.shape[0]
+    arrays = (
+        cur_ids.reshape(1, tok), prev_ids.reshape(1, tok), prev_grads,
+        row_place.reshape(-1, 128), w_gate, w_up, w_out.reshape(4, 128),
+    )
+    return pl.pallas_call(
+        lambda *refs: pack_kernel(*refs, capacity=capacity, rows_shard=rows_shard),
+        out_shape=(
+            jax.ShapeDtypeStruct((shards, capacity + 48, 128), bf16),
+            jax.ShapeDtypeStruct((1, tok), jnp.int32),
+        ),
+        in_specs=[pl.BlockSpec(memory_space=pltpu.SMEM)]
+        + [pl.BlockSpec(memory_space=pltpu.HBM)] * len(arrays),
+        out_specs=(vmem, vmem),
+        scratch_shapes=[pltpu.VMEM(array.shape, array.dtype) for array in arrays]
+        + [pltpu.SemaphoreType.DMA((len(arrays),))],
+        compiler_params=pltpu.CompilerParams(vmem_limit_bytes=62 * 1024 * 1024),
+        name="pack",
+    )(here, *arrays)
 
 
 def decoded(line, capacity):
@@ -73,19 +137,25 @@
 
 
 def tower_kernel(
-    here_ref, answers_ref, target_ref, own_ref, other_ref, w_gate_ref, w_up_ref, w_out_ref,
+    here_ref, answers_ref, target_ref, own_ref, other_ref, w_gate_ref, w_up_ref, shared_ref,
     gain_ref, labels_ref, emb_grad_ref, grads_ref, weights_s, gate_s, up_s, sig_s,
 ):
-    tok = target_ref.shape[0]
+    tok = target_ref.shape[1]
     width = answers_ref.shape[1]
-    shards = w_out_ref.shape[0]
+    shards, span = shared_ref.shape[:2]
+    lines = own_ref.shape[0] // 16
     core = here_ref[0]
     home = here_ref[1]
     weights_s[core] = own_ref[...]
     weights_s[1 - core] = other_ref[...]
-    slot_lane = lax.broadcasted_iota(jnp.int32, (tok, answers_ref.shape[0]), 1)
-    pick = jnp.where(target_ref[...] == slot_lane, 1.0, 0.0).astype(bf16)
-    values = dot32(pick, answers_ref[...])
+    slot_row = lax.broadcasted_iota(jnp.int32, (answers_ref.shape[0], tok), 0)
+    pick = jnp.where(target_ref[...] == slot_row, 1.0, 0.0).astype(bf16)
+    values = lax.dot_general(
+        pick, answers_ref[...], (((0,), (0,)), ((), ())), preferred_element_type=f32
+    )
+    turned = labels_ref[...].T
+    column = lax.broadcasted_iota(jnp.int32, turned.shape, 1) == home
+    targets = jnp.sum(jnp.where(column, turned, 0.0), axis=1, keepdims=True)
     inverse_rms = lax.rsqrt(jnp.mean(values * values, axis=1, keepdims=True) + norm_eps)
     gain = gain_ref[...]
     normed_wide = values * inverse_rms * gain
@@ -96,7 +166,7 @@
         tiles = []
         for tile in (2 * half, 2 * half + 1):
             quarters = [
-                weights_s[side, pl.ds((tile * 4 + k) * (shards - 1) * 32 + hop * 32, 32), :]
+                weights_s[side, pl.ds((tile * 4 + k) * lines + hop * 32, 32), :]
                 for k in range(4)
             ]
             tiles.append(jnp.concatenate(quarters, axis=0))
@@ -106,7 +176,7 @@
         return (w_gate_ref, w_up_ref)[side][:, half * 256 : (half + 1) * 256]
 
     def out_row(shard, half, j):
-        return w_out_ref[shard, pl.ds(2 * half + j, 1), :].astype(f32)
+        return shared_ref[shard, pl.ds(span - 16 + 2 * half + j, 1), :].astype(f32)
 
     def forward(hop, total, block):
         shard = (home + 1 + hop) % shards
@@ -126,7 +196,7 @@
     total = forward(shards - 1, jnp.zeros((tok, 128), f32), home_block)
     total = lax.fori_loop(0, shards - 1, lambda hop, t: forward(hop, t, far_block), total)
     logits = jnp.sum(total, axis=1, keepdims=True)
-    slopes = loss_weight * (jax.nn.sigmoid(logits) - labels_ref[...])
+    slopes = loss_weight * (jax.nn.sigmoid(logits) - targets)
 
     across = (((1,), (1,)), ((), ()))
 
@@ -163,10 +233,10 @@
     ) * jnp.mean(values * scaled, axis=1, keepdims=True)
 
 
-def tower(here, answers, target, own, other, w_gate, w_up, w_out, gain, labels):
-    tok = target.shape[0]
+def tower(here, answers, target, own, other, w_gate, w_up, shared, gain, labels):
+    tok = target.shape[1]
     width = answers.shape[1]
-    shards = w_out.shape[0]
+    shards = shared.shape[0]
     vmem = pl.BlockSpec(memory_space=pltpu.VMEM)
     return pl.pallas_call(
         tower_kernel,
@@ -184,8 +254,8 @@
         ),
         name="tower",
     )(
-        here, answers, target.reshape(-1, 1), own, other, w_gate, w_up, w_out,
-        gain.reshape(1, -1), labels.reshape(-1, 1),
+        here, answers, target, own, other, w_gate, w_up, shared,
+        gain.reshape(1, -1), labels.reshape(shards, tok),
     )
 
 
@@ -245,38 +315,15 @@
     slots = shards * capacity
     core = lax.axis_index("core")
     home = lax.axis_index("emb")
-    here = jnp.stack([core, home]).astype(jnp.int32)
-
-    cur_slot, cur_pos = slots_of(placed(cur_ids, row_place), rows_shard, capacity, shards)
-    prev_slot, prev_pos = slots_of(placed(prev_ids, row_place), rows_shard, capacity, shards)
-    slot_ids = jnp.arange(slots, dtype=jnp.int32)[:, None]
-    cur_pack = (slot_ids == cur_pos[None, :]).astype(bf16)
-    prev_pack = (slot_ids == prev_pos[None, :]).astype(bf16)
-    cur_codes = code_line(dot32(cur_pack, coded(cur_slot)), shards, capacity)
-    prev_codes = code_line(dot32(prev_pack, coded(prev_slot)), shards, capacity)
-    prev_rows = dot32(prev_pack, prev_grads).astype(bf16).reshape(shards, capacity, width)
-
-    at = lax.axis_index(XY)
-    own_side = jnp.where(core == 0, w_gate, w_up)
-    own_slice = lax.dynamic_slice(own_side, ((at % 4) * 32, (at // 4) * 128), (32, 128))
-    shared = jnp.concatenate(
-        [own_slice, w_out.reshape(4, 128), jnp.zeros((10, 128), bf16)], axis=0
-    )
-    first = exchange(
-        jnp.concatenate(
-            [
-                prev_rows,
-                jnp.broadcast_to(shared[None], (shards, *shared.shape)),
-                cur_codes,
-                prev_codes,
-            ],
-            axis=1,
-        ),
-        "emb",
-    )
+    here = jnp.stack([core, home, lax.axis_index(XY)]).astype(jnp.int32)
+
+    payload, cur_pos = pack(
+        here, cur_ids, prev_ids, prev_grads, row_place, w_gate, w_up, w_out,
+        shards, capacity, rows_shard,
+    )
+    first = exchange(payload, "emb")
     got_rows = first[:, :capacity].reshape(slots, width)
     slices = first[:, capacity : capacity + 32]
-    all_out = first[:, capacity + 32 : capacity + 36]
     wanted = decoded(first[:, capacity + 46], capacity)
     got_slots = decoded(first[:, capacity + 47], capacity)
 
@@ -286,36 +333,43 @@
     ).astype(bf16)
     answers = exchange(fetched.reshape(shards, capacity, width), "emb").reshape(slots, width)
 
+    span = rows_shard // plane // 2
+    half_ids = jnp.arange(rows_shard // 2, dtype=jnp.int32)
+    half_ids = half_ids // span * (2 * span) + half_ids % span
+
+    def half_sum(side):
+        hot = (half_ids + side * span)[:, None] == got_slots[None, :]
+        return dot32(hot.astype(bf16), got_rows).reshape(plane, span, width)
+
+    received = swapped(half_sum(1 - core), "core")
+    pair_grad = (half_sum(core) + received).astype(bf16)
+
     foreign = lax.dynamic_slice(
         jnp.concatenate([slices, slices], axis=0), (home + 1, 0, 0), (shards - 1, 32, 128)
     ).reshape((shards - 1) * 32, 128)
-    own_weights = lax.all_gather(foreign, XY, axis=0, tiled=True)
+    lines = foreign.shape[0]
+    plane_in = jnp.concatenate(
+        [jnp.broadcast_to(foreign[None], (plane, *foreign.shape)), pair_grad], axis=1
+    )
+    answers, plane_in = lax.optimization_barrier((answers, plane_in))
+    planes = exchange(plane_in, XY)
+    own_weights = planes.reshape(-1, 128)
     other_weights = swapped(own_weights, "core")
-
-    table_grad = dot32((row_ids[:, None] == got_slots[None, :]).astype(bf16), got_rows)
-    span = rows_shard // plane // 2
-    pieces = table_grad.reshape(plane, 2, span, width)
-    mine = lax.dynamic_index_in_dim(pieces, core, 1, keepdims=False)
-    theirs = lax.dynamic_index_in_dim(pieces, 1 - core, 1, keepdims=False)
-    pair_grad = (mine + swapped(theirs, "core")).astype(bf16)
-
-    answers, pair_grad = lax.optimization_barrier((answers, pair_grad))
-    my_labels = lax.dynamic_slice(labels, (home * tok,), (tok,))
+    half_grad = planes[:, lines:].astype(f32).sum(axis=0)
+
     emb_grad, tower_grads = tower(
-        here, answers, cur_pos, own_weights, other_weights, w_gate, w_up, all_out, gain, my_labels
+        here, answers, cur_pos, own_weights, other_weights, w_gate, w_up, first, gain, labels
     )
 
     received = swapped(tower_grads[1], "core")
     core_sum = (tower_grads[0].astype(f32) + received.astype(f32)).astype(bf16)
-    second = exchange(
-        jnp.concatenate([core_sum.reshape(plane, shards * 32, 128), pair_grad], axis=1), XY
-    )
-    plane_sum = second[:, : shards * 32].astype(f32).sum(axis=0).astype(bf16)
-    half_grad = second[:, shards * 32 :].astype(f32).sum(axis=0)
+    second = exchange(core_sum.reshape(plane, shards * 32, 128), XY)
+    total_grad = (half_grad + swapped(half_grad, "zh")).astype(bf16)
+    second, total_grad = lax.optimization_barrier((second, total_grad))
+    plane_sum = second.astype(f32).sum(axis=0).astype(bf16)
     for_z = jnp.broadcast_to(plane_sum.reshape(1, shards, 32, 128), (2, shards, 32, 128))
     third = exchange(for_z.reshape(2 * shards, 32, 128), ZZ)
     tower_sum = third.astype(f32).sum(axis=0).astype(bf16)
-    total_grad = (half_grad + swapped(half_grad, "zh")).astype(bf16)
     own = to_all(jnp.concatenate([tower_sum, total_grad], axis=0), XY)
     other = swapped(own, "core")
 

time: 168 us -> 163 us (0.970)
  waiting for transfers between devices: 27.7 us -> 35.8 us
  starting transfers between devices: 59.3 us -> 51.6 us
  local copies, waits for them, and re-layouts: 5.71 us -> 0.47 us
  Pallas kernels: 9.53 us -> 13.8 us
  other arithmetic: 5.6 us -> 3.66 us
    all_gather x1 -> x0, blocking collectives: 20.3 us -> none  [step(): own_weights = lax.all_gather(foreign, XY, axis=0, tiled=True)]
    all_to_all x2 -> x3, blocking collectives: 33.6 us -> 52.5 us  [exchange(): return lax.all_to_all(pieces, axis, 0, 0, tiled=True)]
    all_to_all x3, waiting for transfers between devices: 19.1 us -> 24.5 us  [exchange(): return lax.all_to_all(pieces, axis, 0, 0, tiled=True)]
    ppermute x5, starting transfers between devices: 33.6 us -> 28.9 us  [swapped(): return lax.ppermute(array, axis, [(0, 1), (1, 0)])]
    pallas_call x0 -> x1, Pallas kernels: none -> 3.5 us  [pack(): pl.pallas_call(lambda *refs: pack_kernel(*refs, capacity=capacity, rows_s...]
    all_to_all x3, starting transfers between devices: 25.7 us -> 22.7 us  [exchange(): return lax.all_to_all(pieces, axis, 0, 0, tiled=True)]
    ppermute x5, waiting for transfers between devices: 8.58 us -> 11.3 us  [swapped(): return lax.ppermute(array, axis, [(0, 1), (1, 0)])]
    squeeze x1 -> x0, local copies, waits for them, and re-layouts: 1.77 us -> none  [step(): theirs = lax.dynamic_index_in_dim(pieces, 1 - core, 1, keepdims=False)]
  transfers between devices with their start and end apart: 8 -> 8, of which waited for: 5 -> 7; matrix products, arithmetic and copies ran while one was open for 5% -> 2% of each run, Pallas kernels for 0% -> 0%
where the time goes in v3:
time: 163 us; the launch traced here: 162 us
  blocking collectives  52.5 us (32%)
  starting transfers between devices  51.6 us (32%)
  waiting for transfers between devices  35.8 us (22%)
  Pallas kernels  13.8 us (8%)
  other arithmetic  3.66 us (2%)
  matrix products  3.34 us (2%)
    all_to_all x3, blocking collectives, exchange(): return lax.all_to_all(pieces, axis, 0, 0, tiled=True)  52.5 us
    ppermute x5, starting transfers between devices, swapped(): return lax.ppermute(array, axis, [(0, 1), (1, 0)])  28.9 us
    all_to_all x3, waiting for transfers between devices, exchange(): return lax.all_to_all(pieces, axis, 0, 0, tiled=True)  24.5 us
    all_to_all x3, starting transfers between devices, exchange(): return lax.all_to_all(pieces, axis, 0, 0, tiled=True)  22.7 us
    ppermute x5, waiting for transfers between devices, swapped(): return lax.ppermute(array, axis, [(0, 1), (1, 0)])  11.3 us
    pallas_call x1, Pallas kernels, tower(): pl.pallas_call(tower_kernel, out_shape=(jax.ShapeDtypeStruct((tok, width)...  8.21 us
    pallas_call x1, Pallas kernels, pack(): pl.pallas_call(lambda *refs: pack_kernel(*refs, capacity=capacity, rows_s...  3.5 us
    dot_general x3, matrix products, dot32(): return jnp.dot(a, b, preferred_element_type=f32)  3.34 us
  transfers between devices with their start and end apart: 8, of which 7 were waited for; matrix products, arithmetic and copies ran while one was open for 2% of the time, Pallas kernels for 0%

profile of v3, /device:TPU:1, one launch (start us, length us, event | category | flops | bytes accessed | tf_op | source)
XLA Modules:
  0.0 162.0 jit_solution(8012108203530122331)
XLA Ops:
  0.6 0.6 pad_add_fusion.refs_0_.here_ref
  1.2 3.5 %pack.1 = (bf16[8,112,128]{2,1,0:T(8,128)(2,1)}, s32[1,256]{1,0:T(1,128)}) custom-call(s32[3]{0:T(128)} %pad_add_fusion.refs_0_.here_ref, s32[1,256]{1,0:T(1,128)} %bitcast.43, s32[1,256]{1,0:T(1,128)} %bitcast.44, bf16[256,128]{1,0:T(8,128)(2,1)} %refs_3_.2, s32[96,128]{1,0:T(8,128)} %bitcast.41, bf16[128,512]{1,0:T(8,128)(2,1)} %w_gate_ref.1, ...), custom_call_target="tpu_custom_call" | custom-call | tf_op jit(solution)/shard_map/pack/pallas_call | solution.py:118
  4.7 13.1 %all-to-all-start = ((bf16[8,112,128]{2,1,0:T(8,128)(2,1)}), bf16[8,112,128]{2,1,0:T(8,128)(2,1)S(1)}, u32[]{:S(2)}, u32[]{:S(2)}) async-start(bf16[8,112,128]{2,1,0:T(8,128)(2,1)} %get-tuple-element.17), calls=%async_computation | async-start | bytes 458752 | tf_op jit(solution)/shard_map/all_to_all | solution.py:26
  17.9 11.6 %all-to-all-done.shared_ref = bf16[8,112,128]{2,1,0:T(8,128)(2,1)S(1)} async-done(((bf16[8,112,128]{2,1,0:T(8,128)(2,1)}), bf16[8,112,128]{2,1,0:T(8,128)(2,1)S(1)}, u32[]{:S(2)}, u32[]{:S(2)}) %all-to-all-start) | async-done | bytes 229408 | tf_op jit(solution)/shard_map/all_to_all | solution.py:26
  29.5 0.1 slice_add_fusion
  29.6 0.1 eq.58
  29.7 0.4 fusion.3
  30.1 6.1 %collective-permute-start = (f32[16,48,128]{2,1,0:T(8,128)S(1)}, f32[16,48,128]{2,1,0:T(8,128)S(1)}, u32[]{:S(2)}, u32[]{:S(2)}) collective-permute-start(f32[16,48,128]{2,1,0:T(8,128)S(1)} %fusion.3), channel_id=1, source_target_pairs={{0,8},{8,0},{1,9},{9,1},{2,10},{10,2},{3,11},{11,3},{4,12},{12,4},... | collective-permute-start | bytes 1179656 | tf_op jit(solution)/shard_map/ppermute | solution.py:304
  36.2 0.1 slice_add_fusion.1
  36.2 0.1 eq.53
  36.3 2.5 %fusion.13 = bf16[512,128]{1,0:T(8,128)(2,1)} fusion(s32[512]{0:T(512)S(1)} %eq.53, f32[1536,128]{1,0:T(8,128)} %refs_3_.3), kind=kOutput, calls=%fused_computation.11 | convolution fusion | flops 202375168 | bytes 919552 | tf_op jit(solution)/shard_map/dot_general | solution.py:34
  38.8 5.2 %all-to-all-start.1 = ((bf16[8,64,128]{2,1,0:T(8,128)(2,1)}), bf16[8,64,128]{2,1,0:T(8,128)(2,1)S(1)}, u32[]{:S(2)}, u32[]{:S(2)}) async-start(bf16[8,64,128]{2,1,0:T(8,128)(2,1)} %bitcast.9), calls=%async_computation.1 | async-start | bytes 262144 | tf_op jit(solution)/shard_map/all_to_all | solution.py:26
  44.0 0.1 fusion.19
  44.1 0.0 collective-permute-done
  44.1 0.4 fusion.10
  44.5 0.1 broadcast_in_dim.11
  44.7 0.0 copy-start.7
  44.7 0.0 copy-start.2
  44.7 0.0 copy-start.3
  44.7 0.0 copy-start.4
  44.7 0.0 copy-start.5
  44.7 0.0 copy-start.6
  44.7 0.1 pad_maximum_fusion
  44.8 9.8 %all-to-all-done.1 = bf16[8,64,128]{2,1,0:T(8,128)(2,1)S(1)} async-done(((bf16[8,64,128]{2,1,0:T(8,128)(2,1)}), bf16[8,64,128]{2,1,0:T(8,128)(2,1)S(1)}, u32[]{:S(2)}, u32[]{:S(2)}) %all-to-all-start.1) | async-done | bytes 131104 | tf_op jit(solution)/shard_map/all_to_all | solution.py:26
  54.6 21.7 %all_to_all.30 = bf16[16,272,128]{2,1,0:T(8,128)(2,1)S(1)} all-to-all(bf16[16,272,128]{2,1,0:T(8,128)(2,1)S(1)} %pad_maximum_fusion), channel_id=1, replica_groups=mesh['x'=4,'y'=4,'zh'=2,'core'=2,'emb'=8] {'x','y'}, dimensions={0} | all-to-all | bytes 2228224 | tf_op jit(solution)/shard_map/all_to_all | solution.py:26
  76.3 5.5 %collective-permute-start.1 = (bf16[4352,128]{1,0:T(8,128)(2,1)S(1)}, bf16[4352,128]{1,0:T(8,128)(2,1)}, u32[]{:S(2)}, u32[]{:S(2)}) collective-permute-start(bf16[4352,128]{1,0:T(8,128)(2,1)S(1)} %bitcast.31), channel_id=1, source_target_pairs={{0,8},{8,0},{1,9},{9,1},{2,10},{10,2},{3,11},{11,3},{4,12},{12,4},... | collective-permute-start | bytes 3342344 | tf_op jit(solution)/shard_map/ppermute | solution.py:304
  81.8 0.0 copy-done.7
  81.8 2.5 %collective-permute-done.1.other_ref = bf16[4352,128]{1,0:T(8,128)(2,1)} collective-permute-done((bf16[4352,128]{1,0:T(8,128)(2,1)S(1)}, bf16[4352,128]{1,0:T(8,128)(2,1)}, u32[]{:S(2)}, u32[]{:S(2)}) %collective-permute-start.1) | collective-permute-done | bytes 1114144 | tf_op jit(solution)/shard_map/ppermute | solution.py:304
  84.3 0.0 copy-done.2
  84.3 0.0 copy-done.3
  84.3 0.0 copy-done.4
  84.3 0.0 copy-done.6
  84.3 8.2 %tower.1 = (f32[256,128]{1,0:T(8,128)}, bf16[2,4096,128]{2,1,0:T(8,128)(2,1)S(1)}) custom-call(s32[3]{0:T(128)S(1)} %copy-done.4, bf16[512,128]{1,0:T(8,128)(2,1)S(1)} %bitcast.33, s32[1,256]{1,0:T(1,128)S(1)} %copy-done.5, bf16[4352,128]{1,0:T(8,128)(2,1)S(1)} %bitcast.32, bf16[4352,128]{1,0:T(8,128)(2,1)} %collective-permute-done.1.other_ref, ...), custom_call_target="tpu_custom_call" | custom-call | flops 1610612736 | bytes 5242880 | tf_op jit(solution)/shard_map/tower/pallas_call | solution.py:241
  92.5 0.1 slice_bitcast_fusion
  92.6 2.3 %collective-permute-start.2 = (bf16[4096,128]{1,0:T(8,128)(2,1)S(1)}, bf16[4096,128]{1,0:T(8,128)(2,1)S(1)}, u32[]{:S(2)}, u32[]{:S(2)}) collective-permute-start(bf16[4096,128]{1,0:T(8,128)(2,1)S(1)} %slice_bitcast_fusion), channel_id=1, source_target_pairs={{0,8},{8,0},{1,9},{9,1},{2,10},{10,2},{3,11},{11,3},{4,12},{12,4},... | collective-permute-start | bytes 3145736 | tf_op jit(solution)/shard_map/ppermute | solution.py:304
  94.9 2.3 %collective-permute-done.2 = bf16[4096,128]{1,0:T(8,128)(2,1)S(1)} collective-permute-done((bf16[4096,128]{1,0:T(8,128)(2,1)S(1)}, bf16[4096,128]{1,0:T(8,128)(2,1)S(1)}, u32[]{:S(2)}, u32[]{:S(2)}) %collective-permute-start.2) | collective-permute-done | bytes 1048608 | tf_op jit(solution)/shard_map/ppermute | solution.py:304
  97.2 1.3 fusion.1
  98.5 4.5 %all-to-all-start.3 = ((bf16[16,256,128]{2,1,0:T(8,128)(2,1)}), bf16[16,256,128]{2,1,0:T(8,128)(2,1)}, u32[]{:S(2)}, u32[]{:S(2)}) async-start(bf16[16,256,128]{2,1,0:T(8,128)(2,1)} %bitcast.35), calls=%async_computation.3 | async-start | bytes 2097152 | tf_op jit(solution)/shard_map/all_to_all | solution.py:26
  103.0 7.9 %collective-permute-start.3 = (f32[48,128]{1,0:T(8,128)S(1)}, f32[48,128]{1,0:T(8,128)S(1)}, u32[]{:S(2)}, u32[]{:S(2)}) collective-permute-start(f32[48,128]{1,0:T(8,128)S(1)} %convert_reduce_fusion), channel_id=1, source_target_pairs={{0,16},{16,0},{1,17},{17,1},{2,18},{18,2},{3,19},{19,3},{4,20},{20... | collective-permute-start | bytes 73736 | tf_op jit(solution)/shard_map/ppermute | solution.py:304
  110.9 5.3 %collective-permute-done.3 = f32[48,128]{1,0:T(8,128)S(1)} collective-permute-done((f32[48,128]{1,0:T(8,128)S(1)}, f32[48,128]{1,0:T(8,128)S(1)}, u32[]{:S(2)}, u32[]{:S(2)}) %collective-permute-start.3) | collective-permute-done | bytes 24608 | tf_op jit(solution)/shard_map/ppermute | solution.py:304
  116.3 3.1 %all-to-all-done.3 = bf16[16,256,128]{2,1,0:T(8,128)(2,1)} async-done(((bf16[16,256,128]{2,1,0:T(8,128)(2,1)}), bf16[16,256,128]{2,1,0:T(8,128)(2,1)}, u32[]{:S(2)}, u32[]{:S(2)}) %all-to-all-start.3) | async-done | bytes 1048608 | tf_op jit(solution)/shard_map/all_to_all | solution.py:26
  119.3 1.4 reduce_sum.34
  120.7 19.2 %all_to_all.31 = bf16[16,32,128]{2,1,0:T(8,128)(2,1)S(1)} all-to-all(bf16[16,32,128]{2,1,0:T(8,128)(2,1)S(1)} %bitcast.36), channel_id=1, replica_groups=mesh['x'=4,'y'=4,'zh'=2,'core'=2,'emb'=8] {'zh','emb'}, dimensions={0} | all-to-all | bytes 262144 | tf_op jit(solution)/shard_map/all_to_all | solution.py:26
  140.0 11.6 %all_to_all.32.refs_1_ = bf16[16,80,128]{2,1,0:T(8,128)(2,1)S(1)} all-to-all(bf16[16,80,128]{2,1,0:T(8,128)(2,1)S(1)} %broadcast_in_dim.27), channel_id=1, replica_groups=mesh['x'=4,'y'=4,'zh'=2,'core'=2,'emb'=8] {'x','y'}, dimensions={0} | all-to-all | bytes 655360 | tf_op jit(solution)/shard_map/all_to_all | solution.py:26
  151.6 7.1 %collective-permute-start.4 = (bf16[16,80,128]{2,1,0:T(8,128)(2,1)S(1)}, bf16[16,80,128]{2,1,0:T(8,128)(2,1)S(1)}, u32[]{:S(2)}, u32[]{:S(2)}) collective-permute-start(bf16[16,80,128]{2,1,0:T(8,128)(2,1)S(1)} %all_to_all.32.refs_1_), channel_id=1, source_target_pairs={{0,8},{8,0},{1,9},{9,1},{2,10},{10,2},{3,11},{11,3},{4,12},{12,4},... | collective-permute-start | bytes 983048 | tf_op jit(solution)/shard_map/ppermute | solution.py:304
  158.7 1.2 collective-permute-done.4.refs_2_
  160.0 0.0 copy-done.1
  160.0 2.0 %update.1 = (f32[1536,128]{1,0:T(8,128)}, f32[1536,128]{1,0:T(8,128)}, f32[128,512]{1,0:T(8,128)}, f32[128,512]{1,0:T(8,128)}) custom-call(s32[3]{0:T(128)S(1)} %copy-done.4, bf16[16,80,128]{2,1,0:T(8,128)(2,1)S(1)} %all_to_all.32.refs_1_, bf16[16,80,128]{2,1,0:T(8,128)(2,1)S(1)} %collective-permute-done.4.refs_2_, f32[1536,128]{1,0:T(8,128)S(1)} %copy-done, ...), custom_call_target="tpu_custom_call" | custom-call | tf_op jit(solution)/shard_map/update/pallas_call | solution.py:287
  (17 shorter events, 0.2 us)
Async XLA Ops:
  4.7 24.7 %all-to-all-start = ((bf16[8,112,128]{2,1,0:T(8,128)(2,1)}), bf16[8,112,128]{2,1,0:T(8,128)(2,1)S(1)}, u32[]{:S(2)}, u32[]{:S(2)}) async-start(bf16[8,112,128]{2,1,0:T(8,128)(2,1)} %get-tuple-element.17), calls=%async_computation | async-start | bytes 458752 | tf_op jit(solution)/shard_map/all_to_all | solution.py:26
  30.1 14.0 %collective-permute-start = (f32[16,48,128]{2,1,0:T(8,128)S(1)}, f32[16,48,128]{2,1,0:T(8,128)S(1)}, u32[]{:S(2)}, u32[]{:S(2)}) collective-permute-start(f32[16,48,128]{2,1,0:T(8,128)S(1)} %fusion.3), channel_id=1, source_target_pairs={{0,8},{8,0},{1,9},{9,1},{2,10},{10,2},{3,11},{11,3},{4,12},{12,4},... | collective-permute-start | bytes 1179656 | tf_op jit(solution)/shard_map/ppermute | solution.py:304
  38.8 15.8 %all-to-all-start.1 = ((bf16[8,64,128]{2,1,0:T(8,128)(2,1)}), bf16[8,64,128]{2,1,0:T(8,128)(2,1)S(1)}, u32[]{:S(2)}, u32[]{:S(2)}) async-start(bf16[8,64,128]{2,1,0:T(8,128)(2,1)} %bitcast.9), calls=%async_computation.1 | async-start | bytes 262144 | tf_op jit(solution)/shard_map/all_to_all | solution.py:26
  44.7 37.2 %copy-start.7 = (f32[2048]{0:T(1024)S(1)}, f32[2048]{0:T(1024)}, u32[]{:S(2)}) copy-start(f32[2048]{0:T(1024)} %param.17) | copy-start | bytes 24580
  44.7 39.6 %copy-start.2 = (bf16[128,512]{1,0:T(8,128)(2,1)S(1)}, bf16[128,512]{1,0:T(8,128)(2,1)}, u32[]{:S(2)}) copy-start(bf16[128,512]{1,0:T(8,128)(2,1)} %w_gate_ref.1) | copy-start | bytes 393220
  44.7 39.6 %copy-start.3 = (bf16[128,512]{1,0:T(8,128)(2,1)S(1)}, bf16[128,512]{1,0:T(8,128)(2,1)}, u32[]{:S(2)}) copy-start(bf16[128,512]{1,0:T(8,128)(2,1)} %w_up_ref.1) | copy-start | bytes 393220
  44.7 39.6 %copy-start.4 = (s32[3]{0:T(128)S(1)}, s32[3]{0:T(128)}, u32[]{:S(2)}) copy-start(s32[3]{0:T(128)} %pad_add_fusion.refs_0_.here_ref) | copy-start | bytes 40
  44.7 39.6 %copy-start.5 = (s32[1,256]{1,0:T(1,128)S(1)}, s32[1,256]{1,0:T(1,128)}, u32[]{:S(2)}) copy-start(s32[1,256]{1,0:T(1,128)} %get-tuple-element.19.target_ref) | copy-start | bytes 3076
  44.7 39.6 %copy-start.6 = (f32[128]{0:T(128)S(1)}, f32[128]{0:T(128)}, u32[]{:S(2)}) copy-start(f32[128]{0:T(128)} %param.18) | copy-start | bytes 1540
  76.3 8.0 %collective-permute-start.1 = (bf16[4352,128]{1,0:T(8,128)(2,1)S(1)}, bf16[4352,128]{1,0:T(8,128)(2,1)}, u32[]{:S(2)}, u32[]{:S(2)}) collective-permute-start(bf16[4352,128]{1,0:T(8,128)(2,1)S(1)} %bitcast.31), channel_id=1, source_target_pairs={{0,8},{8,0},{1,9},{9,1},{2,10},{10,2},{3,11},{11,3},{4,12},{12,4},... | collective-permute-start | bytes 3342344 | tf_op jit(solution)/shard_map/ppermute | solution.py:304
  92.6 4.6 %collective-permute-start.2 = (bf16[4096,128]{1,0:T(8,128)(2,1)S(1)}, bf16[4096,128]{1,0:T(8,128)(2,1)S(1)}, u32[]{:S(2)}, u32[]{:S(2)}) collective-permute-start(bf16[4096,128]{1,0:T(8,128)(2,1)S(1)} %slice_bitcast_fusion), channel_id=1, source_target_pairs={{0,8},{8,0},{1,9},{9,1},{2,10},{10,2},{3,11},{11,3},{4,12},{12,4},... | collective-permute-start | bytes 3145736 | tf_op jit(solution)/shard_map/ppermute | solution.py:304
  98.5 61.5 %copy-start = (f32[1536,128]{1,0:T(8,128)S(1)}, f32[1536,128]{1,0:T(8,128)}, u32[]{:S(2)}) copy-start(f32[1536,128]{1,0:T(8,128)} %refs_3_.3) | copy-start | bytes 2359300
  98.5 61.5 %copy-start.1 = (f32[1536,128]{1,0:T(8,128)S(1)}, f32[1536,128]{1,0:T(8,128)}, u32[]{:S(2)}) copy-start(f32[1536,128]{1,0:T(8,128)} %refs_4_.1) | copy-start | bytes 2359300
  98.5 20.9 %all-to-all-start.3 = ((bf16[16,256,128]{2,1,0:T(8,128)(2,1)}), bf16[16,256,128]{2,1,0:T(8,128)(2,1)}, u32[]{:S(2)}, u32[]{:S(2)}) async-start(bf16[16,256,128]{2,1,0:T(8,128)(2,1)} %bitcast.35), calls=%async_computation.3 | async-start | bytes 2097152 | tf_op jit(solution)/shard_map/all_to_all | solution.py:26
  103.0 13.3 %collective-permute-start.3 = (f32[48,128]{1,0:T(8,128)S(1)}, f32[48,128]{1,0:T(8,128)S(1)}, u32[]{:S(2)}, u32[]{:S(2)}) collective-permute-start(f32[48,128]{1,0:T(8,128)S(1)} %convert_reduce_fusion), channel_id=1, source_target_pairs={{0,16},{16,0},{1,17},{17,1},{2,18},{18,2},{3,19},{19,3},{4,20},{20... | collective-permute-start | bytes 73736 | tf_op jit(solution)/shard_map/ppermute | solution.py:304
  151.6 8.3 %collective-permute-start.4 = (bf16[16,80,128]{2,1,0:T(8,128)(2,1)S(1)}, bf16[16,80,128]{2,1,0:T(8,128)(2,1)S(1)}, u32[]{:S(2)}, u32[]{:S(2)}) collective-permute-start(bf16[16,80,128]{2,1,0:T(8,128)(2,1)S(1)} %all_to_all.32.refs_1_), channel_id=1, source_target_pairs={{0,8},{8,0},{1,9},{9,1},{2,10},{10,2},{3,11},{11,3},{4,12},{12,4},... | collective-permute-start | bytes 983048 | tf_op jit(solution)/shard_map/ppermute | solution.py:304

commit v4 on v3

--- a/solution.py
+++ b/solution.py
@@ -68,9 +68,7 @@
     return code, owner * capacity + rank
 
 
-def pack_kernel(
-    here_ref, *refs, capacity, rows_shard
-):
+def pack_kernel(*refs, capacity, rows_shard):
     sources, (out_ref, pos_ref), buffers, sems = refs[:7], refs[7:9], refs[9:16], refs[16]
     copies = [
         pltpu.make_async_copy(source, buffer, sems.at[i])
@@ -93,11 +91,11 @@
     slot_row = lax.broadcasted_iota(jnp.int32, (slots, prev_pos.shape[1]), 0)
     pack = jnp.where(slot_row == prev_pos, 1.0, 0.0).astype(bf16)
     rows = dot32(pack, grads_ref[...]).astype(bf16)
-    at = here_ref[2]
+    at = lax.axis_index(XY)
     cut = (pl.ds(pl.multiple_of((at % 4) * 32, 32), 32), pl.ds(pl.multiple_of((at // 4) * 128, 128), 128))
     gate_slice = w_gate_ref[cut].astype(f32)
     up_slice = w_up_ref[cut].astype(f32)
-    own = jnp.where(here_ref[0] == 0, gate_slice, up_slice).astype(bf16)
+    own = jnp.where(lax.axis_index("core") == 0, gate_slice, up_slice).astype(bf16)
     out = jnp.concatenate([w_out_ref[...].astype(f32), jnp.zeros((12, 128), f32)], axis=0)
     tail_row = lax.broadcasted_iota(jnp.int32, (16, 128), 0)
     for shard in range(shards):
@@ -108,7 +106,7 @@
         out_ref[shard, capacity + 32 : capacity + 48, :] = tail.astype(bf16)
 
 
-def pack(here, cur_ids, prev_ids, prev_grads, row_place, w_gate, w_up, w_out, shards, capacity, rows_shard):
+def pack(cur_ids, prev_ids, prev_grads, row_place, w_gate, w_up, w_out, shards, capacity, rows_shard):
     vmem = pl.BlockSpec(memory_space=pltpu.VMEM)
     tok = cur_ids.shape[0]
     arrays = (
@@ -121,14 +119,13 @@
             jax.ShapeDtypeStruct((shards, capacity + 48, 128), bf16),
             jax.ShapeDtypeStruct((1, tok), jnp.int32),
         ),
-        in_specs=[pl.BlockSpec(memory_space=pltpu.SMEM)]
-        + [pl.BlockSpec(memory_space=pltpu.HBM)] * len(arrays),
+        in_specs=[pl.BlockSpec(memory_space=pltpu.HBM)] * len(arrays),
         out_specs=(vmem, vmem),
         scratch_shapes=[pltpu.VMEM(array.shape, array.dtype) for array in arrays]
         + [pltpu.SemaphoreType.DMA((len(arrays),))],
         compiler_params=pltpu.CompilerParams(vmem_limit_bytes=62 * 1024 * 1024),
         name="pack",
-    )(here, *arrays)
+    )(*arrays)
 
 
 def decoded(line, capacity):
@@ -137,15 +134,15 @@
 
 
 def tower_kernel(
-    here_ref, answers_ref, target_ref, own_ref, other_ref, w_gate_ref, w_up_ref, shared_ref,
+    answers_ref, target_ref, own_ref, other_ref, w_gate_ref, w_up_ref, shared_ref,
     gain_ref, labels_ref, emb_grad_ref, grads_ref, weights_s, gate_s, up_s, sig_s,
 ):
     tok = target_ref.shape[1]
     width = answers_ref.shape[1]
     shards, span = shared_ref.shape[:2]
     lines = own_ref.shape[0] // 16
-    core = here_ref[0]
-    home = here_ref[1]
+    core = lax.axis_index("core")
+    home = lax.axis_index("emb")
     weights_s[core] = own_ref[...]
     weights_s[1 - core] = other_ref[...]
     slot_row = lax.broadcasted_iota(jnp.int32, (answers_ref.shape[0], tok), 0)
@@ -233,7 +230,7 @@
     ) * jnp.mean(values * scaled, axis=1, keepdims=True)
 
 
-def tower(here, answers, target, own, other, w_gate, w_up, shared, gain, labels):
+def tower(answers, target, own, other, w_gate, w_up, shared, gain, labels):
     tok = target.shape[1]
     width = answers.shape[1]
     shards = shared.shape[0]
@@ -244,7 +241,7 @@
             jax.ShapeDtypeStruct((tok, width), f32),
             jax.ShapeDtypeStruct((2, shards * 512, width), bf16),
         ),
-        in_specs=[pl.BlockSpec(memory_space=pltpu.SMEM)] + [vmem] * 9,
+        in_specs=[vmem] * 9,
         out_specs=(vmem, vmem),
         scratch_shapes=[pltpu.VMEM((2, *own.shape), bf16)]
         + [pltpu.VMEM((2 * shards, tok, 256), f32)] * 3,
@@ -254,16 +251,16 @@
         ),
         name="tower",
     )(
-        here, answers, target, own, other, w_gate, w_up, shared,
+        answers, target, own, other, w_gate, w_up, shared,
         gain.reshape(1, -1), labels.reshape(shards, tok),
     )
 
 
 def update_kernel(
-    here_ref, own_ref, other_ref, table_ref, accum_ref,
+    own_ref, other_ref, table_ref, accum_ref,
     new_table_ref, new_accum_ref, gate_ref, up_ref, both_s, *, scale,
 ):
-    core = here_ref[0]
+    core = lax.axis_index("core")
     both_s[core] = own_ref[...]
     both_s[1 - core] = other_ref[...]
     plane, lines = own_ref.shape[:2]
@@ -281,7 +278,7 @@
             new_table_ref[rows, :] = table_ref[rows, :] - learn_rate * grad * lax.rsqrt(total)
 
 
-def update(here, own, other, table, accum, scale):
+def update(own, other, table, accum, scale):
     vmem = pl.BlockSpec(memory_space=pltpu.VMEM)
     part = jax.ShapeDtypeStruct((128, 512), f32)
     return pl.pallas_call(
@@ -292,12 +289,12 @@
             part,
             part,
         ),
-        in_specs=[pl.BlockSpec(memory_space=pltpu.SMEM)] + [vmem] * 4,
+        in_specs=[vmem] * 4,
         out_specs=(vmem,) * 4,
         scratch_shapes=[pltpu.VMEM((2, *own.shape), bf16)],
         compiler_params=pltpu.CompilerParams(vmem_limit_bytes=12 * 1024 * 1024),
         name="update",
-    )(here, own, other, table, accum)
+    )(own, other, table, accum)
 
 
 def swapped(array, axis):
@@ -315,10 +312,8 @@
     slots = shards * capacity
     core = lax.axis_index("core")
     home = lax.axis_index("emb")
-    here = jnp.stack([core, home, lax.axis_index(XY)]).astype(jnp.int32)
-
     payload, cur_pos = pack(
-        here, cur_ids, prev_ids, prev_grads, row_place, w_gate, w_up, w_out,
+        cur_ids, prev_ids, prev_grads, row_place, w_gate, w_up, w_out,
         shards, capacity, rows_shard,
     )
     first = exchange(payload, "emb")
@@ -341,32 +336,29 @@
         hot = (half_ids + side * span)[:, None] == got_slots[None, :]
         return dot32(hot.astype(bf16), got_rows).reshape(plane, span, width)
 
-    received = swapped(half_sum(1 - core), "core")
-    pair_grad = (half_sum(core) + received).astype(bf16)
+    pair_sent = swapped(half_sum(1 - core), "core")
+    pair_own = half_sum(core)
 
     foreign = lax.dynamic_slice(
         jnp.concatenate([slices, slices], axis=0), (home + 1, 0, 0), (shards - 1, 32, 128)
     ).reshape((shards - 1) * 32, 128)
-    lines = foreign.shape[0]
-    plane_in = jnp.concatenate(
-        [jnp.broadcast_to(foreign[None], (plane, *foreign.shape)), pair_grad], axis=1
-    )
-    answers, plane_in = lax.optimization_barrier((answers, plane_in))
-    planes = exchange(plane_in, XY)
-    own_weights = planes.reshape(-1, 128)
+    own_weights = lax.all_gather(foreign, XY, axis=0, tiled=True)
     other_weights = swapped(own_weights, "core")
-    half_grad = planes[:, lines:].astype(f32).sum(axis=0)
+    answers, pair_own, pair_sent = lax.optimization_barrier((answers, pair_own, pair_sent))
 
     emb_grad, tower_grads = tower(
-        here, answers, cur_pos, own_weights, other_weights, w_gate, w_up, first, gain, labels
+        answers, cur_pos, own_weights, other_weights, w_gate, w_up, first, gain, labels
     )
 
     received = swapped(tower_grads[1], "core")
     core_sum = (tower_grads[0].astype(f32) + received.astype(f32)).astype(bf16)
-    second = exchange(core_sum.reshape(plane, shards * 32, 128), XY)
+    pair_grad = (pair_own + pair_sent).astype(bf16)
+    second = exchange(
+        jnp.concatenate([core_sum.reshape(plane, shards * 32, 128), pair_grad], axis=1), XY
+    )
+    plane_sum = second[:, : shards * 32].astype(f32).sum(axis=0).astype(bf16)
+    half_grad = second[:, shards * 32 :].astype(f32).sum(axis=0)
     total_grad = (half_grad + swapped(half_grad, "zh")).astype(bf16)
-    second, total_grad = lax.optimization_barrier((second, total_grad))
-    plane_sum = second.astype(f32).sum(axis=0).astype(bf16)
     for_z = jnp.broadcast_to(plane_sum.reshape(1, shards, 32, 128), (2, shards, 32, 128))
     third = exchange(for_z.reshape(2 * shards, 32, 128), ZZ)
     tower_sum = third.astype(f32).sum(axis=0).astype(bf16)
@@ -374,7 +366,7 @@
     other = swapped(own, "core")
 
     tower_scale = 1.0 / math.sqrt(tok * shards * lax.axis_size(DP))
-    new_table, new_accum, gate_sum, up_sum = update(here, own, other, table, accum, tower_scale)
+    new_table, new_accum, gate_sum, up_sum = update(own, other, table, accum, tower_scale)
     return (new_table, new_accum, gate_sum, up_sum, emb_grad)
 
 

time: 163 us -> 158 us (0.969)
  waiting for transfers between devices: 35.8 us -> 25.1 us
  starting transfers between devices: 51.6 us -> 59.5 us
  Pallas kernels: 13.8 us -> 11.3 us
  other arithmetic: 3.66 us -> 1.9 us
    all_gather x0 -> x1, blocking collectives: none -> 20.4 us  [step(): own_weights = lax.all_gather(foreign, XY, axis=0, tiled=True)]
    all_to_all x3 -> x2, blocking collectives: 52.5 us -> 33.6 us  [exchange(): return lax.all_to_all(pieces, axis, 0, 0, tiled=True)]
    all_to_all x3, waiting for transfers between devices: 24.5 us -> 17.1 us  [exchange(): return lax.all_to_all(pieces, axis, 0, 0, tiled=True)]
    ppermute x5, starting transfers between devices: 28.9 us -> 33.8 us  [swapped(): return lax.ppermute(array, axis, [(0, 1), (1, 0)])]
    ppermute x5, waiting for transfers between devices: 11.3 us -> 8.04 us  [swapped(): return lax.ppermute(array, axis, [(0, 1), (1, 0)])]
    all_to_all x3, starting transfers between devices: 22.7 us -> 25.7 us  [exchange(): return lax.all_to_all(pieces, axis, 0, 0, tiled=True)]
  transfers between devices with their start and end apart: 8 -> 8, of which waited for: 7 -> 6; matrix products, arithmetic and copies ran while one was open for 2% -> 3% of each run, Pallas kernels for 0% -> 0%
where the time goes in v4:
time: 158 us; the launch traced here: 157 us
  starting transfers between devices  59.5 us (38%)
  blocking collectives  54 us (34%)
  waiting for transfers between devices  25.1 us (16%)
  Pallas kernels  11.3 us (7%)
  matrix products  3.69 us (2%)
  other arithmetic  1.9 us (1%)
    ppermute x5, starting transfers between devices, swapped(): return lax.ppermute(array, axis, [(0, 1), (1, 0)])  33.8 us
    all_to_all x2, blocking collectives, exchange(): return lax.all_to_all(pieces, axis, 0, 0, tiled=True)  33.6 us
    all_to_all x3, starting transfers between devices, exchange(): return lax.all_to_all(pieces, axis, 0, 0, tiled=True)  25.7 us
    all_gather x1, blocking collectives, step(): own_weights = lax.all_gather(foreign, XY, axis=0, tiled=True)  20.4 us
    all_to_all x3, waiting for transfers between devices, exchange(): return lax.all_to_all(pieces, axis, 0, 0, tiled=True)  17.1 us
    ppermute x5, waiting for transfers between devices, swapped(): return lax.ppermute(array, axis, [(0, 1), (1, 0)])  8.04 us
    pallas_call x1, Pallas kernels, tower(): pl.pallas_call(tower_kernel, out_shape=(jax.ShapeDtypeStruct((tok, width)...  6.86 us
    dot_general x3, matrix products, dot32(): return jnp.dot(a, b, preferred_element_type=f32)  3.69 us
  transfers between devices with their start and end apart: 8, of which 6 were waited for; matrix products, arithmetic and copies ran while one was open for 3% of the time, Pallas kernels for 0%

profile of v4, /device:TPU:1, one launch (start us, length us, event | category | flops | bytes accessed | tf_op | source)
XLA Modules:
  0.0 157.3 jit_solution(7032741720554176245)
XLA Ops:
  0.6 0.0 copy-start
  0.6 2.9 %pack.1 = (bf16[8,112,128]{2,1,0:T(8,128)(2,1)}, s32[1,256]{1,0:T(1,128)}) custom-call(s32[1,256]{1,0:T(1,128)} %bitcast.36, s32[1,256]{1,0:T(1,128)} %bitcast.37, bf16[256,128]{1,0:T(8,128)(2,1)} %refs_2_.2, s32[96,128]{1,0:T(8,128)} %bitcast.34, bf16[128,512]{1,0:T(8,128)(2,1)} %w_gate_ref.1, bf16[128,512]{1,0:T(8,128)(2,1)} %w_up_ref.1, ...), custom_call_target="tpu_custom_call" | custom-call | tf_op jit(solution)/shard_map/pack/pallas_call | solution.py:116
  3.5 13.1 %all-to-all-start = ((bf16[8,112,128]{2,1,0:T(8,128)(2,1)}), bf16[8,112,128]{2,1,0:T(8,128)(2,1)S(1)}, u32[]{:S(2)}, u32[]{:S(2)}) async-start(bf16[8,112,128]{2,1,0:T(8,128)(2,1)} %get-tuple-element.16), calls=%async_computation | async-start | bytes 458752 | tf_op jit(solution)/shard_map/all_to_all | solution.py:26
  16.7 11.6 %all-to-all-done.shared_ref = bf16[8,112,128]{2,1,0:T(8,128)(2,1)S(1)} async-done(((bf16[8,112,128]{2,1,0:T(8,128)(2,1)}), bf16[8,112,128]{2,1,0:T(8,128)(2,1)S(1)}, u32[]{:S(2)}, u32[]{:S(2)}) %all-to-all-start) | async-done | bytes 229408 | tf_op jit(solution)/shard_map/all_to_all | solution.py:26
  28.3 0.1 slice_add_fusion
  28.4 0.1 fusion.13
  28.5 0.0 copy-start.2
  28.5 0.0 copy-start.3
  28.5 0.0 copy-start.4
  28.5 0.0 copy-start.5
  28.5 20.4 %all_gather.3.own_ref = bf16[3584,128]{1,0:T(8,128)(2,1)S(1)} all-gather(bf16[224,128]{1,0:T(8,128)(2,1)S(1)} %bitcast.31), channel_id=1, replica_groups=mesh['x'=4,'y'=4,'zh'=2,'core'=2,'emb'=8] {'x','y'}, dimensions={0}, use_global_device_ids=true | all-gather | bytes 974848 | tf_op jit(solution)/shard_map/all_gather | solution.py:345
  49.0 10.7 %collective-permute-start.1 = (bf16[3584,128]{1,0:T(8,128)(2,1)S(1)}, bf16[3584,128]{1,0:T(8,128)(2,1)S(1)}, u32[]{:S(2)}, u32[]{:S(2)}) collective-permute-start(bf16[3584,128]{1,0:T(8,128)(2,1)S(1)} %all_gather.3.own_ref), channel_id=1, source_target_pairs={{0,8},{8,0},{1,9},{9,1},{2,10},{10,2},{3,11},{11,3},{4,12},{12,4},... | collective-permute-start | bytes 2752520 | tf_op jit(solution)/shard_map/ppermute | solution.py:301
  59.6 0.1 slice_add_fusion.1
  59.7 0.1 eq.58
  59.8 0.1 eq.53
  59.8 0.0 copy-done
  59.8 1.3 fusion.7
  61.2 5.2 %all-to-all-start.1 = ((bf16[8,64,128]{2,1,0:T(8,128)(2,1)}), bf16[8,64,128]{2,1,0:T(8,128)(2,1)S(1)}, u32[]{:S(2)}, u32[]{:S(2)}) async-start(bf16[8,64,128]{2,1,0:T(8,128)(2,1)} %bitcast.6), calls=%async_computation.1 | async-start | bytes 262144 | tf_op jit(solution)/shard_map/all_to_all | solution.py:26
  66.4 1.2 fusion.3
  67.6 2.2 %collective-permute-start = (f32[16,48,128]{2,1,0:T(8,128)}, f32[16,48,128]{2,1,0:T(8,128)}, u32[]{:S(2)}, u32[]{:S(2)}) collective-permute-start(f32[16,48,128]{2,1,0:T(8,128)} %fusion.3), channel_id=1, source_target_pairs={{0,8},{8,0},{1,9},{9,1},{2,10},{10,2},{3,11},{11,3},{4,12},{12,4},... | collective-permute-start | bytes 1179656 | tf_op jit(solution)/shard_map/ppermute | solution.py:301
  69.8 0.0 copy-done.7
  69.8 1.2 fusion.5
  71.0 0.5 collective-permute-done
  71.5 5.4 %all-to-all-done.1 = bf16[8,64,128]{2,1,0:T(8,128)(2,1)S(1)} async-done(((bf16[8,64,128]{2,1,0:T(8,128)(2,1)}), bf16[8,64,128]{2,1,0:T(8,128)(2,1)S(1)}, u32[]{:S(2)}, u32[]{:S(2)}) %all-to-all-start.1) | async-done | bytes 131104 | tf_op jit(solution)/shard_map/all_to_all | solution.py:26
  77.0 0.0 collective-permute-done.1.other_ref
  77.0 0.0 copy-done.2
  77.0 0.0 copy-done.3
  77.0 0.0 copy-done.4
  77.0 0.0 copy-done.5
  77.0 6.9 %tower.1 = (f32[256,128]{1,0:T(8,128)}, bf16[2,4096,128]{2,1,0:T(8,128)(2,1)S(1)}) custom-call(bf16[512,128]{1,0:T(8,128)(2,1)S(1)} %bitcast.27, s32[1,256]{1,0:T(1,128)S(1)} %copy-done.4, bf16[3584,128]{1,0:T(8,128)(2,1)S(1)} %all_gather.3.own_ref, bf16[3584,128]{1,0:T(8,128)(2,1)S(1)} %collective-permute-done.1.other_ref, bf16[128,512]{1,0:T(8,128)(2,1)S(1)} %copy-done.2, ...), custom_call_target="tpu_custom_call" | custom-call | flops 1610612736 | bytes 5242880 | tf_op jit(solution)/shard_map/tower/pallas_call | solution.py:238
  83.9 0.1 slice_bitcast_fusion
  83.9 4.3 %collective-permute-start.2 = (bf16[4096,128]{1,0:T(8,128)(2,1)S(1)}, bf16[4096,128]{1,0:T(8,128)(2,1)S(1)}, u32[]{:S(2)}, u32[]{:S(2)}) collective-permute-start(bf16[4096,128]{1,0:T(8,128)(2,1)S(1)} %slice_bitcast_fusion), channel_id=1, source_target_pairs={{0,8},{8,0},{1,9},{9,1},{2,10},{10,2},{3,11},{11,3},{4,12},{12,4},... | collective-permute-start | bytes 3145736 | tf_op jit(solution)/shard_map/ppermute | solution.py:301
  88.3 0.0 copy-done.6
  88.3 1.1 add_convert_fusion
  89.4 1.2 collective-permute-done.2
  90.6 0.3 fusion.1
  90.8 0.1 pad_maximum_fusion
  90.9 22.4 %all_to_all.25 = bf16[16,304,128]{2,1,0:T(8,128)(2,1)S(1)} all-to-all(bf16[16,304,128]{2,1,0:T(8,128)(2,1)S(1)} %pad_maximum_fusion), channel_id=1, replica_groups=mesh['x'=4,'y'=4,'zh'=2,'core'=2,'emb'=8] {'x','y'}, dimensions={0} | all-to-all | bytes 2490368 | tf_op jit(solution)/shard_map/all_to_all | solution.py:26
  113.4 0.1 slice_reduce_fusion
  113.5 0.7 broadcast_in_dim.7
  114.2 7.4 %all-to-all-start.3 = ((bf16[16,32,128]{2,1,0:T(8,128)(2,1)}), bf16[16,32,128]{2,1,0:T(8,128)(2,1)S(1)}, u32[]{:S(2)}, u32[]{:S(2)}) async-start(bf16[16,32,128]{2,1,0:T(8,128)(2,1)} %bitcast.18), calls=%async_computation.3 | async-start | bytes 262144 | tf_op jit(solution)/shard_map/all_to_all | solution.py:26
  121.6 12.0 %collective-permute-start.3 = (f32[48,128]{1,0:T(8,128)S(1)}, f32[48,128]{1,0:T(8,128)S(1)}, u32[]{:S(2)}, u32[]{:S(2)}) collective-permute-start(f32[48,128]{1,0:T(8,128)S(1)} %convert_reduce_fusion), channel_id=1, source_target_pairs={{0,16},{16,0},{1,17},{17,1},{2,18},{18,2},{3,19},{19,3},{4,20},{20... | collective-permute-start | bytes 73736 | tf_op jit(solution)/shard_map/ppermute | solution.py:301
  133.6 5.1 %collective-permute-done.3 = f32[48,128]{1,0:T(8,128)S(1)} collective-permute-done((f32[48,128]{1,0:T(8,128)S(1)}, f32[48,128]{1,0:T(8,128)S(1)}, u32[]{:S(2)}, u32[]{:S(2)}) %collective-permute-start.3) | collective-permute-done | bytes 24608 | tf_op jit(solution)/shard_map/ppermute | solution.py:301
  138.7 0.0 all-to-all-done.3
  138.8 11.1 %all_to_all.26.refs_0_ = bf16[16,80,128]{2,1,0:T(8,128)(2,1)S(1)} all-to-all(bf16[16,80,128]{2,1,0:T(8,128)(2,1)S(1)} %broadcast_in_dim.8), channel_id=1, replica_groups=mesh['x'=4,'y'=4,'zh'=2,'core'=2,'emb'=8] {'x','y'}, dimensions={0} | all-to-all | bytes 655360 | tf_op jit(solution)/shard_map/all_to_all | solution.py:26
  150.0 4.6 %collective-permute-start.4 = (bf16[16,80,128]{2,1,0:T(8,128)(2,1)S(1)}, bf16[16,80,128]{2,1,0:T(8,128)(2,1)S(1)}, u32[]{:S(2)}, u32[]{:S(2)}) collective-permute-start(bf16[16,80,128]{2,1,0:T(8,128)(2,1)S(1)} %all_to_all.26.refs_0_), channel_id=1, source_target_pairs={{0,8},{8,0},{1,9},{9,1},{2,10},{10,2},{3,11},{11,3},{4,12},{12,4},... | collective-permute-start | bytes 983048 | tf_op jit(solution)/shard_map/ppermute | solution.py:301
  154.5 1.2 collective-permute-done.4.refs_1_
  155.8 1.5 update.1
  (16 shorter events, 0.2 us)
Async XLA Ops:
  0.6 59.2 %copy-start = (f32[1536,128]{1,0:T(8,128)S(1)}, f32[1536,128]{1,0:T(8,128)}, u32[]{:S(2)}) copy-start(f32[1536,128]{1,0:T(8,128)} %refs_2_.3) | copy-start | bytes 2359300
  3.5 24.8 %all-to-all-start = ((bf16[8,112,128]{2,1,0:T(8,128)(2,1)}), bf16[8,112,128]{2,1,0:T(8,128)(2,1)S(1)}, u32[]{:S(2)}, u32[]{:S(2)}) async-start(bf16[8,112,128]{2,1,0:T(8,128)(2,1)} %get-tuple-element.16), calls=%async_computation | async-start | bytes 458752 | tf_op jit(solution)/shard_map/all_to_all | solution.py:26
  16.6 53.2 %copy-start.7 = (f32[2048]{0:T(1024)S(1)}, f32[2048]{0:T(1024)}, u32[]{:S(2)}) copy-start(f32[2048]{0:T(1024)} %param.17) | copy-start | bytes 24580
  28.5 48.5 %copy-start.2 = (bf16[128,512]{1,0:T(8,128)(2,1)S(1)}, bf16[128,512]{1,0:T(8,128)(2,1)}, u32[]{:S(2)}) copy-start(bf16[128,512]{1,0:T(8,128)(2,1)} %w_gate_ref.1) | copy-start | bytes 393220
  28.5 48.5 %copy-start.3 = (bf16[128,512]{1,0:T(8,128)(2,1)S(1)}, bf16[128,512]{1,0:T(8,128)(2,1)}, u32[]{:S(2)}) copy-start(bf16[128,512]{1,0:T(8,128)(2,1)} %w_up_ref.1) | copy-start | bytes 393220
  28.5 48.5 %copy-start.4 = (s32[1,256]{1,0:T(1,128)S(1)}, s32[1,256]{1,0:T(1,128)}, u32[]{:S(2)}) copy-start(s32[1,256]{1,0:T(1,128)} %get-tuple-element.18.target_ref) | copy-start | bytes 3076
  28.5 48.5 %copy-start.5 = (f32[128]{0:T(128)S(1)}, f32[128]{0:T(128)}, u32[]{:S(2)}) copy-start(f32[128]{0:T(128)} %param.18) | copy-start | bytes 1540
  49.0 28.0 %collective-permute-start.1 = (bf16[3584,128]{1,0:T(8,128)(2,1)S(1)}, bf16[3584,128]{1,0:T(8,128)(2,1)S(1)}, u32[]{:S(2)}, u32[]{:S(2)}) collective-permute-start(bf16[3584,128]{1,0:T(8,128)(2,1)S(1)} %all_gather.3.own_ref), channel_id=1, source_target_pairs={{0,8},{8,0},{1,9},{9,1},{2,10},{10,2},{3,11},{11,3},{4,12},{12,4},... | collective-permute-start | bytes 2752520 | tf_op jit(solution)/shard_map/ppermute | solution.py:301
  61.2 15.8 %all-to-all-start.1 = ((bf16[8,64,128]{2,1,0:T(8,128)(2,1)}), bf16[8,64,128]{2,1,0:T(8,128)(2,1)S(1)}, u32[]{:S(2)}, u32[]{:S(2)}) async-start(bf16[8,64,128]{2,1,0:T(8,128)(2,1)} %bitcast.6), calls=%async_computation.1 | async-start | bytes 262144 | tf_op jit(solution)/shard_map/all_to_all | solution.py:26
  67.6 3.9 %collective-permute-start = (f32[16,48,128]{2,1,0:T(8,128)}, f32[16,48,128]{2,1,0:T(8,128)}, u32[]{:S(2)}, u32[]{:S(2)}) collective-permute-start(f32[16,48,128]{2,1,0:T(8,128)} %fusion.3), channel_id=1, source_target_pairs={{0,8},{8,0},{1,9},{9,1},{2,10},{10,2},{3,11},{11,3},{4,12},{12,4},... | collective-permute-start | bytes 1179656 | tf_op jit(solution)/shard_map/ppermute | solution.py:301
  83.9 4.4 %copy-start.6 = (f32[16,48,128]{2,1,0:T(8,128)S(1)}, f32[16,48,128]{2,1,0:T(8,128)}, u32[]{:S(2)}) copy-start(f32[16,48,128]{2,1,0:T(8,128)} %fusion.5) | copy-start | bytes 1179652
  83.9 6.6 %collective-permute-start.2 = (bf16[4096,128]{1,0:T(8,128)(2,1)S(1)}, bf16[4096,128]{1,0:T(8,128)(2,1)S(1)}, u32[]{:S(2)}, u32[]{:S(2)}) collective-permute-start(bf16[4096,128]{1,0:T(8,128)(2,1)S(1)} %slice_bitcast_fusion), channel_id=1, source_target_pairs={{0,8},{8,0},{1,9},{9,1},{2,10},{10,2},{3,11},{11,3},{4,12},{12,4},... | collective-permute-start | bytes 3145736 | tf_op jit(solution)/shard_map/ppermute | solution.py:301
  113.4 42.4 %copy-start.1 = (f32[1536,128]{1,0:T(8,128)S(1)}, f32[1536,128]{1,0:T(8,128)}, u32[]{:S(2)}) copy-start(f32[1536,128]{1,0:T(8,128)} %refs_3_.1) | copy-start | bytes 2359300
  114.2 24.5 %all-to-all-start.3 = ((bf16[16,32,128]{2,1,0:T(8,128)(2,1)}), bf16[16,32,128]{2,1,0:T(8,128)(2,1)S(1)}, u32[]{:S(2)}, u32[]{:S(2)}) async-start(bf16[16,32,128]{2,1,0:T(8,128)(2,1)} %bitcast.18), calls=%async_computation.3 | async-start | bytes 262144 | tf_op jit(solution)/shard_map/all_to_all | solution.py:26
  121.6 17.1 %collective-permute-start.3 = (f32[48,128]{1,0:T(8,128)S(1)}, f32[48,128]{1,0:T(8,128)S(1)}, u32[]{:S(2)}, u32[]{:S(2)}) collective-permute-start(f32[48,128]{1,0:T(8,128)S(1)} %convert_reduce_fusion), channel_id=1, source_target_pairs={{0,16},{16,0},{1,17},{17,1},{2,18},{18,2},{3,19},{19,3},{4,20},{20... | collective-permute-start | bytes 73736 | tf_op jit(solution)/shard_map/ppermute | solution.py:301
  150.0 5.8 %collective-permute-start.4 = (bf16[16,80,128]{2,1,0:T(8,128)(2,1)S(1)}, bf16[16,80,128]{2,1,0:T(8,128)(2,1)S(1)}, u32[]{:S(2)}, u32[]{:S(2)}) collective-permute-start(bf16[16,80,128]{2,1,0:T(8,128)(2,1)S(1)} %all_to_all.26.refs_0_), channel_id=1, source_target_pairs={{0,8},{8,0},{1,9},{9,1},{2,10},{10,2},{3,11},{11,3},{4,12},{12,4},... | collective-permute-start | bytes 983048 | tf_op jit(solution)/shard_map/ppermute | solution.py:301

commit v5 on v4

--- a/solution.py
+++ b/solution.py
@@ -74,10 +74,10 @@
         pltpu.make_async_copy(source, buffer, sems.at[i])
         for i, (source, buffer) in enumerate(zip(sources, buffers, strict=True))
     ]
-    for copy in copies:
-        copy.start()
-    for copy in copies:
-        copy.wait()
+    for i in (0, 1, 3, 2, 4, 5, 6):
+        copies[i].start()
+    for i in (0, 1, 3):
+        copies[i].wait()
     cur_ref, prev_ref, grads_ref, places_ref, w_gate_ref, w_up_ref, w_out_ref = buffers
     shards = out_ref.shape[0]
     places = places_ref[...]
@@ -90,6 +90,8 @@
     slots = shards * capacity
     slot_row = lax.broadcasted_iota(jnp.int32, (slots, prev_pos.shape[1]), 0)
     pack = jnp.where(slot_row == prev_pos, 1.0, 0.0).astype(bf16)
+    for i in (2, 4, 5, 6):
+        copies[i].wait()
     rows = dot32(pack, grads_ref[...]).astype(bf16)
     at = lax.axis_index(XY)
     cut = (pl.ds(pl.multiple_of((at % 4) * 32, 32), 32), pl.ds(pl.multiple_of((at // 4) * 128, 128), 128))
@@ -135,7 +137,7 @@
 
 def tower_kernel(
     answers_ref, target_ref, own_ref, other_ref, w_gate_ref, w_up_ref, shared_ref,
-    gain_ref, labels_ref, emb_grad_ref, grads_ref, weights_s, gate_s, up_s, sig_s,
+    gain_ref, labels_ref, table_part_ref, emb_grad_ref, grads_ref, weights_s, gate_s, up_s,
 ):
     tok = target_ref.shape[1]
     width = answers_ref.shape[1]
@@ -182,10 +184,10 @@
             gate = dot32(normed, block(hop, half, 0))
             up = dot32(normed, block(hop, half, 1))
             sig = jax.nn.sigmoid(gate)
-            gate_s[at] = gate
-            up_s[at] = up
-            sig_s[at] = sig
-            hidden = (gate * sig * up).astype(bf16).astype(f32)
+            act = gate * sig
+            gate_s[at] = up * (sig + act * (1.0 - sig))
+            up_s[at] = act
+            hidden = (act * up).astype(bf16).astype(f32)
             for j in range(2):
                 total = total + hidden[:, j * 128 : (j + 1) * 128] * out_row(shard, half, j)
         return total
@@ -201,13 +203,10 @@
         shard = (home + 1 + hop) % shards
         for half in range(2):
             at = hop * 2 + half
-            gate = gate_s[at]
-            up = up_s[at]
-            sig = sig_s[at]
             out = jnp.concatenate([out_row(shard, half, j) for j in range(2)], axis=1)
             back_hidden = slopes * out
-            back_gate = (back_hidden * up * sig * (1.0 + gate * (1.0 - sig))).astype(bf16)
-            back_up = (back_hidden * (gate * sig)).astype(bf16)
+            back_gate = (back_hidden * gate_s[at]).astype(bf16)
+            back_up = (back_hidden * up_s[at]).astype(bf16)
             for side, part in ((0, back_gate), (1, back_up)):
                 back = back + lax.dot_general(
                     part, block(hop, half, side), across, preferred_element_type=f32
@@ -218,19 +217,20 @@
                     tile = 2 * half + j
                     for k in range(4):
                         grads_ref[
-                            place, pl.ds((tile * 4 + k) * shards * 32 + shard * 32, 32), :
+                            place, tile * 4 + k, pl.ds(shard * 32, 32), :
                         ] = grad[k * 32 : (k + 1) * 32, j * 128 : (j + 1) * 128]
         return back
 
     back = backward(shards - 1, jnp.zeros((tok, width), f32), home_block)
     back = lax.fori_loop(0, shards - 1, lambda hop, b: backward(hop, b, far_block), back)
+    grads_ref[:, :, shards * 32 :, :] = table_part_ref[...].astype(bf16)
     scaled = back * gain
     emb_grad_ref[...] = inverse_rms * scaled - values * (
         inverse_rms * inverse_rms * inverse_rms
     ) * jnp.mean(values * scaled, axis=1, keepdims=True)
 
 
-def tower(answers, target, own, other, w_gate, w_up, shared, gain, labels):
+def tower(answers, target, own, other, w_gate, w_up, shared, gain, labels, table_part):
     tok = target.shape[1]
     width = answers.shape[1]
     shards = shared.shape[0]
@@ -239,20 +239,20 @@
         tower_kernel,
         out_shape=(
             jax.ShapeDtypeStruct((tok, width), f32),
-            jax.ShapeDtypeStruct((2, shards * 512, width), bf16),
-        ),
-        in_specs=[vmem] * 9,
+            jax.ShapeDtypeStruct((2, 16, shards * 32 + table_part.shape[2], width), bf16),
+        ),
+        in_specs=[vmem] * 10,
         out_specs=(vmem, vmem),
         scratch_shapes=[pltpu.VMEM((2, *own.shape), bf16)]
-        + [pltpu.VMEM((2 * shards, tok, 256), f32)] * 3,
-        compiler_params=pltpu.CompilerParams(vmem_limit_bytes=24 * 1024 * 1024),
+        + [pltpu.VMEM((2 * shards, tok, 256), f32)] * 2,
+        compiler_params=pltpu.CompilerParams(vmem_limit_bytes=20 * 1024 * 1024),
         cost_estimate=pl.CostEstimate(
             flops=6 * 2 * tok * width * 4096, bytes_accessed=5 << 20, transcendentals=2 << 20
         ),
         name="tower",
     )(
         answers, target, own, other, w_gate, w_up, shared,
-        gain.reshape(1, -1), labels.reshape(shards, tok),
+        gain.reshape(1, -1), labels.reshape(shards, tok), table_part,
     )
 
 
@@ -317,6 +317,7 @@
         shards, capacity, rows_shard,
     )
     first = exchange(payload, "emb")
+    rows_table = lax.optimization_barrier(table.astype(bf16))
     got_rows = first[:, :capacity].reshape(slots, width)
     slices = first[:, capacity : capacity + 32]
     wanted = decoded(first[:, capacity + 46], capacity)
@@ -324,38 +325,30 @@
 
     row_ids = jnp.arange(rows_shard, dtype=jnp.int32)
     fetched = dot32(
-        (wanted[:, None] == row_ids[None, :]).astype(bf16), table.astype(bf16)
+        (wanted[:, None] == row_ids[None, :]).astype(bf16), rows_table
     ).astype(bf16)
     answers = exchange(fetched.reshape(shards, capacity, width), "emb").reshape(slots, width)
 
     span = rows_shard // plane // 2
     half_ids = jnp.arange(rows_shard // 2, dtype=jnp.int32)
     half_ids = half_ids // span * (2 * span) + half_ids % span
-
-    def half_sum(side):
-        hot = (half_ids + side * span)[:, None] == got_slots[None, :]
-        return dot32(hot.astype(bf16), got_rows).reshape(plane, span, width)
-
-    pair_sent = swapped(half_sum(1 - core), "core")
-    pair_own = half_sum(core)
+    part_ids = jnp.concatenate([half_ids + core * span, half_ids + (1 - core) * span])
+    table_part = dot32((part_ids[:, None] == got_slots[None, :]).astype(bf16), got_rows)
+    table_part = table_part.reshape(2, plane, span, width)
 
     foreign = lax.dynamic_slice(
         jnp.concatenate([slices, slices], axis=0), (home + 1, 0, 0), (shards - 1, 32, 128)
     ).reshape((shards - 1) * 32, 128)
     own_weights = lax.all_gather(foreign, XY, axis=0, tiled=True)
     other_weights = swapped(own_weights, "core")
-    answers, pair_own, pair_sent = lax.optimization_barrier((answers, pair_own, pair_sent))
-
     emb_grad, tower_grads = tower(
-        answers, cur_pos, own_weights, other_weights, w_gate, w_up, first, gain, labels
+        answers, cur_pos, own_weights, other_weights, w_gate, w_up, first, gain, labels,
+        table_part,
     )
 
     received = swapped(tower_grads[1], "core")
     core_sum = (tower_grads[0].astype(f32) + received.astype(f32)).astype(bf16)
-    pair_grad = (pair_own + pair_sent).astype(bf16)
-    second = exchange(
-        jnp.concatenate([core_sum.reshape(plane, shards * 32, 128), pair_grad], axis=1), XY
-    )
+    second = exchange(core_sum, XY)
     plane_sum = second[:, : shards * 32].astype(f32).sum(axis=0).astype(bf16)
     half_grad = second[:, shards * 32 :].astype(f32).sum(axis=0)
     total_grad = (half_grad + swapped(half_grad, "zh")).astype(bf16)

time: 158 us -> 158 us (level)
  waiting for transfers between devices: 25.1 us -> 28.3 us
  starting transfers between devices: 59.5 us -> 57.1 us
  matrix products: 3.69 us -> 1.97 us
    all_to_all x3, waiting for transfers between devices: 17.1 us -> 19.5 us  [exchange(): return lax.all_to_all(pieces, axis, 0, 0, tiled=True)]
    ppermute x5 -> x4, starting transfers between devices: 33.8 us -> 31.4 us  [swapped(): return lax.ppermute(array, axis, [(0, 1), (1, 0)])]
    dot_general x3 -> x2, matrix products: 3.69 us -> 1.97 us  [dot32(): return jnp.dot(a, b, preferred_element_type=f32)]
    ppermute x5 -> x4, waiting for transfers between devices: 8.04 us -> 8.86 us  [swapped(): return lax.ppermute(array, axis, [(0, 1), (1, 0)])]
  transfers between devices with their start and end apart: 8 -> 7, of which waited for: 6 -> 5; matrix products, arithmetic and copies ran while one was open for 3% -> 3% of each run, Pallas kernels for 0% -> 0%
where the time goes in v5:
time: 158 us
  starting transfers between devices  57.1 us (36%)
  blocking collectives  54 us (34%)
  waiting for transfers between devices  28.3 us (18%)
  Pallas kernels  11.6 us (7%)
  other arithmetic  1.97 us (1%)
  matrix products  1.97 us (1%)
  local copies, waits for them, and re-layouts  1.71 us (1%)
    all_to_all x2, blocking collectives, exchange(): return lax.all_to_all(pieces, axis, 0, 0, tiled=True)  33.7 us
    ppermute x4, starting transfers between devices, swapped(): return lax.ppermute(array, axis, [(0, 1), (1, 0)])  31.4 us
    all_to_all x3, starting transfers between devices, exchange(): return lax.all_to_all(pieces, axis, 0, 0, tiled=True)  25.7 us
    all_gather x1, blocking collectives, step(): own_weights = lax.all_gather(foreign, XY, axis=0, tiled=True)  20.3 us
    all_to_all x3, waiting for transfers between devices, exchange(): return lax.all_to_all(pieces, axis, 0, 0, tiled=True)  19.5 us
    ppermute x4, waiting for transfers between devices, swapped(): return lax.ppermute(array, axis, [(0, 1), (1, 0)])  8.86 us
    pallas_call x1, Pallas kernels, tower(): pl.pallas_call(tower_kernel, out_shape=(jax.ShapeDtypeStruct((tok, width)...  7.24 us
  transfers between devices with their start and end apart: 7, of which 5 were waited for; matrix products, arithmetic and copies ran while one was open for 3% of the time, Pallas kernels for 0%

profile of v5, /device:TPU:1, one launch (start us, length us, event | category | flops | bytes accessed | tf_op | source)
XLA Modules:
  0.0 157.5 jit_solution(7526089651995072199)
XLA Ops:
  0.6 2.8 %pack.1 = (bf16[8,112,128]{2,1,0:T(8,128)(2,1)}, s32[1,256]{1,0:T(1,128)}) custom-call(s32[1,256]{1,0:T(1,128)} %bitcast.35, s32[1,256]{1,0:T(1,128)} %bitcast.36, bf16[256,128]{1,0:T(8,128)(2,1)} %refs_2_.2, s32[96,128]{1,0:T(8,128)} %bitcast.33, bf16[128,512]{1,0:T(8,128)(2,1)} %w_gate_ref.1, bf16[128,512]{1,0:T(8,128)(2,1)} %w_up_ref.1, ...), custom_call_target="tpu_custom_call" | custom-call | tf_op jit(solution)/shard_map/pack/pallas_call | solution.py:118
  3.4 13.1 %all-to-all-start = ((bf16[8,112,128]{2,1,0:T(8,128)(2,1)}), bf16[8,112,128]{2,1,0:T(8,128)(2,1)S(1)}, u32[]{:S(2)}, u32[]{:S(2)}) async-start(bf16[8,112,128]{2,1,0:T(8,128)(2,1)} %get-tuple-element.13), calls=%async_computation | async-start | bytes 458752 | tf_op jit(solution)/shard_map/all_to_all | solution.py:26
  16.5 0.7 reshape.126.labels_ref
  17.2 1.2 convert_element_type.44
  18.4 0.0 copy-start.2
  18.4 0.0 copy-start.3
  18.4 0.0 copy-start.4
  18.4 0.0 copy-start.5
  18.5 9.7 %all-to-all-done.shared_ref = bf16[8,112,128]{2,1,0:T(8,128)(2,1)S(1)} async-done(((bf16[8,112,128]{2,1,0:T(8,128)(2,1)}), bf16[8,112,128]{2,1,0:T(8,128)(2,1)S(1)}, u32[]{:S(2)}, u32[]{:S(2)}) %all-to-all-start) | async-done | bytes 229408 | tf_op jit(solution)/shard_map/all_to_all | solution.py:26
  28.2 0.1 fusion.8
  28.3 20.3 %all_gather.3.own_ref = bf16[3584,128]{1,0:T(8,128)(2,1)S(1)} all-gather(bf16[224,128]{1,0:T(8,128)(2,1)S(1)} %bitcast.31), channel_id=1, replica_groups=mesh['x'=4,'y'=4,'zh'=2,'core'=2,'emb'=8] {'x','y'}, dimensions={0}, use_global_device_ids=true | all-gather | bytes 974848 | tf_op jit(solution)/shard_map/all_gather | solution.py:342
  48.6 10.7 %collective-permute-start = (bf16[3584,128]{1,0:T(8,128)(2,1)S(1)}, bf16[3584,128]{1,0:T(8,128)(2,1)S(1)}, u32[]{:S(2)}, u32[]{:S(2)}) collective-permute-start(bf16[3584,128]{1,0:T(8,128)(2,1)S(1)} %all_gather.3.own_ref), channel_id=1, source_target_pairs={{0,8},{8,0},{1,9},{9,1},{2,10},{10,2},{3,11},{11,3},{4,12},{12,4},... | collective-permute-start | bytes 2752520 | tf_op jit(solution)/shard_map/ppermute | solution.py:301
  59.3 0.1 slice_add_fusion.1
  59.3 0.1 eq.37
  59.4 1.3 fusion.7
  60.7 5.2 %all-to-all-start.1 = ((bf16[8,64,128]{2,1,0:T(8,128)(2,1)}), bf16[8,64,128]{2,1,0:T(8,128)(2,1)S(1)}, u32[]{:S(2)}, u32[]{:S(2)}) async-start(bf16[8,64,128]{2,1,0:T(8,128)(2,1)} %bitcast.6), calls=%async_computation.1 | async-start | bytes 262144 | tf_op jit(solution)/shard_map/all_to_all | solution.py:26
  66.0 0.1 slice_add_fusion
  66.0 0.1 eq.42
  66.1 0.6 fusion.1.table_part_ref
  66.8 9.8 %all-to-all-done.1 = bf16[8,64,128]{2,1,0:T(8,128)(2,1)S(1)} async-done(((bf16[8,64,128]{2,1,0:T(8,128)(2,1)}), bf16[8,64,128]{2,1,0:T(8,128)(2,1)S(1)}, u32[]{:S(2)}, u32[]{:S(2)}) %all-to-all-start.1) | async-done | bytes 131104 | tf_op jit(solution)/shard_map/all_to_all | solution.py:26
  76.5 0.0 collective-permute-done.other_ref
  76.5 0.0 copy-done.2
  76.5 0.0 copy-done.3
  76.5 0.0 copy-done.4
  76.6 0.0 copy-done.5
  76.6 7.2 %tower.1 = (f32[256,128]{1,0:T(8,128)}, bf16[2,16,304,128]{3,2,1,0:T(8,128)(2,1)S(1)}) custom-call(bf16[512,128]{1,0:T(8,128)(2,1)S(1)} %bitcast.28, s32[1,256]{1,0:T(1,128)S(1)} %copy-done.4, bf16[3584,128]{1,0:T(8,128)(2,1)S(1)} %all_gather.3.own_ref, bf16[3584,128]{1,0:T(8,128)(2,1)S(1)} %collective-permute-done.other_ref, ...), custom_call_target="tpu_custom_call" | custom-call | flops 1610612736 | bytes 5242880 | tf_op jit(solution)/shard_map/tower/pallas_call | solution.py:238
  83.8 0.1 slice_bitcast_fusion
  83.9 4.2 %collective-permute-start.1 = (bf16[16,304,128]{2,1,0:T(8,128)(2,1)S(1)}, bf16[16,304,128]{2,1,0:T(8,128)(2,1)S(1)}, u32[]{:S(2)}, u32[]{:S(2)}) collective-permute-start(bf16[16,304,128]{2,1,0:T(8,128)(2,1)S(1)} %slice_bitcast_fusion), channel_id=1, source_target_pairs={{0,8},{8,0},{1,9},{9,1},{2,10},{10,2},{3,11},{11,3},{4,12},{12,4},... | collective-permute-start | bytes 3735560 | tf_op jit(solution)/shard_map/ppermute | solution.py:301
  88.1 2.5 %collective-permute-done.1 = bf16[16,304,128]{2,1,0:T(8,128)(2,1)S(1)} collective-permute-done((bf16[16,304,128]{2,1,0:T(8,128)(2,1)S(1)}, bf16[16,304,128]{2,1,0:T(8,128)(2,1)S(1)}, u32[]{:S(2)}, u32[]{:S(2)}) %collective-permute-start.1) | collective-permute-done | bytes 1245216 | tf_op jit(solution)/shard_map/ppermute | solution.py:301
  90.6 0.3 fusion.3
  91.0 0.0 copy-start
  91.0 0.0 copy-start.1
  91.0 22.6 %all_to_all.25 = bf16[16,304,128]{2,1,0:T(8,128)(2,1)S(1)} all-to-all(bf16[16,304,128]{2,1,0:T(8,128)(2,1)S(1)} %fusion.3), channel_id=1, replica_groups=mesh['x'=4,'y'=4,'zh'=2,'core'=2,'emb'=8] {'x','y'}, dimensions={0} | all-to-all | bytes 2490368 | tf_op jit(solution)/shard_map/all_to_all | solution.py:26
  113.6 0.1 slice_reduce_fusion
  113.7 0.7 broadcast_in_dim.7
  114.4 7.4 %all-to-all-start.3 = ((bf16[16,32,128]{2,1,0:T(8,128)(2,1)}), bf16[16,32,128]{2,1,0:T(8,128)(2,1)S(1)}, u32[]{:S(2)}, u32[]{:S(2)}) async-start(bf16[16,32,128]{2,1,0:T(8,128)(2,1)} %bitcast.17), calls=%async_computation.3 | async-start | bytes 262144 | tf_op jit(solution)/shard_map/all_to_all | solution.py:26
  121.8 12.0 %collective-permute-start.2 = (f32[48,128]{1,0:T(8,128)S(1)}, f32[48,128]{1,0:T(8,128)S(1)}, u32[]{:S(2)}, u32[]{:S(2)}) collective-permute-start(f32[48,128]{1,0:T(8,128)S(1)} %convert_reduce_fusion), channel_id=1, source_target_pairs={{0,16},{16,0},{1,17},{17,1},{2,18},{18,2},{3,19},{19,3},{4,20},{20... | collective-permute-start | bytes 73736 | tf_op jit(solution)/shard_map/ppermute | solution.py:301
  133.8 5.1 %collective-permute-done.2 = f32[48,128]{1,0:T(8,128)S(1)} collective-permute-done((f32[48,128]{1,0:T(8,128)S(1)}, f32[48,128]{1,0:T(8,128)S(1)}, u32[]{:S(2)}, u32[]{:S(2)}) %collective-permute-start.2) | collective-permute-done | bytes 24608 | tf_op jit(solution)/shard_map/ppermute | solution.py:301
  138.9 0.0 all-to-all-done.3
  139.0 11.1 %all_to_all.26.refs_0_ = bf16[16,80,128]{2,1,0:T(8,128)(2,1)S(1)} all-to-all(bf16[16,80,128]{2,1,0:T(8,128)(2,1)S(1)} %broadcast_in_dim.8), channel_id=1, replica_groups=mesh['x'=4,'y'=4,'zh'=2,'core'=2,'emb'=8] {'x','y'}, dimensions={0} | all-to-all | bytes 655360 | tf_op jit(solution)/shard_map/all_to_all | solution.py:26
  150.1 4.6 %collective-permute-start.3 = (bf16[16,80,128]{2,1,0:T(8,128)(2,1)S(1)}, bf16[16,80,128]{2,1,0:T(8,128)(2,1)S(1)}, u32[]{:S(2)}, u32[]{:S(2)}) collective-permute-start(bf16[16,80,128]{2,1,0:T(8,128)(2,1)S(1)} %all_to_all.26.refs_0_), channel_id=1, source_target_pairs={{0,8},{8,0},{1,9},{9,1},{2,10},{10,2},{3,11},{11,3},{4,12},{12,4},... | collective-permute-start | bytes 983048 | tf_op jit(solution)/shard_map/ppermute | solution.py:301
  154.7 1.2 collective-permute-done.3.refs_1_
  156.0 0.0 copy-done
  156.0 0.0 copy-done.1
  156.0 1.5 update.1
  (11 shorter events, 0.2 us)
Async XLA Ops:
  3.4 24.7 %all-to-all-start = ((bf16[8,112,128]{2,1,0:T(8,128)(2,1)}), bf16[8,112,128]{2,1,0:T(8,128)(2,1)S(1)}, u32[]{:S(2)}, u32[]{:S(2)}) async-start(bf16[8,112,128]{2,1,0:T(8,128)(2,1)} %get-tuple-element.13), calls=%async_computation | async-start | bytes 458752 | tf_op jit(solution)/shard_map/all_to_all | solution.py:26
  18.4 58.2 %copy-start.2 = (bf16[128,512]{1,0:T(8,128)(2,1)S(1)}, bf16[128,512]{1,0:T(8,128)(2,1)}, u32[]{:S(2)}) copy-start(bf16[128,512]{1,0:T(8,128)(2,1)} %w_gate_ref.1) | copy-start | bytes 393220
  18.4 58.1 %copy-start.3 = (bf16[128,512]{1,0:T(8,128)(2,1)S(1)}, bf16[128,512]{1,0:T(8,128)(2,1)}, u32[]{:S(2)}) copy-start(bf16[128,512]{1,0:T(8,128)(2,1)} %w_up_ref.1) | copy-start | bytes 393220
  18.4 58.1 %copy-start.4 = (s32[1,256]{1,0:T(1,128)S(1)}, s32[1,256]{1,0:T(1,128)}, u32[]{:S(2)}) copy-start(s32[1,256]{1,0:T(1,128)} %get-tuple-element.14.target_ref) | copy-start | bytes 3076
  18.4 58.1 %copy-start.5 = (f32[128]{0:T(128)S(1)}, f32[128]{0:T(128)}, u32[]{:S(2)}) copy-start(f32[128]{0:T(128)} %param.18) | copy-start | bytes 1540
  48.6 27.9 %collective-permute-start = (bf16[3584,128]{1,0:T(8,128)(2,1)S(1)}, bf16[3584,128]{1,0:T(8,128)(2,1)S(1)}, u32[]{:S(2)}, u32[]{:S(2)}) collective-permute-start(bf16[3584,128]{1,0:T(8,128)(2,1)S(1)} %all_gather.3.own_ref), channel_id=1, source_target_pairs={{0,8},{8,0},{1,9},{9,1},{2,10},{10,2},{3,11},{11,3},{4,12},{12,4},... | collective-permute-start | bytes 2752520 | tf_op jit(solution)/shard_map/ppermute | solution.py:301
  60.7 15.8 %all-to-all-start.1 = ((bf16[8,64,128]{2,1,0:T(8,128)(2,1)}), bf16[8,64,128]{2,1,0:T(8,128)(2,1)S(1)}, u32[]{:S(2)}, u32[]{:S(2)}) async-start(bf16[8,64,128]{2,1,0:T(8,128)(2,1)} %bitcast.6), calls=%async_computation.1 | async-start | bytes 262144 | tf_op jit(solution)/shard_map/all_to_all | solution.py:26
  83.9 6.8 %collective-permute-start.1 = (bf16[16,304,128]{2,1,0:T(8,128)(2,1)S(1)}, bf16[16,304,128]{2,1,0:T(8,128)(2,1)S(1)}, u32[]{:S(2)}, u32[]{:S(2)}) collective-permute-start(bf16[16,304,128]{2,1,0:T(8,128)(2,1)S(1)} %slice_bitcast_fusion), channel_id=1, source_target_pairs={{0,8},{8,0},{1,9},{9,1},{2,10},{10,2},{3,11},{11,3},{4,12},{12,4},... | collective-permute-start | bytes 3735560 | tf_op jit(solution)/shard_map/ppermute | solution.py:301
  91.0 65.0 %copy-start = (f32[1536,128]{1,0:T(8,128)S(1)}, f32[1536,128]{1,0:T(8,128)}, u32[]{:S(2)}) copy-start(f32[1536,128]{1,0:T(8,128)} %refs_2_.3) | copy-start | bytes 2359300
  91.0 65.0 %copy-start.1 = (f32[1536,128]{1,0:T(8,128)S(1)}, f32[1536,128]{1,0:T(8,128)}, u32[]{:S(2)}) copy-start(f32[1536,128]{1,0:T(8,128)} %refs_3_.1) | copy-start | bytes 2359300
  114.4 24.5 %all-to-all-start.3 = ((bf16[16,32,128]{2,1,0:T(8,128)(2,1)}), bf16[16,32,128]{2,1,0:T(8,128)(2,1)S(1)}, u32[]{:S(2)}, u32[]{:S(2)}) async-start(bf16[16,32,128]{2,1,0:T(8,128)(2,1)} %bitcast.17), calls=%async_computation.3 | async-start | bytes 262144 | tf_op jit(solution)/shard_map/all_to_all | solution.py:26
  121.8 17.1 %collective-permute-start.2 = (f32[48,128]{1,0:T(8,128)S(1)}, f32[48,128]{1,0:T(8,128)S(1)}, u32[]{:S(2)}, u32[]{:S(2)}) collective-permute-start(f32[48,128]{1,0:T(8,128)S(1)} %convert_reduce_fusion), channel_id=1, source_target_pairs={{0,16},{16,0},{1,17},{17,1},{2,18},{18,2},{3,19},{19,3},{4,20},{20... | collective-permute-start | bytes 73736 | tf_op jit(solution)/shard_map/ppermute | solution.py:301
  150.1 5.8 %collective-permute-start.3 = (bf16[16,80,128]{2,1,0:T(8,128)(2,1)S(1)}, bf16[16,80,128]{2,1,0:T(8,128)(2,1)S(1)}, u32[]{:S(2)}, u32[]{:S(2)}) collective-permute-start(bf16[16,80,128]{2,1,0:T(8,128)(2,1)S(1)} %all_to_all.26.refs_0_), channel_id=1, source_target_pairs={{0,8},{8,0},{1,9},{9,1},{2,10},{10,2},{3,11},{11,3},{4,12},{12,4},... | collective-permute-start | bytes 983048 | tf_op jit(solution)/shard_map/ppermute | solution.py:301

commit v6 on v5

--- a/solution.py
+++ b/solution.py
@@ -193,7 +193,7 @@
         return total
 
     total = forward(shards - 1, jnp.zeros((tok, 128), f32), home_block)
-    total = lax.fori_loop(0, shards - 1, lambda hop, t: forward(hop, t, far_block), total)
+    total = lax.fori_loop(0, shards - 1, lambda hop, t: forward(hop, t, far_block), total, unroll=True)
     logits = jnp.sum(total, axis=1, keepdims=True)
     slopes = loss_weight * (jax.nn.sigmoid(logits) - targets)
 
@@ -222,8 +222,8 @@
         return back
 
     back = backward(shards - 1, jnp.zeros((tok, width), f32), home_block)
-    back = lax.fori_loop(0, shards - 1, lambda hop, b: backward(hop, b, far_block), back)
-    grads_ref[:, :, shards * 32 :, :] = table_part_ref[...].astype(bf16)
+    back = lax.fori_loop(0, shards - 1, lambda hop, b: backward(hop, b, far_block), back, unroll=True)
+    grads_ref[:, :, shards * 32 :, :] = table_part_ref[...]
     scaled = back * gain
     emb_grad_ref[...] = inverse_rms * scaled - values * (
         inverse_rms * inverse_rms * inverse_rms
@@ -334,7 +334,7 @@
     half_ids = half_ids // span * (2 * span) + half_ids % span
     part_ids = jnp.concatenate([half_ids + core * span, half_ids + (1 - core) * span])
     table_part = dot32((part_ids[:, None] == got_slots[None, :]).astype(bf16), got_rows)
-    table_part = table_part.reshape(2, plane, span, width)
+    table_part = table_part.astype(bf16).reshape(2, plane, span, width)
 
     foreign = lax.dynamic_slice(
         jnp.concatenate([slices, slices], axis=0), (home + 1, 0, 0), (shards - 1, 32, 128)

time: 158 us -> 157 us (level)
  no operation moved by 1% of the time
where the time goes in v6:
time: 157 us; the launch traced here: 156 us
  starting transfers between devices  57.1 us (36%)
  blocking collectives  54 us (34%)
  waiting for transfers between devices  28.3 us (18%)
  Pallas kernels  10.5 us (7%)
  matrix products  1.99 us (1%)
  other arithmetic  1.97 us (1%)
  local copies, waits for them, and re-layouts  1.71 us (1%)
    all_to_all x2, blocking collectives, exchange(): return lax.all_to_all(pieces, axis, 0, 0, tiled=True)  33.7 us
    ppermute x4, starting transfers between devices, swapped(): return lax.ppermute(array, axis, [(0, 1), (1, 0)])  31.4 us
    all_to_all x3, starting transfers between devices, exchange(): return lax.all_to_all(pieces, axis, 0, 0, tiled=True)  25.7 us
    all_gather x1, blocking collectives, step(): own_weights = lax.all_gather(foreign, XY, axis=0, tiled=True)  20.3 us
    all_to_all x3, waiting for transfers between devices, exchange(): return lax.all_to_all(pieces, axis, 0, 0, tiled=True)  19.4 us
    ppermute x4, waiting for transfers between devices, swapped(): return lax.ppermute(array, axis, [(0, 1), (1, 0)])  8.86 us
    pallas_call x1, Pallas kernels, tower(): pl.pallas_call(tower_kernel, out_shape=(jax.ShapeDtypeStruct((tok, width)...  6.22 us
  transfers between devices with their start and end apart: 7, of which 5 were waited for; matrix products, arithmetic and copies ran while one was open for 3% of the time, Pallas kernels for 0%

profile of v6, /device:TPU:1, one launch (start us, length us, event | category | flops | bytes accessed | tf_op | source)
XLA Modules:
  0.0 156.5 jit_solution(12238215729821824015)
XLA Ops:
  0.6 2.8 %pack.1 = (bf16[8,112,128]{2,1,0:T(8,128)(2,1)}, s32[1,256]{1,0:T(1,128)}) custom-call(s32[1,256]{1,0:T(1,128)} %bitcast.33, s32[1,256]{1,0:T(1,128)} %bitcast.34, bf16[256,128]{1,0:T(8,128)(2,1)} %refs_2_.2, s32[96,128]{1,0:T(8,128)} %bitcast.31, bf16[128,512]{1,0:T(8,128)(2,1)} %w_gate_ref.1, bf16[128,512]{1,0:T(8,128)(2,1)} %w_up_ref.1, ...), custom_call_target="tpu_custom_call" | custom-call | tf_op jit(solution)/shard_map/pack/pallas_call | solution.py:118
  3.4 13.1 %all-to-all-start = ((bf16[8,112,128]{2,1,0:T(8,128)(2,1)}), bf16[8,112,128]{2,1,0:T(8,128)(2,1)S(1)}, u32[]{:S(2)}, u32[]{:S(2)}) async-start(bf16[8,112,128]{2,1,0:T(8,128)(2,1)} %get-tuple-element.13), calls=%async_computation | async-start | bytes 458752 | tf_op jit(solution)/shard_map/all_to_all | solution.py:26
  16.5 0.7 reshape.66.labels_ref
  17.2 1.2 convert_element_type.47
  18.4 0.0 copy-start.2
  18.4 0.0 copy-start.3
  18.4 0.0 copy-start.4
  18.4 0.0 copy-start.5
  18.5 9.7 %all-to-all-done.shared_ref = bf16[8,112,128]{2,1,0:T(8,128)(2,1)S(1)} async-done(((bf16[8,112,128]{2,1,0:T(8,128)(2,1)}), bf16[8,112,128]{2,1,0:T(8,128)(2,1)S(1)}, u32[]{:S(2)}, u32[]{:S(2)}) %all-to-all-start) | async-done | bytes 229408 | tf_op jit(solution)/shard_map/all_to_all | solution.py:26
  28.2 0.1 fusion.11
  28.3 20.3 %all_gather.3.own_ref = bf16[3584,128]{1,0:T(8,128)(2,1)S(1)} all-gather(bf16[224,128]{1,0:T(8,128)(2,1)S(1)} %bitcast.29), channel_id=1, replica_groups=mesh['x'=4,'y'=4,'zh'=2,'core'=2,'emb'=8] {'x','y'}, dimensions={0}, use_global_device_ids=true | all-gather | bytes 974848 | tf_op jit(solution)/shard_map/all_gather | solution.py:342
  48.6 10.7 %collective-permute-start = (bf16[3584,128]{1,0:T(8,128)(2,1)S(1)}, bf16[3584,128]{1,0:T(8,128)(2,1)S(1)}, u32[]{:S(2)}, u32[]{:S(2)}) collective-permute-start(bf16[3584,128]{1,0:T(8,128)(2,1)S(1)} %all_gather.3.own_ref), channel_id=1, source_target_pairs={{0,8},{8,0},{1,9},{9,1},{2,10},{10,2},{3,11},{11,3},{4,12},{12,4},... | collective-permute-start | bytes 2752520 | tf_op jit(solution)/shard_map/ppermute | solution.py:301
  59.3 0.1 slice_add_fusion.1
  59.3 0.1 eq.32
  59.4 1.3 fusion.10
  60.7 5.2 %all-to-all-start.1 = ((bf16[8,64,128]{2,1,0:T(8,128)(2,1)}), bf16[8,64,128]{2,1,0:T(8,128)(2,1)S(1)}, u32[]{:S(2)}, u32[]{:S(2)}) async-start(bf16[8,64,128]{2,1,0:T(8,128)(2,1)} %bitcast.6), calls=%async_computation.1 | async-start | bytes 262144 | tf_op jit(solution)/shard_map/all_to_all | solution.py:26
  66.0 0.1 slice_add_fusion
  66.0 0.1 eq.37
  66.1 0.7 fusion.4
  66.8 9.7 %all-to-all-done.1 = bf16[8,64,128]{2,1,0:T(8,128)(2,1)S(1)} async-done(((bf16[8,64,128]{2,1,0:T(8,128)(2,1)}), bf16[8,64,128]{2,1,0:T(8,128)(2,1)S(1)}, u32[]{:S(2)}, u32[]{:S(2)}) %all-to-all-start.1) | async-done | bytes 131104 | tf_op jit(solution)/shard_map/all_to_all | solution.py:26
  76.5 0.0 collective-permute-done.other_ref
  76.5 0.0 copy-done.2
  76.5 0.0 copy-done.3
  76.5 0.0 copy-done.4
  76.6 0.0 copy-done.5
  76.6 6.2 %tower.1 = (f32[256,128]{1,0:T(8,128)}, bf16[2,16,304,128]{3,2,1,0:T(8,128)(2,1)S(1)}) custom-call(bf16[512,128]{1,0:T(8,128)(2,1)S(1)} %bitcast.25, s32[1,256]{1,0:T(1,128)S(1)} %copy-done.4, bf16[3584,128]{1,0:T(8,128)(2,1)S(1)} %all_gather.3.own_ref, bf16[3584,128]{1,0:T(8,128)(2,1)S(1)} %collective-permute-done.other_ref, ...), custom_call_target="tpu_custom_call" | custom-call | flops 1610612736 | bytes 5242880 | tf_op jit(solution)/shard_map/tower/pallas_call | solution.py:238
  82.8 0.1 slice_bitcast_fusion
  82.9 4.2 %collective-permute-start.1 = (bf16[16,304,128]{2,1,0:T(8,128)(2,1)S(1)}, bf16[16,304,128]{2,1,0:T(8,128)(2,1)S(1)}, u32[]{:S(2)}, u32[]{:S(2)}) collective-permute-start(bf16[16,304,128]{2,1,0:T(8,128)(2,1)S(1)} %slice_bitcast_fusion), channel_id=1, source_target_pairs={{0,8},{8,0},{1,9},{9,1},{2,10},{10,2},{3,11},{11,3},{4,12},{12,4},... | collective-permute-start | bytes 3735560 | tf_op jit(solution)/shard_map/ppermute | solution.py:301
  87.1 2.5 %collective-permute-done.1 = bf16[16,304,128]{2,1,0:T(8,128)(2,1)S(1)} collective-permute-done((bf16[16,304,128]{2,1,0:T(8,128)(2,1)S(1)}, bf16[16,304,128]{2,1,0:T(8,128)(2,1)S(1)}, u32[]{:S(2)}, u32[]{:S(2)}) %collective-permute-start.1) | collective-permute-done | bytes 1245216 | tf_op jit(solution)/shard_map/ppermute | solution.py:301
  89.6 0.3 fusion.3
  90.0 0.0 copy-start
  90.0 0.0 copy-start.1
  90.0 22.6 %all_to_all.25 = bf16[16,304,128]{2,1,0:T(8,128)(2,1)S(1)} all-to-all(bf16[16,304,128]{2,1,0:T(8,128)(2,1)S(1)} %fusion.3), channel_id=1, replica_groups=mesh['x'=4,'y'=4,'zh'=2,'core'=2,'emb'=8] {'x','y'}, dimensions={0} | all-to-all | bytes 2490368 | tf_op jit(solution)/shard_map/all_to_all | solution.py:26
  112.5 0.1 slice_reduce_fusion
  112.7 0.7 broadcast_in_dim.7
  113.3 7.4 %all-to-all-start.3 = ((bf16[16,32,128]{2,1,0:T(8,128)(2,1)}), bf16[16,32,128]{2,1,0:T(8,128)(2,1)S(1)}, u32[]{:S(2)}, u32[]{:S(2)}) async-start(bf16[16,32,128]{2,1,0:T(8,128)(2,1)} %bitcast.16), calls=%async_computation.3 | async-start | bytes 262144 | tf_op jit(solution)/shard_map/all_to_all | solution.py:26
  120.8 12.0 %collective-permute-start.2 = (f32[48,128]{1,0:T(8,128)S(1)}, f32[48,128]{1,0:T(8,128)S(1)}, u32[]{:S(2)}, u32[]{:S(2)}) collective-permute-start(f32[48,128]{1,0:T(8,128)S(1)} %convert_reduce_fusion), channel_id=1, source_target_pairs={{0,16},{16,0},{1,17},{17,1},{2,18},{18,2},{3,19},{19,3},{4,20},{20... | collective-permute-start | bytes 73736 | tf_op jit(solution)/shard_map/ppermute | solution.py:301
  132.8 5.1 %collective-permute-done.2 = f32[48,128]{1,0:T(8,128)S(1)} collective-permute-done((f32[48,128]{1,0:T(8,128)S(1)}, f32[48,128]{1,0:T(8,128)S(1)}, u32[]{:S(2)}, u32[]{:S(2)}) %collective-permute-start.2) | collective-permute-done | bytes 24608 | tf_op jit(solution)/shard_map/ppermute | solution.py:301
  137.9 0.0 all-to-all-done.3
  138.0 11.1 %all_to_all.26.refs_0_ = bf16[16,80,128]{2,1,0:T(8,128)(2,1)S(1)} all-to-all(bf16[16,80,128]{2,1,0:T(8,128)(2,1)S(1)} %broadcast_in_dim.8), channel_id=1, replica_groups=mesh['x'=4,'y'=4,'zh'=2,'core'=2,'emb'=8] {'x','y'}, dimensions={0} | all-to-all | bytes 655360 | tf_op jit(solution)/shard_map/all_to_all | solution.py:26
  149.1 4.6 %collective-permute-start.3 = (bf16[16,80,128]{2,1,0:T(8,128)(2,1)S(1)}, bf16[16,80,128]{2,1,0:T(8,128)(2,1)S(1)}, u32[]{:S(2)}, u32[]{:S(2)}) collective-permute-start(bf16[16,80,128]{2,1,0:T(8,128)(2,1)S(1)} %all_to_all.26.refs_0_), channel_id=1, source_target_pairs={{0,8},{8,0},{1,9},{9,1},{2,10},{10,2},{3,11},{11,3},{4,12},{12,4},... | collective-permute-start | bytes 983048 | tf_op jit(solution)/shard_map/ppermute | solution.py:301
  153.7 1.2 collective-permute-done.3.refs_1_
  154.9 0.0 copy-done
  155.0 0.0 copy-done.1
  155.0 1.5 update.1
  (11 shorter events, 0.2 us)
Async XLA Ops:
  3.4 24.7 %all-to-all-start = ((bf16[8,112,128]{2,1,0:T(8,128)(2,1)}), bf16[8,112,128]{2,1,0:T(8,128)(2,1)S(1)}, u32[]{:S(2)}, u32[]{:S(2)}) async-start(bf16[8,112,128]{2,1,0:T(8,128)(2,1)} %get-tuple-element.13), calls=%async_computation | async-start | bytes 458752 | tf_op jit(solution)/shard_map/all_to_all | solution.py:26
  18.4 58.1 %copy-start.2 = (bf16[128,512]{1,0:T(8,128)(2,1)S(1)}, bf16[128,512]{1,0:T(8,128)(2,1)}, u32[]{:S(2)}) copy-start(bf16[128,512]{1,0:T(8,128)(2,1)} %w_gate_ref.1) | copy-start | bytes 393220
  18.4 58.1 %copy-start.3 = (bf16[128,512]{1,0:T(8,128)(2,1)S(1)}, bf16[128,512]{1,0:T(8,128)(2,1)}, u32[]{:S(2)}) copy-start(bf16[128,512]{1,0:T(8,128)(2,1)} %w_up_ref.1) | copy-start | bytes 393220
  18.4 58.1 %copy-start.4 = (s32[1,256]{1,0:T(1,128)S(1)}, s32[1,256]{1,0:T(1,128)}, u32[]{:S(2)}) copy-start(s32[1,256]{1,0:T(1,128)} %get-tuple-element.14.target_ref) | copy-start | bytes 3076
  18.4 58.1 %copy-start.5 = (f32[128]{0:T(128)S(1)}, f32[128]{0:T(128)}, u32[]{:S(2)}) copy-start(f32[128]{0:T(128)} %param.18) | copy-start | bytes 1540
  48.6 27.9 %collective-permute-start = (bf16[3584,128]{1,0:T(8,128)(2,1)S(1)}, bf16[3584,128]{1,0:T(8,128)(2,1)S(1)}, u32[]{:S(2)}, u32[]{:S(2)}) collective-permute-start(bf16[3584,128]{1,0:T(8,128)(2,1)S(1)} %all_gather.3.own_ref), channel_id=1, source_target_pairs={{0,8},{8,0},{1,9},{9,1},{2,10},{10,2},{3,11},{11,3},{4,12},{12,4},... | collective-permute-start | bytes 2752520 | tf_op jit(solution)/shard_map/ppermute | solution.py:301
  60.7 15.8 %all-to-all-start.1 = ((bf16[8,64,128]{2,1,0:T(8,128)(2,1)}), bf16[8,64,128]{2,1,0:T(8,128)(2,1)S(1)}, u32[]{:S(2)}, u32[]{:S(2)}) async-start(bf16[8,64,128]{2,1,0:T(8,128)(2,1)} %bitcast.6), calls=%async_computation.1 | async-start | bytes 262144 | tf_op jit(solution)/shard_map/all_to_all | solution.py:26
  82.9 6.8 %collective-permute-start.1 = (bf16[16,304,128]{2,1,0:T(8,128)(2,1)S(1)}, bf16[16,304,128]{2,1,0:T(8,128)(2,1)S(1)}, u32[]{:S(2)}, u32[]{:S(2)}) collective-permute-start(bf16[16,304,128]{2,1,0:T(8,128)(2,1)S(1)} %slice_bitcast_fusion), channel_id=1, source_target_pairs={{0,8},{8,0},{1,9},{9,1},{2,10},{10,2},{3,11},{11,3},{4,12},{12,4},... | collective-permute-start | bytes 3735560 | tf_op jit(solution)/shard_map/ppermute | solution.py:301
  90.0 65.0 %copy-start = (f32[1536,128]{1,0:T(8,128)S(1)}, f32[1536,128]{1,0:T(8,128)}, u32[]{:S(2)}) copy-start(f32[1536,128]{1,0:T(8,128)} %refs_2_.3) | copy-start | bytes 2359300
  90.0 65.0 %copy-start.1 = (f32[1536,128]{1,0:T(8,128)S(1)}, f32[1536,128]{1,0:T(8,128)}, u32[]{:S(2)}) copy-start(f32[1536,128]{1,0:T(8,128)} %refs_3_.1) | copy-start | bytes 2359300
  113.3 24.5 %all-to-all-start.3 = ((bf16[16,32,128]{2,1,0:T(8,128)(2,1)}), bf16[16,32,128]{2,1,0:T(8,128)(2,1)S(1)}, u32[]{:S(2)}, u32[]{:S(2)}) async-start(bf16[16,32,128]{2,1,0:T(8,128)(2,1)} %bitcast.16), calls=%async_computation.3 | async-start | bytes 262144 | tf_op jit(solution)/shard_map/all_to_all | solution.py:26
  120.8 17.1 %collective-permute-start.2 = (f32[48,128]{1,0:T(8,128)S(1)}, f32[48,128]{1,0:T(8,128)S(1)}, u32[]{:S(2)}, u32[]{:S(2)}) collective-permute-start(f32[48,128]{1,0:T(8,128)S(1)} %convert_reduce_fusion), channel_id=1, source_target_pairs={{0,16},{16,0},{1,17},{17,1},{2,18},{18,2},{3,19},{19,3},{4,20},{20... | collective-permute-start | bytes 73736 | tf_op jit(solution)/shard_map/ppermute | solution.py:301
  149.1 5.8 %collective-permute-start.3 = (bf16[16,80,128]{2,1,0:T(8,128)(2,1)S(1)}, bf16[16,80,128]{2,1,0:T(8,128)(2,1)S(1)}, u32[]{:S(2)}, u32[]{:S(2)}) collective-permute-start(bf16[16,80,128]{2,1,0:T(8,128)(2,1)S(1)} %all_to_all.26.refs_0_), channel_id=1, source_target_pairs={{0,8},{8,0},{1,9},{9,1},{2,10},{10,2},{3,11},{11,3},{4,12},{12,4},... | collective-permute-start | bytes 983048 | tf_op jit(solution)/shard_map/ppermute | solution.py:301

commit v7 on v6

--- a/solution.py
+++ b/solution.py
@@ -13,6 +13,7 @@
 DP_EMB = ("x", "y", "zh", "core", "emb")
 XY = ("x", "y")
 ZZ = ("zh", "emb")
+
 
 loss_weight = 64.0
 learn_rate = 0.1
@@ -153,19 +154,22 @@
         pick, answers_ref[...], (((0,), (0,)), ((), ())), preferred_element_type=f32
     )
     turned = labels_ref[...].T
-    column = lax.broadcasted_iota(jnp.int32, turned.shape, 1) == home
-    targets = jnp.sum(jnp.where(column, turned, 0.0), axis=1, keepdims=True)
+    mine = lax.broadcasted_iota(jnp.int32, turned.shape, 1) == home
+    targets = jnp.sum(jnp.where(mine, turned, 0.0), axis=1, keepdims=True)
     inverse_rms = lax.rsqrt(jnp.mean(values * values, axis=1, keepdims=True) + norm_eps)
     gain = gain_ref[...]
     normed_wide = values * inverse_rms * gain
     normed = normed_wide.astype(bf16)
     normed_t = normed_wide.T.astype(bf16)
 
+    column = lax.axis_index("x")
+
     def far_block(hop, half, side):
         tiles = []
         for tile in (2 * half, 2 * half + 1):
+            turn = (tile - column + 4) % 4
             quarters = [
-                weights_s[side, pl.ds((tile * 4 + k) * lines + hop * 32, 32), :]
+                weights_s[side, pl.ds(pl.multiple_of((k * 4 + turn) * lines + hop * 32, 32), 32), :]
                 for k in range(4)
             ]
             tiles.append(jnp.concatenate(quarters, axis=0))
@@ -339,7 +343,11 @@
     foreign = lax.dynamic_slice(
         jnp.concatenate([slices, slices], axis=0), (home + 1, 0, 0), (shards - 1, 32, 128)
     ).reshape((shards - 1) * 32, 128)
-    own_weights = lax.all_gather(foreign, XY, axis=0, tiled=True)
+    ring = lax.axis_size("x")
+    turns = [foreign]
+    for step in range(1, ring):
+        turns.append(lax.ppermute(foreign, "x", [(i, (i - step) % ring) for i in range(ring)]))
+    own_weights = lax.all_gather(jnp.concatenate(turns, axis=0), "y", axis=0, tiled=True)
     other_weights = swapped(own_weights, "core")
     emb_grad, tower_grads = tower(
         answers, cur_pos, own_weights, other_weights, w_gate, w_up, first, gain, labels,

time: 157 us -> 162 us (1.032)
  starting transfers between devices: 57.1 us -> 68.5 us
  blocking collectives: 54 us -> 45.6 us
  waiting for transfers between devices: 28.3 us -> 30.2 us
    ppermute x0 -> x3, starting transfers between devices: none -> 10.6 us  [step(): lax.ppermute(foreign, 'x', [(i, (i - step) % ring) for i in range(ring)])]
    all_gather x1, blocking collectives: 20.3 us -> 11.7 us  [step(): lax.all_gather(jnp.concatenate(turns, axis=0), 'y', axis=0, tiled=True)]
    ppermute x0 -> x3, waiting for transfers between devices: none -> 1.79 us  [step(): lax.ppermute(foreign, 'x', [(i, (i - step) % ring) for i in range(ring)])]
  transfers between devices with their start and end apart: 7 -> 10, of which waited for: 5 -> 6; matrix products, arithmetic and copies ran while one was open for 3% -> 3% of each run, Pallas kernels for 0% -> 0%
where the time goes in v7:
time: 162 us; the launch traced here: 161 us
  starting transfers between devices  68.5 us (42%)
  blocking collectives  45.6 us (28%)
  waiting for transfers between devices  30.2 us (19%)
  Pallas kernels  10.4 us (6%)
  matrix products  1.99 us (1%)
  other arithmetic  1.97 us (1%)
  local copies, waits for them, and re-layouts  1.71 us (1%)
    all_to_all x2, blocking collectives, exchange(): return lax.all_to_all(pieces, axis, 0, 0, tiled=True)  33.8 us
    ppermute x4, starting transfers between devices, swapped(): return lax.ppermute(array, axis, [(0, 1), (1, 0)])  31.1 us
    all_to_all x3, starting transfers between devices, exchange(): return lax.all_to_all(pieces, axis, 0, 0, tiled=True)  26.8 us
    all_to_all x3, waiting for transfers between devices, exchange(): return lax.all_to_all(pieces, axis, 0, 0, tiled=True)  19.5 us
    all_gather x1, blocking collectives, step(): lax.all_gather(jnp.concatenate(turns, axis=0), 'y', axis=0, tiled=True)  11.7 us
    ppermute x3, starting transfers between devices, step(): lax.ppermute(foreign, 'x', [(i, (i - step) % ring) for i in range(ring)])  10.6 us
    ppermute x4, waiting for transfers between devices, swapped(): return lax.ppermute(array, axis, [(0, 1), (1, 0)])  8.86 us
    pallas_call x1, Pallas kernels, tower(): pl.pallas_call(tower_kernel, out_shape=(jax.ShapeDtypeStruct((tok, width)...  6.1 us
  transfers between devices with their start and end apart: 10, of which 6 were waited for; matrix products, arithmetic and copies ran while one was open for 3% of the time, Pallas kernels for 0%

profile of v7, /device:TPU:1, one launch (start us, length us, event | category | flops | bytes accessed | tf_op | source)
XLA Modules:
  0.0 161.2 jit_solution(16690493188900496958)
XLA Ops:
  0.6 2.8 %pack.1 = (bf16[8,112,128]{2,1,0:T(8,128)(2,1)}, s32[1,256]{1,0:T(1,128)}) custom-call(s32[1,256]{1,0:T(1,128)} %bitcast.36, s32[1,256]{1,0:T(1,128)} %bitcast.37, bf16[256,128]{1,0:T(8,128)(2,1)} %refs_2_.2, s32[96,128]{1,0:T(8,128)} %bitcast.34, bf16[128,512]{1,0:T(8,128)(2,1)} %w_gate_ref.1, bf16[128,512]{1,0:T(8,128)(2,1)} %w_up_ref.1, ...), custom_call_target="tpu_custom_call" | custom-call | tf_op jit(solution)/shard_map/pack/pallas_call | solution.py:119
  3.4 13.1 %all-to-all-start = ((bf16[8,112,128]{2,1,0:T(8,128)(2,1)}), bf16[8,112,128]{2,1,0:T(8,128)(2,1)S(1)}, u32[]{:S(2)}, u32[]{:S(2)}) async-start(bf16[8,112,128]{2,1,0:T(8,128)(2,1)} %get-tuple-element.13), calls=%async_computation | async-start | bytes 458752 | tf_op jit(solution)/shard_map/all_to_all | solution.py:27
  16.5 0.7 reshape.66.labels_ref
  17.2 1.2 convert_element_type.47
  18.4 9.7 %all-to-all-done.shared_ref = bf16[8,112,128]{2,1,0:T(8,128)(2,1)S(1)} async-done(((bf16[8,112,128]{2,1,0:T(8,128)(2,1)}), bf16[8,112,128]{2,1,0:T(8,128)(2,1)S(1)}, u32[]{:S(2)}, u32[]{:S(2)}) %all-to-all-start) | async-done | bytes 229408 | tf_op jit(solution)/shard_map/all_to_all | solution.py:27
  28.2 0.1 fusion.11
  28.2 3.1 %collective-permute-start.2 = (bf16[224,128]{1,0:T(8,128)(2,1)S(1)}, bf16[224,128]{1,0:T(8,128)(2,1)S(1)}, u32[]{:S(2)}, u32[]{:S(2)}) collective-permute-start(bf16[224,128]{1,0:T(8,128)(2,1)S(1)} %bitcast.29), channel_id=1, source_target_pairs={{0,128},{128,256},{256,384},{384,0},{1,129},{129,257},{257,385},{3... | collective-permute-start | bytes 172040 | tf_op jit(solution)/shard_map/ppermute | solution.py:349
  31.4 4.3 %collective-permute-start.1 = (bf16[224,128]{1,0:T(8,128)(2,1)S(1)}, bf16[224,128]{1,0:T(8,128)(2,1)S(1)}, u32[]{:S(2)}, u32[]{:S(2)}) collective-permute-start(bf16[224,128]{1,0:T(8,128)(2,1)S(1)} %bitcast.30), channel_id=1, source_target_pairs={{0,256},{128,384},{256,0},{384,128},{1,257},{129,385},{257,1},{385... | collective-permute-start | bytes 172040 | tf_op jit(solution)/shard_map/ppermute | solution.py:349
  35.7 3.1 %collective-permute-start = (bf16[224,128]{1,0:T(8,128)(2,1)S(1)}, bf16[224,128]{1,0:T(8,128)(2,1)S(1)}, u32[]{:S(2)}, u32[]{:S(2)}) collective-permute-start(bf16[224,128]{1,0:T(8,128)(2,1)S(1)} %bitcast.31), channel_id=1, source_target_pairs={{0,384},{128,0},{256,128},{384,256},{1,385},{129,1},{257,129},{385... | collective-permute-start | bytes 172040 | tf_op jit(solution)/shard_map/ppermute | solution.py:349
  38.8 0.0 collective-permute-done.2
  38.9 0.0 collective-permute-done.1
  38.9 1.8 %collective-permute-done = bf16[224,128]{1,0:T(8,128)(2,1)S(1)} collective-permute-done((bf16[224,128]{1,0:T(8,128)(2,1)S(1)}, bf16[224,128]{1,0:T(8,128)(2,1)S(1)}, u32[]{:S(2)}, u32[]{:S(2)}) %collective-permute-start) | collective-permute-done | bytes 57376 | tf_op jit(solution)/shard_map/ppermute | solution.py:349
  40.7 0.0 copy-start.2
  40.7 0.0 copy-start.3
  40.7 0.0 copy-start.4
  40.7 0.0 copy-start.5
  40.7 11.7 %all_gather.3.own_ref = bf16[3584,128]{1,0:T(8,128)(2,1)S(1)} all-gather(bf16[896,128]{1,0:T(8,128)(2,1)S(1)} %pad_maximum_fusion), channel_id=1, replica_groups=mesh['x'=4,'y'=4,'zh'=2,'core'=2,'emb'=8] {'y'}, dimensions={0}, use_global_device_ids=true | all-gather | bytes 1146880 | tf_op jit(solution)/shard_map/all_gather | solution.py:350
  52.5 10.3 %collective-permute-start.3 = (bf16[3584,128]{1,0:T(8,128)(2,1)S(1)}, bf16[3584,128]{1,0:T(8,128)(2,1)S(1)}, u32[]{:S(2)}, u32[]{:S(2)}) collective-permute-start(bf16[3584,128]{1,0:T(8,128)(2,1)S(1)} %all_gather.3.own_ref), channel_id=1, source_target_pairs={{0,8},{8,0},{1,9},{9,1},{2,10},{10,2},{3,11},{11,3},{4,12},{12,4},... | collective-permute-start | bytes 2752520 | tf_op jit(solution)/shard_map/ppermute | solution.py:305
  62.8 0.1 slice_add_fusion.1
  62.9 0.1 eq.32
  63.0 1.3 fusion.10
  64.3 6.3 %all-to-all-start.1 = ((bf16[8,64,128]{2,1,0:T(8,128)(2,1)}), bf16[8,64,128]{2,1,0:T(8,128)(2,1)S(1)}, u32[]{:S(2)}, u32[]{:S(2)}) async-start(bf16[8,64,128]{2,1,0:T(8,128)(2,1)} %bitcast.6), calls=%async_computation.1 | async-start | bytes 262144 | tf_op jit(solution)/shard_map/all_to_all | solution.py:27
  70.6 0.1 slice_add_fusion
  70.7 0.1 eq.37
  70.8 0.7 fusion.4
  71.5 9.7 %all-to-all-done.1 = bf16[8,64,128]{2,1,0:T(8,128)(2,1)S(1)} async-done(((bf16[8,64,128]{2,1,0:T(8,128)(2,1)}), bf16[8,64,128]{2,1,0:T(8,128)(2,1)S(1)}, u32[]{:S(2)}, u32[]{:S(2)}) %all-to-all-start.1) | async-done | bytes 131104 | tf_op jit(solution)/shard_map/all_to_all | solution.py:27
  81.2 0.0 collective-permute-done.3.other_ref
  81.2 0.0 copy-done.2
  81.2 0.0 copy-done.3
  81.2 0.0 copy-done.4
  81.2 6.1 %tower.1 = (f32[256,128]{1,0:T(8,128)}, bf16[2,16,304,128]{3,2,1,0:T(8,128)(2,1)S(1)}) custom-call(bf16[512,128]{1,0:T(8,128)(2,1)S(1)} %bitcast.25, s32[1,256]{1,0:T(1,128)S(1)} %copy-done.4, bf16[3584,128]{1,0:T(8,128)(2,1)S(1)} %all_gather.3.own_ref, bf16[3584,128]{1,0:T(8,128)(2,1)S(1)} %collective-permute-done.3.other_ref, ...), custom_call_target="tpu_custom_call" | custom-call | flops 1610612736 | bytes 5242880 | tf_op jit(solution)/shard_map/tower/pallas_call | solution.py:242
  87.3 0.1 slice_bitcast_fusion
  87.4 4.2 %collective-permute-start.4 = (bf16[16,304,128]{2,1,0:T(8,128)(2,1)S(1)}, bf16[16,304,128]{2,1,0:T(8,128)(2,1)S(1)}, u32[]{:S(2)}, u32[]{:S(2)}) collective-permute-start(bf16[16,304,128]{2,1,0:T(8,128)(2,1)S(1)} %slice_bitcast_fusion), channel_id=1, source_target_pairs={{0,8},{8,0},{1,9},{9,1},{2,10},{10,2},{3,11},{11,3},{4,12},{12,4},... | collective-permute-start | bytes 3735560 | tf_op jit(solution)/shard_map/ppermute | solution.py:305
  91.6 2.5 %collective-permute-done.4 = bf16[16,304,128]{2,1,0:T(8,128)(2,1)S(1)} collective-permute-done((bf16[16,304,128]{2,1,0:T(8,128)(2,1)S(1)}, bf16[16,304,128]{2,1,0:T(8,128)(2,1)S(1)}, u32[]{:S(2)}, u32[]{:S(2)}) %collective-permute-start.4) | collective-permute-done | bytes 1245216 | tf_op jit(solution)/shard_map/ppermute | solution.py:305
  94.2 0.3 fusion.3
  94.5 0.0 copy-start
  94.5 0.0 copy-start.1
  94.5 22.7 %all_to_all.25 = bf16[16,304,128]{2,1,0:T(8,128)(2,1)S(1)} all-to-all(bf16[16,304,128]{2,1,0:T(8,128)(2,1)S(1)} %fusion.3), channel_id=1, replica_groups=mesh['x'=4,'y'=4,'zh'=2,'core'=2,'emb'=8] {'x','y'}, dimensions={0} | all-to-all | bytes 2490368 | tf_op jit(solution)/shard_map/all_to_all | solution.py:27
  117.2 0.1 slice_reduce_fusion
  117.4 0.7 broadcast_in_dim.7
  118.1 7.4 %all-to-all-start.3 = ((bf16[16,32,128]{2,1,0:T(8,128)(2,1)}), bf16[16,32,128]{2,1,0:T(8,128)(2,1)S(1)}, u32[]{:S(2)}, u32[]{:S(2)}) async-start(bf16[16,32,128]{2,1,0:T(8,128)(2,1)} %bitcast.16), calls=%async_computation.3 | async-start | bytes 262144 | tf_op jit(solution)/shard_map/all_to_all | solution.py:27
  125.5 12.0 %collective-permute-start.5 = (f32[48,128]{1,0:T(8,128)S(1)}, f32[48,128]{1,0:T(8,128)S(1)}, u32[]{:S(2)}, u32[]{:S(2)}) collective-permute-start(f32[48,128]{1,0:T(8,128)S(1)} %convert_reduce_fusion), channel_id=1, source_target_pairs={{0,16},{16,0},{1,17},{17,1},{2,18},{18,2},{3,19},{19,3},{4,20},{20... | collective-permute-start | bytes 73736 | tf_op jit(solution)/shard_map/ppermute | solution.py:305
  137.5 5.1 %collective-permute-done.5 = f32[48,128]{1,0:T(8,128)S(1)} collective-permute-done((f32[48,128]{1,0:T(8,128)S(1)}, f32[48,128]{1,0:T(8,128)S(1)}, u32[]{:S(2)}, u32[]{:S(2)}) %collective-permute-start.5) | collective-permute-done | bytes 24608 | tf_op jit(solution)/shard_map/ppermute | solution.py:305
  142.6 0.0 all-to-all-done.3
  142.7 11.1 %all_to_all.26.refs_0_ = bf16[16,80,128]{2,1,0:T(8,128)(2,1)S(1)} all-to-all(bf16[16,80,128]{2,1,0:T(8,128)(2,1)S(1)} %broadcast_in_dim.8), channel_id=1, replica_groups=mesh['x'=4,'y'=4,'zh'=2,'core'=2,'emb'=8] {'x','y'}, dimensions={0} | all-to-all | bytes 655360 | tf_op jit(solution)/shard_map/all_to_all | solution.py:27
  153.8 4.6 %collective-permute-start.6 = (bf16[16,80,128]{2,1,0:T(8,128)(2,1)S(1)}, bf16[16,80,128]{2,1,0:T(8,128)(2,1)S(1)}, u32[]{:S(2)}, u32[]{:S(2)}) collective-permute-start(bf16[16,80,128]{2,1,0:T(8,128)(2,1)S(1)} %all_to_all.26.refs_0_), channel_id=1, source_target_pairs={{0,8},{8,0},{1,9},{9,1},{2,10},{10,2},{3,11},{11,3},{4,12},{12,4},... | collective-permute-start | bytes 983048 | tf_op jit(solution)/shard_map/ppermute | solution.py:305
  158.4 1.2 collective-permute-done.6.refs_1_
  159.7 1.5 update.1
  (15 shorter events, 0.2 us)
Async XLA Ops:
  3.4 24.7 %all-to-all-start = ((bf16[8,112,128]{2,1,0:T(8,128)(2,1)}), bf16[8,112,128]{2,1,0:T(8,128)(2,1)S(1)}, u32[]{:S(2)}, u32[]{:S(2)}) async-start(bf16[8,112,128]{2,1,0:T(8,128)(2,1)} %get-tuple-element.13), calls=%async_computation | async-start | bytes 458752 | tf_op jit(solution)/shard_map/all_to_all | solution.py:27
  28.2 10.6 %collective-permute-start.2 = (bf16[224,128]{1,0:T(8,128)(2,1)S(1)}, bf16[224,128]{1,0:T(8,128)(2,1)S(1)}, u32[]{:S(2)}, u32[]{:S(2)}) collective-permute-start(bf16[224,128]{1,0:T(8,128)(2,1)S(1)} %bitcast.29), channel_id=1, source_target_pairs={{0,128},{128,256},{256,384},{384,0},{1,129},{129,257},{257,385},{3... | collective-permute-start | bytes 172040 | tf_op jit(solution)/shard_map/ppermute | solution.py:349
  31.4 7.5 %collective-permute-start.1 = (bf16[224,128]{1,0:T(8,128)(2,1)S(1)}, bf16[224,128]{1,0:T(8,128)(2,1)S(1)}, u32[]{:S(2)}, u32[]{:S(2)}) collective-permute-start(bf16[224,128]{1,0:T(8,128)(2,1)S(1)} %bitcast.30), channel_id=1, source_target_pairs={{0,256},{128,384},{256,0},{384,128},{1,257},{129,385},{257,1},{385... | collective-permute-start | bytes 172040 | tf_op jit(solution)/shard_map/ppermute | solution.py:349
  35.7 4.9 %collective-permute-start = (bf16[224,128]{1,0:T(8,128)(2,1)S(1)}, bf16[224,128]{1,0:T(8,128)(2,1)S(1)}, u32[]{:S(2)}, u32[]{:S(2)}) collective-permute-start(bf16[224,128]{1,0:T(8,128)(2,1)S(1)} %bitcast.31), channel_id=1, source_target_pairs={{0,384},{128,0},{256,128},{384,256},{1,385},{129,1},{257,129},{385... | collective-permute-start | bytes 172040 | tf_op jit(solution)/shard_map/ppermute | solution.py:349
  40.7 40.5 %copy-start.2 = (bf16[128,512]{1,0:T(8,128)(2,1)S(1)}, bf16[128,512]{1,0:T(8,128)(2,1)}, u32[]{:S(2)}) copy-start(bf16[128,512]{1,0:T(8,128)(2,1)} %w_gate_ref.1) | copy-start | bytes 393220
  40.7 40.5 %copy-start.3 = (bf16[128,512]{1,0:T(8,128)(2,1)S(1)}, bf16[128,512]{1,0:T(8,128)(2,1)}, u32[]{:S(2)}) copy-start(bf16[128,512]{1,0:T(8,128)(2,1)} %w_up_ref.1) | copy-start | bytes 393220
  40.7 40.5 %copy-start.4 = (s32[1,256]{1,0:T(1,128)S(1)}, s32[1,256]{1,0:T(1,128)}, u32[]{:S(2)}) copy-start(s32[1,256]{1,0:T(1,128)} %get-tuple-element.14.target_ref) | copy-start | bytes 3076
  40.7 40.5 %copy-start.5 = (f32[128]{0:T(128)S(1)}, f32[128]{0:T(128)}, u32[]{:S(2)}) copy-start(f32[128]{0:T(128)} %param.18) | copy-start | bytes 1540
  52.5 28.7 %collective-permute-start.3 = (bf16[3584,128]{1,0:T(8,128)(2,1)S(1)}, bf16[3584,128]{1,0:T(8,128)(2,1)S(1)}, u32[]{:S(2)}, u32[]{:S(2)}) collective-permute-start(bf16[3584,128]{1,0:T(8,128)(2,1)S(1)} %all_gather.3.own_ref), channel_id=1, source_target_pairs={{0,8},{8,0},{1,9},{9,1},{2,10},{10,2},{3,11},{11,3},{4,12},{12,4},... | collective-permute-start | bytes 2752520 | tf_op jit(solution)/shard_map/ppermute | solution.py:305
  64.3 16.9 %all-to-all-start.1 = ((bf16[8,64,128]{2,1,0:T(8,128)(2,1)}), bf16[8,64,128]{2,1,0:T(8,128)(2,1)S(1)}, u32[]{:S(2)}, u32[]{:S(2)}) async-start(bf16[8,64,128]{2,1,0:T(8,128)(2,1)} %bitcast.6), calls=%async_computation.1 | async-start | bytes 262144 | tf_op jit(solution)/shard_map/all_to_all | solution.py:27
  87.4 6.8 %collective-permute-start.4 = (bf16[16,304,128]{2,1,0:T(8,128)(2,1)S(1)}, bf16[16,304,128]{2,1,0:T(8,128)(2,1)S(1)}, u32[]{:S(2)}, u32[]{:S(2)}) collective-permute-start(bf16[16,304,128]{2,1,0:T(8,128)(2,1)S(1)} %slice_bitcast_fusion), channel_id=1, source_target_pairs={{0,8},{8,0},{1,9},{9,1},{2,10},{10,2},{3,11},{11,3},{4,12},{12,4},... | collective-permute-start | bytes 3735560 | tf_op jit(solution)/shard_map/ppermute | solution.py:305
  94.5 65.1 %copy-start = (f32[1536,128]{1,0:T(8,128)S(1)}, f32[1536,128]{1,0:T(8,128)}, u32[]{:S(2)}) copy-start(f32[1536,128]{1,0:T(8,128)} %refs_2_.3) | copy-start | bytes 2359300
  94.5 65.1 %copy-start.1 = (f32[1536,128]{1,0:T(8,128)S(1)}, f32[1536,128]{1,0:T(8,128)}, u32[]{:S(2)}) copy-start(f32[1536,128]{1,0:T(8,128)} %refs_3_.1) | copy-start | bytes 2359300
  118.1 24.5 %all-to-all-start.3 = ((bf16[16,32,128]{2,1,0:T(8,128)(2,1)}), bf16[16,32,128]{2,1,0:T(8,128)(2,1)S(1)}, u32[]{:S(2)}, u32[]{:S(2)}) async-start(bf16[16,32,128]{2,1,0:T(8,128)(2,1)} %bitcast.16), calls=%async_computation.3 | async-start | bytes 262144 | tf_op jit(solution)/shard_map/all_to_all | solution.py:27
  125.5 17.1 %collective-permute-start.5 = (f32[48,128]{1,0:T(8,128)S(1)}, f32[48,128]{1,0:T(8,128)S(1)}, u32[]{:S(2)}, u32[]{:S(2)}) collective-permute-start(f32[48,128]{1,0:T(8,128)S(1)} %convert_reduce_fusion), channel_id=1, source_target_pairs={{0,16},{16,0},{1,17},{17,1},{2,18},{18,2},{3,19},{19,3},{4,20},{20... | collective-permute-start | bytes 73736 | tf_op jit(solution)/shard_map/ppermute | solution.py:305
  153.8 5.8 %collective-permute-start.6 = (bf16[16,80,128]{2,1,0:T(8,128)(2,1)S(1)}, bf16[16,80,128]{2,1,0:T(8,128)(2,1)S(1)}, u32[]{:S(2)}, u32[]{:S(2)}) collective-permute-start(bf16[16,80,128]{2,1,0:T(8,128)(2,1)S(1)} %all_to_all.26.refs_0_), channel_id=1, source_target_pairs={{0,8},{8,0},{1,9},{9,1},{2,10},{10,2},{3,11},{11,3},{4,12},{12,4},... | collective-permute-start | bytes 983048 | tf_op jit(solution)/shard_map/ppermute | solution.py:305

commit v8 on v6

--- a/solution.py
+++ b/solution.py
@@ -13,6 +13,7 @@
 DP_EMB = ("x", "y", "zh", "core", "emb")
 XY = ("x", "y")
 ZZ = ("zh", "emb")
+
 
 loss_weight = 64.0
 learn_rate = 0.1
@@ -153,8 +154,8 @@
         pick, answers_ref[...], (((0,), (0,)), ((), ())), preferred_element_type=f32
     )
     turned = labels_ref[...].T
-    column = lax.broadcasted_iota(jnp.int32, turned.shape, 1) == home
-    targets = jnp.sum(jnp.where(column, turned, 0.0), axis=1, keepdims=True)
+    mine = lax.broadcasted_iota(jnp.int32, turned.shape, 1) == home
+    targets = jnp.sum(jnp.where(mine, turned, 0.0), axis=1, keepdims=True)
     inverse_rms = lax.rsqrt(jnp.mean(values * values, axis=1, keepdims=True) + norm_eps)
     gain = gain_ref[...]
     normed_wide = values * inverse_rms * gain
@@ -165,7 +166,7 @@
         tiles = []
         for tile in (2 * half, 2 * half + 1):
             quarters = [
-                weights_s[side, pl.ds((tile * 4 + k) * lines + hop * 32, 32), :]
+                weights_s[side, pl.ds((k * 4 + tile) * lines + hop * 32, 32), :]
                 for k in range(4)
             ]
             tiles.append(jnp.concatenate(quarters, axis=0))
@@ -324,11 +325,8 @@
     got_slots = decoded(first[:, capacity + 47], capacity)
 
     row_ids = jnp.arange(rows_shard, dtype=jnp.int32)
-    fetched = dot32(
-        (wanted[:, None] == row_ids[None, :]).astype(bf16), rows_table
-    ).astype(bf16)
-    answers = exchange(fetched.reshape(shards, capacity, width), "emb").reshape(slots, width)
-
+    hot = (wanted[:, None] == row_ids[None, :]).astype(bf16)
+    fetched = dot32(hot, rows_table).astype(bf16)
     span = rows_shard // plane // 2
     half_ids = jnp.arange(rows_shard // 2, dtype=jnp.int32)
     half_ids = half_ids // span * (2 * span) + half_ids % span
@@ -339,7 +337,10 @@
     foreign = lax.dynamic_slice(
         jnp.concatenate([slices, slices], axis=0), (home + 1, 0, 0), (shards - 1, 32, 128)
     ).reshape((shards - 1) * 32, 128)
-    own_weights = lax.all_gather(foreign, XY, axis=0, tiled=True)
+    column = to_all(foreign, "x")
+    column, fetched = lax.optimization_barrier((column, fetched))
+    answers = exchange(fetched.reshape(shards, capacity, width), "emb").reshape(slots, width)
+    own_weights = lax.all_gather(column.reshape(-1, 128), "y", axis=0, tiled=True)
     other_weights = swapped(own_weights, "core")
     emb_grad, tower_grads = tower(
         answers, cur_pos, own_weights, other_weights, w_gate, w_up, first, gain, labels,

time: 157 us -> 156 us (level)
  blocking collectives: 54 us -> 44.7 us
  waiting for transfers between devices: 28.3 us -> 33.1 us
  starting transfers between devices: 57.1 us -> 61 us
    all_gather x1, blocking collectives: 20.3 us -> 12.1 us  [step(): lax.all_gather(column.reshape(-1, 128), 'y', axis=0, tiled=True)]
    all_to_all x3 -> x4, waiting for transfers between devices: 19.4 us -> 24.2 us  [exchange(): return lax.all_to_all(pieces, axis, 0, 0, tiled=True)]
    all_to_all x3 -> x4, starting transfers between devices: 25.7 us -> 30.2 us  [exchange(): return lax.all_to_all(pieces, axis, 0, 0, tiled=True)]
  transfers between devices with their start and end apart: 7 -> 8, of which waited for: 5 -> 6; matrix products, arithmetic and copies ran while one was open for 3% -> 2% of each run, Pallas kernels for 0% -> 0%
where the time goes in v8:
time: 156 us
  starting transfers between devices  61 us (39%)
  blocking collectives  44.7 us (29%)
  waiting for transfers between devices  33.1 us (21%)
  Pallas kernels  10.5 us (7%)
  matrix products  1.98 us (1%)
  other arithmetic  1.97 us (1%)
  local copies, waits for them, and re-layouts  1.73 us (1%)
    all_to_all x2, blocking collectives, exchange(): return lax.all_to_all(pieces, axis, 0, 0, tiled=True)  32.6 us
    ppermute x4, starting transfers between devices, swapped(): return lax.ppermute(array, axis, [(0, 1), (1, 0)])  30.8 us
    all_to_all x4, starting transfers between devices, exchange(): return lax.all_to_all(pieces, axis, 0, 0, tiled=True)  30.2 us
    all_to_all x4, waiting for transfers between devices, exchange(): return lax.all_to_all(pieces, axis, 0, 0, tiled=True)  24.2 us
    all_gather x1, blocking collectives, step(): lax.all_gather(column.reshape(-1, 128), 'y', axis=0, tiled=True)  12.1 us
    ppermute x4, waiting for transfers between devices, swapped(): return lax.ppermute(array, axis, [(0, 1), (1, 0)])  8.86 us
    pallas_call x1, Pallas kernels, tower(): pl.pallas_call(tower_kernel, out_shape=(jax.ShapeDtypeStruct((tok, width)...  6.21 us
  transfers between devices with their start and end apart: 8, of which 6 were waited for; matrix products, arithmetic and copies ran while one was open for 2% of the time, Pallas kernels for 0%

profile of v8, /device:TPU:1, one launch (start us, length us, event | category | flops | bytes accessed | tf_op | source)
XLA Modules:
  0.0 155.7 jit_solution(3163366752404953293)
XLA Ops:
  0.6 2.8 %pack.1 = (bf16[8,112,128]{2,1,0:T(8,128)(2,1)}, s32[1,256]{1,0:T(1,128)}) custom-call(s32[1,256]{1,0:T(1,128)} %bitcast.35, s32[1,256]{1,0:T(1,128)} %bitcast.36, bf16[256,128]{1,0:T(8,128)(2,1)} %refs_2_.2, s32[96,128]{1,0:T(8,128)} %bitcast.33, bf16[128,512]{1,0:T(8,128)(2,1)} %w_gate_ref.1, bf16[128,512]{1,0:T(8,128)(2,1)} %w_up_ref.1, ...), custom_call_target="tpu_custom_call" | custom-call | tf_op jit(solution)/shard_map/pack/pallas_call | solution.py:119
  3.4 13.1 %all-to-all-start = ((bf16[8,112,128]{2,1,0:T(8,128)(2,1)}), bf16[8,112,128]{2,1,0:T(8,128)(2,1)S(1)}, u32[]{:S(2)}, u32[]{:S(2)}) async-start(bf16[8,112,128]{2,1,0:T(8,128)(2,1)} %get-tuple-element.15), calls=%async_computation | async-start | bytes 458752 | tf_op jit(solution)/shard_map/all_to_all | solution.py:27
  16.5 0.0 copy-start.6
  16.5 1.2 convert_element_type.47
  17.7 10.5 %all-to-all-done.shared_ref = bf16[8,112,128]{2,1,0:T(8,128)(2,1)S(1)} async-done(((bf16[8,112,128]{2,1,0:T(8,128)(2,1)}), bf16[8,112,128]{2,1,0:T(8,128)(2,1)S(1)}, u32[]{:S(2)}, u32[]{:S(2)}) %all-to-all-start) | async-done | bytes 229408 | tf_op jit(solution)/shard_map/all_to_all | solution.py:27
  28.2 0.1 slice_add_fusion.1
  28.3 0.1 eq.32
  28.4 0.1 fusion.11
  28.4 0.7 broadcast_in_dim.11
  29.1 4.0 %all-to-all-start.1 = ((bf16[4,224,128]{2,1,0:T(8,128)(2,1)}), bf16[4,224,128]{2,1,0:T(8,128)(2,1)S(1)}, u32[]{:S(2)}, u32[]{:S(2)}) async-start(bf16[4,224,128]{2,1,0:T(8,128)(2,1)} %broadcast_in_dim.11), calls=%async_computation.1 | async-start | bytes 458752 | tf_op jit(solution)/shard_map/all_to_all | solution.py:27
  33.2 0.0 copy-start.2
  33.2 0.0 copy-start.3
  33.2 0.0 copy-start.5
  33.2 1.3 fusion.10
  34.5 4.0 %all-to-all-done.1 = bf16[4,224,128]{2,1,0:T(8,128)(2,1)S(1)} async-done(((bf16[4,224,128]{2,1,0:T(8,128)(2,1)}), bf16[4,224,128]{2,1,0:T(8,128)(2,1)S(1)}, u32[]{:S(2)}, u32[]{:S(2)}) %all-to-all-start.1) | async-done | bytes 229408 | tf_op jit(solution)/shard_map/all_to_all | solution.py:27
  38.5 12.1 %all_gather.3.own_ref = bf16[3584,128]{1,0:T(8,128)(2,1)S(1)} all-gather(bf16[896,128]{1,0:T(8,128)(2,1)S(1)} %bitcast.29), channel_id=1, replica_groups=mesh['x'=4,'y'=4,'zh'=2,'core'=2,'emb'=8] {'y'}, dimensions={0}, use_global_device_ids=true | all-gather | bytes 1146880 | tf_op jit(solution)/shard_map/all_gather | solution.py:343
  50.6 10.0 %collective-permute-start = (bf16[3584,128]{1,0:T(8,128)(2,1)S(1)}, bf16[3584,128]{1,0:T(8,128)(2,1)S(1)}, u32[]{:S(2)}, u32[]{:S(2)}) collective-permute-start(bf16[3584,128]{1,0:T(8,128)(2,1)S(1)} %all_gather.3.own_ref), channel_id=1, source_target_pairs={{0,8},{8,0},{1,9},{9,1},{2,10},{10,2},{3,11},{11,3},{4,12},{12,4},... | collective-permute-start | bytes 2752520 | tf_op jit(solution)/shard_map/ppermute | solution.py:302
  60.6 0.0 copy-done.6
  60.6 5.7 %all-to-all-start.2 = ((bf16[8,64,128]{2,1,0:T(8,128)(2,1)}), bf16[8,64,128]{2,1,0:T(8,128)(2,1)S(1)}, u32[]{:S(2)}, u32[]{:S(2)}) async-start(bf16[8,64,128]{2,1,0:T(8,128)(2,1)} %bitcast.7), calls=%async_computation.2 | async-start | bytes 262144 | tf_op jit(solution)/shard_map/all_to_all | solution.py:27
  66.3 0.1 slice_add_fusion
  66.4 0.1 eq.37
  66.5 0.7 fusion.4
  67.1 9.7 %all-to-all-done.2 = bf16[8,64,128]{2,1,0:T(8,128)(2,1)S(1)} async-done(((bf16[8,64,128]{2,1,0:T(8,128)(2,1)}), bf16[8,64,128]{2,1,0:T(8,128)(2,1)S(1)}, u32[]{:S(2)}, u32[]{:S(2)}) %all-to-all-start.2) | async-done | bytes 131104 | tf_op jit(solution)/shard_map/all_to_all | solution.py:27
  76.9 0.0 collective-permute-done.other_ref
  76.9 0.0 copy-done.2
  76.9 0.0 copy-done.3
  76.9 0.0 copy-done.4
  76.9 0.0 copy-done.5
  76.9 6.2 %tower.1 = (f32[256,128]{1,0:T(8,128)}, bf16[2,16,304,128]{3,2,1,0:T(8,128)(2,1)S(1)}) custom-call(bf16[512,128]{1,0:T(8,128)(2,1)S(1)} %bitcast.26, s32[1,256]{1,0:T(1,128)S(1)} %copy-done.4, bf16[3584,128]{1,0:T(8,128)(2,1)S(1)} %all_gather.3.own_ref, bf16[3584,128]{1,0:T(8,128)(2,1)S(1)} %collective-permute-done.other_ref, ...), custom_call_target="tpu_custom_call" | custom-call | flops 1610612736 | bytes 5242880 | tf_op jit(solution)/shard_map/tower/pallas_call | solution.py:239
  83.1 0.1 slice_bitcast_fusion
  83.2 4.2 %collective-permute-start.1 = (bf16[16,304,128]{2,1,0:T(8,128)(2,1)S(1)}, bf16[16,304,128]{2,1,0:T(8,128)(2,1)S(1)}, u32[]{:S(2)}, u32[]{:S(2)}) collective-permute-start(bf16[16,304,128]{2,1,0:T(8,128)(2,1)S(1)} %slice_bitcast_fusion), channel_id=1, source_target_pairs={{0,8},{8,0},{1,9},{9,1},{2,10},{10,2},{3,11},{11,3},{4,12},{12,4},... | collective-permute-start | bytes 3735560 | tf_op jit(solution)/shard_map/ppermute | solution.py:302
  87.4 2.5 %collective-permute-done.1 = bf16[16,304,128]{2,1,0:T(8,128)(2,1)S(1)} collective-permute-done((bf16[16,304,128]{2,1,0:T(8,128)(2,1)S(1)}, bf16[16,304,128]{2,1,0:T(8,128)(2,1)S(1)}, u32[]{:S(2)}, u32[]{:S(2)}) %collective-permute-start.1) | collective-permute-done | bytes 1245216 | tf_op jit(solution)/shard_map/ppermute | solution.py:302
  90.0 0.3 fusion.3
  90.3 0.0 copy-start
  90.3 0.0 copy-start.1
  90.3 21.5 %all_to_all.30 = bf16[16,304,128]{2,1,0:T(8,128)(2,1)S(1)} all-to-all(bf16[16,304,128]{2,1,0:T(8,128)(2,1)S(1)} %fusion.3), channel_id=1, replica_groups=mesh['x'=4,'y'=4,'zh'=2,'core'=2,'emb'=8] {'x','y'}, dimensions={0} | all-to-all | bytes 2490368 | tf_op jit(solution)/shard_map/all_to_all | solution.py:27
  111.8 0.1 slice_reduce_fusion
  111.9 0.7 broadcast_in_dim.25
  112.6 7.4 %all-to-all-start.4 = ((bf16[16,32,128]{2,1,0:T(8,128)(2,1)}), bf16[16,32,128]{2,1,0:T(8,128)(2,1)S(1)}, u32[]{:S(2)}, u32[]{:S(2)}) async-start(bf16[16,32,128]{2,1,0:T(8,128)(2,1)} %bitcast.17), calls=%async_computation.4 | async-start | bytes 262144 | tf_op jit(solution)/shard_map/all_to_all | solution.py:27
  120.1 12.0 %collective-permute-start.2 = (f32[48,128]{1,0:T(8,128)S(1)}, f32[48,128]{1,0:T(8,128)S(1)}, u32[]{:S(2)}, u32[]{:S(2)}) collective-permute-start(f32[48,128]{1,0:T(8,128)S(1)} %convert_reduce_fusion), channel_id=1, source_target_pairs={{0,16},{16,0},{1,17},{17,1},{2,18},{18,2},{3,19},{19,3},{4,20},{20... | collective-permute-start | bytes 73736 | tf_op jit(solution)/shard_map/ppermute | solution.py:302
  132.1 5.1 %collective-permute-done.2 = f32[48,128]{1,0:T(8,128)S(1)} collective-permute-done((f32[48,128]{1,0:T(8,128)S(1)}, f32[48,128]{1,0:T(8,128)S(1)}, u32[]{:S(2)}, u32[]{:S(2)}) %collective-permute-start.2) | collective-permute-done | bytes 24608 | tf_op jit(solution)/shard_map/ppermute | solution.py:302
  137.2 0.0 all-to-all-done.4
  137.3 11.1 %all_to_all.31.refs_0_ = bf16[16,80,128]{2,1,0:T(8,128)(2,1)S(1)} all-to-all(bf16[16,80,128]{2,1,0:T(8,128)(2,1)S(1)} %broadcast_in_dim.26), channel_id=1, replica_groups=mesh['x'=4,'y'=4,'zh'=2,'core'=2,'emb'=8] {'x','y'}, dimensions={0} | all-to-all | bytes 655360 | tf_op jit(solution)/shard_map/all_to_all | solution.py:27
  148.4 4.6 %collective-permute-start.3 = (bf16[16,80,128]{2,1,0:T(8,128)(2,1)S(1)}, bf16[16,80,128]{2,1,0:T(8,128)(2,1)S(1)}, u32[]{:S(2)}, u32[]{:S(2)}) collective-permute-start(bf16[16,80,128]{2,1,0:T(8,128)(2,1)S(1)} %all_to_all.31.refs_0_), channel_id=1, source_target_pairs={{0,8},{8,0},{1,9},{9,1},{2,10},{10,2},{3,11},{11,3},{4,12},{12,4},... | collective-permute-start | bytes 983048 | tf_op jit(solution)/shard_map/ppermute | solution.py:302
  153.0 1.2 collective-permute-done.3.refs_1_
  154.2 0.0 copy-done
  154.2 0.0 copy-done.1
  154.2 1.5 update.1
  (13 shorter events, 0.2 us)
Async XLA Ops:
  3.4 24.7 %all-to-all-start = ((bf16[8,112,128]{2,1,0:T(8,128)(2,1)}), bf16[8,112,128]{2,1,0:T(8,128)(2,1)S(1)}, u32[]{:S(2)}, u32[]{:S(2)}) async-start(bf16[8,112,128]{2,1,0:T(8,128)(2,1)} %get-tuple-element.15), calls=%async_computation | async-start | bytes 458752 | tf_op jit(solution)/shard_map/all_to_all | solution.py:27
  16.5 44.1 %copy-start.6 = (f32[2048]{0:T(1024)S(1)}, f32[2048]{0:T(1024)}, u32[]{:S(2)}) copy-start(f32[2048]{0:T(1024)} %param.17) | copy-start | bytes 24580
  29.1 9.4 %all-to-all-start.1 = ((bf16[4,224,128]{2,1,0:T(8,128)(2,1)}), bf16[4,224,128]{2,1,0:T(8,128)(2,1)S(1)}, u32[]{:S(2)}, u32[]{:S(2)}) async-start(bf16[4,224,128]{2,1,0:T(8,128)(2,1)} %broadcast_in_dim.11), calls=%async_computation.1 | async-start | bytes 458752 | tf_op jit(solution)/shard_map/all_to_all | solution.py:27
  33.2 43.7 %copy-start.2 = (bf16[128,512]{1,0:T(8,128)(2,1)S(1)}, bf16[128,512]{1,0:T(8,128)(2,1)}, u32[]{:S(2)}) copy-start(bf16[128,512]{1,0:T(8,128)(2,1)} %w_gate_ref.1) | copy-start | bytes 393220
  33.2 43.7 %copy-start.3 = (bf16[128,512]{1,0:T(8,128)(2,1)S(1)}, bf16[128,512]{1,0:T(8,128)(2,1)}, u32[]{:S(2)}) copy-start(bf16[128,512]{1,0:T(8,128)(2,1)} %w_up_ref.1) | copy-start | bytes 393220
  33.2 43.7 %copy-start.4 = (s32[1,256]{1,0:T(1,128)S(1)}, s32[1,256]{1,0:T(1,128)}, u32[]{:S(2)}) copy-start(s32[1,256]{1,0:T(1,128)} %get-tuple-element.17.target_ref) | copy-start | bytes 3076
  33.2 43.7 %copy-start.5 = (f32[128]{0:T(128)S(1)}, f32[128]{0:T(128)}, u32[]{:S(2)}) copy-start(f32[128]{0:T(128)} %param.18) | copy-start | bytes 1540
  50.6 26.3 %collective-permute-start = (bf16[3584,128]{1,0:T(8,128)(2,1)S(1)}, bf16[3584,128]{1,0:T(8,128)(2,1)S(1)}, u32[]{:S(2)}, u32[]{:S(2)}) collective-permute-start(bf16[3584,128]{1,0:T(8,128)(2,1)S(1)} %all_gather.3.own_ref), channel_id=1, source_target_pairs={{0,8},{8,0},{1,9},{9,1},{2,10},{10,2},{3,11},{11,3},{4,12},{12,4},... | collective-permute-start | bytes 2752520 | tf_op jit(solution)/shard_map/ppermute | solution.py:302
  60.6 16.3 %all-to-all-start.2 = ((bf16[8,64,128]{2,1,0:T(8,128)(2,1)}), bf16[8,64,128]{2,1,0:T(8,128)(2,1)S(1)}, u32[]{:S(2)}, u32[]{:S(2)}) async-start(bf16[8,64,128]{2,1,0:T(8,128)(2,1)} %bitcast.7), calls=%async_computation.2 | async-start | bytes 262144 | tf_op jit(solution)/shard_map/all_to_all | solution.py:27
  83.2 6.8 %collective-permute-start.1 = (bf16[16,304,128]{2,1,0:T(8,128)(2,1)S(1)}, bf16[16,304,128]{2,1,0:T(8,128)(2,1)S(1)}, u32[]{:S(2)}, u32[]{:S(2)}) collective-permute-start(bf16[16,304,128]{2,1,0:T(8,128)(2,1)S(1)} %slice_bitcast_fusion), channel_id=1, source_target_pairs={{0,8},{8,0},{1,9},{9,1},{2,10},{10,2},{3,11},{11,3},{4,12},{12,4},... | collective-permute-start | bytes 3735560 | tf_op jit(solution)/shard_map/ppermute | solution.py:302
  90.3 63.9 %copy-start = (f32[1536,128]{1,0:T(8,128)S(1)}, f32[1536,128]{1,0:T(8,128)}, u32[]{:S(2)}) copy-start(f32[1536,128]{1,0:T(8,128)} %refs_2_.3) | copy-start | bytes 2359300
  90.3 63.9 %copy-start.1 = (f32[1536,128]{1,0:T(8,128)S(1)}, f32[1536,128]{1,0:T(8,128)}, u32[]{:S(2)}) copy-start(f32[1536,128]{1,0:T(8,128)} %refs_3_.1) | copy-start | bytes 2359300
  112.6 24.5 %all-to-all-start.4 = ((bf16[16,32,128]{2,1,0:T(8,128)(2,1)}), bf16[16,32,128]{2,1,0:T(8,128)(2,1)S(1)}, u32[]{:S(2)}, u32[]{:S(2)}) async-start(bf16[16,32,128]{2,1,0:T(8,128)(2,1)} %bitcast.17), calls=%async_computation.4 | async-start | bytes 262144 | tf_op jit(solution)/shard_map/all_to_all | solution.py:27
  120.1 17.1 %collective-permute-start.2 = (f32[48,128]{1,0:T(8,128)S(1)}, f32[48,128]{1,0:T(8,128)S(1)}, u32[]{:S(2)}, u32[]{:S(2)}) collective-permute-start(f32[48,128]{1,0:T(8,128)S(1)} %convert_reduce_fusion), channel_id=1, source_target_pairs={{0,16},{16,0},{1,17},{17,1},{2,18},{18,2},{3,19},{19,3},{4,20},{20... | collective-permute-start | bytes 73736 | tf_op jit(solution)/shard_map/ppermute | solution.py:302
  148.4 5.8 %collective-permute-start.3 = (bf16[16,80,128]{2,1,0:T(8,128)(2,1)S(1)}, bf16[16,80,128]{2,1,0:T(8,128)(2,1)S(1)}, u32[]{:S(2)}, u32[]{:S(2)}) collective-permute-start(bf16[16,80,128]{2,1,0:T(8,128)(2,1)S(1)} %all_to_all.31.refs_0_), channel_id=1, source_target_pairs={{0,8},{8,0},{1,9},{9,1},{2,10},{10,2},{3,11},{11,3},{4,12},{12,4},... | collective-permute-start | bytes 983048 | tf_op jit(solution)/shard_map/ppermute | solution.py:302

commit v9 on v8

--- a/solution.py
+++ b/solution.py
@@ -94,8 +94,10 @@
     for i in (2, 4, 5, 6):
         copies[i].wait()
     rows = dot32(pack, grads_ref[...]).astype(bf16)
-    at = lax.axis_index(XY)
-    cut = (pl.ds(pl.multiple_of((at % 4) * 32, 32), 32), pl.ds(pl.multiple_of((at // 4) * 128, 128), 128))
+    cut = (
+        pl.ds(pl.multiple_of((lax.axis_index("x") % 2) * 64, 64), 64),
+        pl.ds(pl.multiple_of(lax.axis_index("y") * 128, 128), 128),
+    )
     gate_slice = w_gate_ref[cut].astype(f32)
     up_slice = w_up_ref[cut].astype(f32)
     own = jnp.where(lax.axis_index("core") == 0, gate_slice, up_slice).astype(bf16)
@@ -103,10 +105,10 @@
     tail_row = lax.broadcasted_iota(jnp.int32, (16, 128), 0)
     for shard in range(shards):
         out_ref[shard, :capacity, :] = rows[shard * capacity : (shard + 1) * capacity]
-        out_ref[shard, capacity : capacity + 32, :] = own
+        out_ref[shard, capacity : capacity + 64, :] = own
         tail = jnp.where(tail_row == 14, cur_code[shard : shard + 1], out)
         tail = jnp.where(tail_row == 15, prev_code[shard : shard + 1], tail)
-        out_ref[shard, capacity + 32 : capacity + 48, :] = tail.astype(bf16)
+        out_ref[shard, capacity + 64 : capacity + 80, :] = tail.astype(bf16)
 
 
 def pack(cur_ids, prev_ids, prev_grads, row_place, w_gate, w_up, w_out, shards, capacity, rows_shard):
@@ -119,7 +121,7 @@
     return pl.pallas_call(
         lambda *refs: pack_kernel(*refs, capacity=capacity, rows_shard=rows_shard),
         out_shape=(
-            jax.ShapeDtypeStruct((shards, capacity + 48, 128), bf16),
+            jax.ShapeDtypeStruct((shards, capacity + 80, 128), bf16),
             jax.ShapeDtypeStruct((1, tok), jnp.int32),
         ),
         in_specs=[pl.BlockSpec(memory_space=pltpu.HBM)] * len(arrays),
@@ -143,7 +145,7 @@
     tok = target_ref.shape[1]
     width = answers_ref.shape[1]
     shards, span = shared_ref.shape[:2]
-    lines = own_ref.shape[0] // 16
+    lines = own_ref.shape[0] // 8
     core = lax.axis_index("core")
     home = lax.axis_index("emb")
     weights_s[core] = own_ref[...]
@@ -162,14 +164,16 @@
     normed = normed_wide.astype(bf16)
     normed_t = normed_wide.T.astype(bf16)
 
+    turns = (lax.axis_index("x") % 2, 1 - lax.axis_index("x") % 2)
+
     def far_block(hop, half, side):
         tiles = []
         for tile in (2 * half, 2 * half + 1):
-            quarters = [
-                weights_s[side, pl.ds((k * 4 + tile) * lines + hop * 32, 32), :]
-                for k in range(4)
+            parts = [
+                weights_s[side, pl.ds(pl.multiple_of((tile * 2 + turn) * lines + hop * 64, 64), 64), :]
+                for turn in turns
             ]
-            tiles.append(jnp.concatenate(quarters, axis=0))
+            tiles.append(jnp.concatenate(parts, axis=0))
         return jnp.concatenate(tiles, axis=1)
 
     def home_block(hop, half, side):
@@ -320,9 +324,9 @@
     first = exchange(payload, "emb")
     rows_table = lax.optimization_barrier(table.astype(bf16))
     got_rows = first[:, :capacity].reshape(slots, width)
-    slices = first[:, capacity : capacity + 32]
-    wanted = decoded(first[:, capacity + 46], capacity)
-    got_slots = decoded(first[:, capacity + 47], capacity)
+    slices = first[:, capacity : capacity + 64]
+    wanted = decoded(first[:, capacity + 78], capacity)
+    got_slots = decoded(first[:, capacity + 79], capacity)
 
     row_ids = jnp.arange(rows_shard, dtype=jnp.int32)
     hot = (wanted[:, None] == row_ids[None, :]).astype(bf16)
@@ -335,12 +339,13 @@
     table_part = table_part.astype(bf16).reshape(2, plane, span, width)
 
     foreign = lax.dynamic_slice(
-        jnp.concatenate([slices, slices], axis=0), (home + 1, 0, 0), (shards - 1, 32, 128)
-    ).reshape((shards - 1) * 32, 128)
-    column = to_all(foreign, "x")
-    column, fetched = lax.optimization_barrier((column, fetched))
+        jnp.concatenate([slices, slices], axis=0), (home + 1, 0, 0), (shards - 1, 64, 128)
+    ).reshape((shards - 1) * 64, 128)
+    beside = lax.ppermute(foreign, "x", [(i, i ^ 1) for i in range(lax.axis_size("x"))])
     answers = exchange(fetched.reshape(shards, capacity, width), "emb").reshape(slots, width)
-    own_weights = lax.all_gather(column.reshape(-1, 128), "y", axis=0, tiled=True)
+    own_weights = lax.all_gather(
+        jnp.concatenate([foreign, beside], axis=0), "y", axis=0, tiled=True
+    )
     other_weights = swapped(own_weights, "core")
     emb_grad, tower_grads = tower(
         answers, cur_pos, own_weights, other_weights, w_gate, w_up, first, gain, labels,

time: 156 us -> 158 us (1.013)
  blocking collectives: 44.7 us -> 47.2 us
  starting transfers between devices: 61 us -> 58.7 us
    all_to_all x4 -> x3, starting transfers between devices: 30.2 us -> 25.3 us  [exchange(): return lax.all_to_all(pieces, axis, 0, 0, tiled=True)]
    ppermute x0 -> x1, starting transfers between devices: none -> 3.13 us  [step(): lax.ppermute(foreign, 'x', [(i, i ^ 1) for i in range(lax.axis_size('x'))])]
    ppermute x0 -> x1, waiting for transfers between devices: none -> 2.32 us  [step(): lax.ppermute(foreign, 'x', [(i, i ^ 1) for i in range(lax.axis_size('x'))])]
    all_to_all x2, blocking collectives: 32.6 us -> 34.7 us  [exchange(): return lax.all_to_all(pieces, axis, 0, 0, tiled=True)]
    all_to_all x4 -> x3, waiting for transfers between devices: 24.2 us -> 22.8 us  [exchange(): return lax.all_to_all(pieces, axis, 0, 0, tiled=True)]
  transfers between devices with their start and end apart: 8 -> 8, of which waited for: 6 -> 6; matrix products, arithmetic and copies ran while one was open for 2% -> 3% of each run, Pallas kernels for 0% -> 0%
where the time goes in v9:
time: 158 us; the launch traced here: 157 us
  starting transfers between devices  58.7 us (37%)
  blocking collectives  47.2 us (30%)
  waiting for transfers between devices  34 us (22%)
  Pallas kernels  10.6 us (7%)
  other arithmetic  1.99 us (1%)
  matrix products  1.99 us (1%)
  local copies, waits for them, and re-layouts  1.71 us (1%)
    all_to_all x2, blocking collectives, exchange(): return lax.all_to_all(pieces, axis, 0, 0, tiled=True)  34.7 us
    ppermute x4, starting transfers between devices, swapped(): return lax.ppermute(array, axis, [(0, 1), (1, 0)])  30.3 us
    all_to_all x3, starting transfers between devices, exchange(): return lax.all_to_all(pieces, axis, 0, 0, tiled=True)  25.3 us
    all_to_all x3, waiting for transfers between devices, exchange(): return lax.all_to_all(pieces, axis, 0, 0, tiled=True)  22.8 us
    all_gather x1, blocking collectives, step(): lax.all_gather(jnp.concatenate([foreign, beside], axis=0), 'y', axis=0, t...  12.4 us
    ppermute x4, waiting for transfers between devices, swapped(): return lax.ppermute(array, axis, [(0, 1), (1, 0)])  8.86 us
    pallas_call x1, Pallas kernels, tower(): pl.pallas_call(tower_kernel, out_shape=(jax.ShapeDtypeStruct((tok, width)...  6.27 us
  transfers between devices with their start and end apart: 8, of which 6 were waited for; matrix products, arithmetic and copies ran while one was open for 3% of the time, Pallas kernels for 0%

profile of v9, /device:TPU:1, one launch (start us, length us, event | category | flops | bytes accessed | tf_op | source)
XLA Modules:
  0.0 157.0 jit_solution(3088581925033445746)
XLA Ops:
  0.6 2.8 %pack.1 = (bf16[8,144,128]{2,1,0:T(8,128)(2,1)}, s32[1,256]{1,0:T(1,128)}) custom-call(s32[1,256]{1,0:T(1,128)} %bitcast.34, s32[1,256]{1,0:T(1,128)} %bitcast.35, bf16[256,128]{1,0:T(8,128)(2,1)} %refs_2_.2, s32[96,128]{1,0:T(8,128)} %bitcast.32, bf16[128,512]{1,0:T(8,128)(2,1)} %w_gate_ref.1, bf16[128,512]{1,0:T(8,128)(2,1)} %w_up_ref.1, ...), custom_call_target="tpu_custom_call" | custom-call | tf_op jit(solution)/shard_map/pack/pallas_call | solution.py:121
  3.5 13.1 %all-to-all-start = ((bf16[8,144,128]{2,1,0:T(8,128)(2,1)}), bf16[8,144,128]{2,1,0:T(8,128)(2,1)S(1)}, u32[]{:S(2)}, u32[]{:S(2)}) async-start(bf16[8,144,128]{2,1,0:T(8,128)(2,1)} %get-tuple-element.13), calls=%async_computation | async-start | bytes 589824 | tf_op jit(solution)/shard_map/all_to_all | solution.py:27
  16.5 0.7 reshape.66.labels_ref
  17.2 1.2 convert_element_type.47
  18.4 13.0 %all-to-all-done.shared_ref = bf16[8,144,128]{2,1,0:T(8,128)(2,1)S(1)} async-done(((bf16[8,144,128]{2,1,0:T(8,128)(2,1)}), bf16[8,144,128]{2,1,0:T(8,128)(2,1)S(1)}, u32[]{:S(2)}, u32[]{:S(2)}) %all-to-all-start) | async-done | bytes 294944 | tf_op jit(solution)/shard_map/all_to_all | solution.py:27
  31.5 0.1 fusion.11
  31.6 3.1 %collective-permute-start = (bf16[448,128]{1,0:T(8,128)(2,1)S(1)}, bf16[448,128]{1,0:T(8,128)(2,1)S(1)}, u32[]{:S(2)}, u32[]{:S(2)}) collective-permute-start(bf16[448,128]{1,0:T(8,128)(2,1)S(1)} %bitcast.28), channel_id=1, source_target_pairs={{0,128},{128,0},{256,384},{384,256},{1,129},{129,1},{257,385},{385... | collective-permute-start | bytes 344072 | tf_op jit(solution)/shard_map/ppermute | solution.py:344
  34.8 0.0 copy-start.2
  34.8 0.0 copy-start.3
  34.8 0.0 copy-start.4
  34.8 0.0 copy-start.5
  34.8 2.3 %collective-permute-done = bf16[448,128]{1,0:T(8,128)(2,1)S(1)} collective-permute-done((bf16[448,128]{1,0:T(8,128)(2,1)S(1)}, bf16[448,128]{1,0:T(8,128)(2,1)S(1)}, u32[]{:S(2)}, u32[]{:S(2)}) %collective-permute-start) | collective-permute-done | bytes 114720 | tf_op jit(solution)/shard_map/ppermute | solution.py:344
  37.1 12.4 %all_gather.3.own_ref = bf16[3584,128]{1,0:T(8,128)(2,1)S(1)} all-gather(bf16[896,128]{1,0:T(8,128)(2,1)S(1)} %pad_maximum_fusion), channel_id=1, replica_groups=mesh['x'=4,'y'=4,'zh'=2,'core'=2,'emb'=8] {'y'}, dimensions={0}, use_global_device_ids=true | all-gather | bytes 1146880 | tf_op jit(solution)/shard_map/all_gather | solution.py:346
  49.6 9.5 %collective-permute-start.1 = (bf16[3584,128]{1,0:T(8,128)(2,1)S(1)}, bf16[3584,128]{1,0:T(8,128)(2,1)S(1)}, u32[]{:S(2)}, u32[]{:S(2)}) collective-permute-start(bf16[3584,128]{1,0:T(8,128)(2,1)S(1)} %all_gather.3.own_ref), channel_id=1, source_target_pairs={{0,8},{8,0},{1,9},{9,1},{2,10},{10,2},{3,11},{11,3},{4,12},{12,4},... | collective-permute-start | bytes 2752520 | tf_op jit(solution)/shard_map/ppermute | solution.py:306
  59.1 0.1 slice_add_fusion.1
  59.2 0.1 eq.32
  59.2 1.3 fusion.10
  60.6 4.8 %all-to-all-start.1 = ((bf16[8,64,128]{2,1,0:T(8,128)(2,1)}), bf16[8,64,128]{2,1,0:T(8,128)(2,1)S(1)}, u32[]{:S(2)}, u32[]{:S(2)}) async-start(bf16[8,64,128]{2,1,0:T(8,128)(2,1)} %bitcast.6), calls=%async_computation.1 | async-start | bytes 262144 | tf_op jit(solution)/shard_map/all_to_all | solution.py:27
  65.4 0.1 slice_add_fusion
  65.5 0.1 eq.37
  65.6 0.7 fusion.4
  66.2 9.8 %all-to-all-done.1 = bf16[8,64,128]{2,1,0:T(8,128)(2,1)S(1)} async-done(((bf16[8,64,128]{2,1,0:T(8,128)(2,1)}), bf16[8,64,128]{2,1,0:T(8,128)(2,1)S(1)}, u32[]{:S(2)}, u32[]{:S(2)}) %all-to-all-start.1) | async-done | bytes 131104 | tf_op jit(solution)/shard_map/all_to_all | solution.py:27
  76.0 0.0 collective-permute-done.1.other_ref
  76.0 0.0 copy-done.2
  76.0 0.0 copy-done.3
  76.0 0.0 copy-done.4
  76.0 0.0 copy-done.5
  76.0 6.3 %tower.1 = (f32[256,128]{1,0:T(8,128)}, bf16[2,16,304,128]{3,2,1,0:T(8,128)(2,1)S(1)}) custom-call(bf16[512,128]{1,0:T(8,128)(2,1)S(1)} %bitcast.25, s32[1,256]{1,0:T(1,128)S(1)} %copy-done.4, bf16[3584,128]{1,0:T(8,128)(2,1)S(1)} %all_gather.3.own_ref, bf16[3584,128]{1,0:T(8,128)(2,1)S(1)} %collective-permute-done.1.other_ref, ...), custom_call_target="tpu_custom_call" | custom-call | flops 1610612736 | bytes 5242880 | tf_op jit(solution)/shard_map/tower/pallas_call | solution.py:243
  82.3 0.1 slice_bitcast_fusion
  82.4 4.2 %collective-permute-start.2 = (bf16[16,304,128]{2,1,0:T(8,128)(2,1)S(1)}, bf16[16,304,128]{2,1,0:T(8,128)(2,1)S(1)}, u32[]{:S(2)}, u32[]{:S(2)}) collective-permute-start(bf16[16,304,128]{2,1,0:T(8,128)(2,1)S(1)} %slice_bitcast_fusion), channel_id=1, source_target_pairs={{0,8},{8,0},{1,9},{9,1},{2,10},{10,2},{3,11},{11,3},{4,12},{12,4},... | collective-permute-start | bytes 3735560 | tf_op jit(solution)/shard_map/ppermute | solution.py:306
  86.6 2.5 %collective-permute-done.2 = bf16[16,304,128]{2,1,0:T(8,128)(2,1)S(1)} collective-permute-done((bf16[16,304,128]{2,1,0:T(8,128)(2,1)S(1)}, bf16[16,304,128]{2,1,0:T(8,128)(2,1)S(1)}, u32[]{:S(2)}, u32[]{:S(2)}) %collective-permute-start.2) | collective-permute-done | bytes 1245216 | tf_op jit(solution)/shard_map/ppermute | solution.py:306
  89.1 0.3 fusion.3
  89.5 0.0 copy-start
  89.5 0.0 copy-start.1
  89.5 23.6 %all_to_all.25 = bf16[16,304,128]{2,1,0:T(8,128)(2,1)S(1)} all-to-all(bf16[16,304,128]{2,1,0:T(8,128)(2,1)S(1)} %fusion.3), channel_id=1, replica_groups=mesh['x'=4,'y'=4,'zh'=2,'core'=2,'emb'=8] {'x','y'}, dimensions={0} | all-to-all | bytes 2490368 | tf_op jit(solution)/shard_map/all_to_all | solution.py:27
  113.1 0.1 slice_reduce_fusion
  113.2 0.7 broadcast_in_dim.7
  113.9 7.4 %all-to-all-start.3 = ((bf16[16,32,128]{2,1,0:T(8,128)(2,1)}), bf16[16,32,128]{2,1,0:T(8,128)(2,1)S(1)}, u32[]{:S(2)}, u32[]{:S(2)}) async-start(bf16[16,32,128]{2,1,0:T(8,128)(2,1)} %bitcast.16), calls=%async_computation.3 | async-start | bytes 262144 | tf_op jit(solution)/shard_map/all_to_all | solution.py:27
  121.4 12.0 %collective-permute-start.3 = (f32[48,128]{1,0:T(8,128)S(1)}, f32[48,128]{1,0:T(8,128)S(1)}, u32[]{:S(2)}, u32[]{:S(2)}) collective-permute-start(f32[48,128]{1,0:T(8,128)S(1)} %convert_reduce_fusion), channel_id=1, source_target_pairs={{0,16},{16,0},{1,17},{17,1},{2,18},{18,2},{3,19},{19,3},{4,20},{20... | collective-permute-start | bytes 73736 | tf_op jit(solution)/shard_map/ppermute | solution.py:306
  133.4 5.1 %collective-permute-done.3 = f32[48,128]{1,0:T(8,128)S(1)} collective-permute-done((f32[48,128]{1,0:T(8,128)S(1)}, f32[48,128]{1,0:T(8,128)S(1)}, u32[]{:S(2)}, u32[]{:S(2)}) %collective-permute-start.3) | collective-permute-done | bytes 24608 | tf_op jit(solution)/shard_map/ppermute | solution.py:306
  138.4 0.0 all-to-all-done.3
  138.5 11.1 %all_to_all.26.refs_0_ = bf16[16,80,128]{2,1,0:T(8,128)(2,1)S(1)} all-to-all(bf16[16,80,128]{2,1,0:T(8,128)(2,1)S(1)} %broadcast_in_dim.8), channel_id=1, replica_groups=mesh['x'=4,'y'=4,'zh'=2,'core'=2,'emb'=8] {'x','y'}, dimensions={0} | all-to-all | bytes 655360 | tf_op jit(solution)/shard_map/all_to_all | solution.py:27
  149.7 4.6 %collective-permute-start.4 = (bf16[16,80,128]{2,1,0:T(8,128)(2,1)S(1)}, bf16[16,80,128]{2,1,0:T(8,128)(2,1)S(1)}, u32[]{:S(2)}, u32[]{:S(2)}) collective-permute-start(bf16[16,80,128]{2,1,0:T(8,128)(2,1)S(1)} %all_to_all.26.refs_0_), channel_id=1, source_target_pairs={{0,8},{8,0},{1,9},{9,1},{2,10},{10,2},{3,11},{11,3},{4,12},{12,4},... | collective-permute-start | bytes 983048 | tf_op jit(solution)/shard_map/ppermute | solution.py:306
  154.3 1.2 collective-permute-done.4.refs_1_
  155.5 0.0 copy-done
  155.5 0.0 copy-done.1
  155.5 1.5 update.1
  (11 shorter events, 0.2 us)
Async XLA Ops:
  3.5 28.0 %all-to-all-start = ((bf16[8,144,128]{2,1,0:T(8,128)(2,1)}), bf16[8,144,128]{2,1,0:T(8,128)(2,1)S(1)}, u32[]{:S(2)}, u32[]{:S(2)}) async-start(bf16[8,144,128]{2,1,0:T(8,128)(2,1)} %get-tuple-element.13), calls=%async_computation | async-start | bytes 589824 | tf_op jit(solution)/shard_map/all_to_all | solution.py:27
  31.6 5.5 %collective-permute-start = (bf16[448,128]{1,0:T(8,128)(2,1)S(1)}, bf16[448,128]{1,0:T(8,128)(2,1)S(1)}, u32[]{:S(2)}, u32[]{:S(2)}) collective-permute-start(bf16[448,128]{1,0:T(8,128)(2,1)S(1)} %bitcast.28), channel_id=1, source_target_pairs={{0,128},{128,0},{256,384},{384,256},{1,129},{129,1},{257,385},{385... | collective-permute-start | bytes 344072 | tf_op jit(solution)/shard_map/ppermute | solution.py:344
  34.8 41.2 %copy-start.2 = (bf16[128,512]{1,0:T(8,128)(2,1)S(1)}, bf16[128,512]{1,0:T(8,128)(2,1)}, u32[]{:S(2)}) copy-start(bf16[128,512]{1,0:T(8,128)(2,1)} %w_gate_ref.1) | copy-start | bytes 393220
  34.8 41.2 %copy-start.3 = (bf16[128,512]{1,0:T(8,128)(2,1)S(1)}, bf16[128,512]{1,0:T(8,128)(2,1)}, u32[]{:S(2)}) copy-start(bf16[128,512]{1,0:T(8,128)(2,1)} %w_up_ref.1) | copy-start | bytes 393220
  34.8 41.2 %copy-start.4 = (s32[1,256]{1,0:T(1,128)S(1)}, s32[1,256]{1,0:T(1,128)}, u32[]{:S(2)}) copy-start(s32[1,256]{1,0:T(1,128)} %get-tuple-element.14.target_ref) | copy-start | bytes 3076
  34.8 41.2 %copy-start.5 = (f32[128]{0:T(128)S(1)}, f32[128]{0:T(128)}, u32[]{:S(2)}) copy-start(f32[128]{0:T(128)} %param.18) | copy-start | bytes 1540
  49.6 26.4 %collective-permute-start.1 = (bf16[3584,128]{1,0:T(8,128)(2,1)S(1)}, bf16[3584,128]{1,0:T(8,128)(2,1)S(1)}, u32[]{:S(2)}, u32[]{:S(2)}) collective-permute-start(bf16[3584,128]{1,0:T(8,128)(2,1)S(1)} %all_gather.3.own_ref), channel_id=1, source_target_pairs={{0,8},{8,0},{1,9},{9,1},{2,10},{10,2},{3,11},{11,3},{4,12},{12,4},... | collective-permute-start | bytes 2752520 | tf_op jit(solution)/shard_map/ppermute | solution.py:306
  60.6 15.4 %all-to-all-start.1 = ((bf16[8,64,128]{2,1,0:T(8,128)(2,1)}), bf16[8,64,128]{2,1,0:T(8,128)(2,1)S(1)}, u32[]{:S(2)}, u32[]{:S(2)}) async-start(bf16[8,64,128]{2,1,0:T(8,128)(2,1)} %bitcast.6), calls=%async_computation.1 | async-start | bytes 262144 | tf_op jit(solution)/shard_map/all_to_all | solution.py:27
  82.4 6.8 %collective-permute-start.2 = (bf16[16,304,128]{2,1,0:T(8,128)(2,1)S(1)}, bf16[16,304,128]{2,1,0:T(8,128)(2,1)S(1)}, u32[]{:S(2)}, u32[]{:S(2)}) collective-permute-start(bf16[16,304,128]{2,1,0:T(8,128)(2,1)S(1)} %slice_bitcast_fusion), channel_id=1, source_target_pairs={{0,8},{8,0},{1,9},{9,1},{2,10},{10,2},{3,11},{11,3},{4,12},{12,4},... | collective-permute-start | bytes 3735560 | tf_op jit(solution)/shard_map/ppermute | solution.py:306
  89.5 66.0 %copy-start = (f32[1536,128]{1,0:T(8,128)S(1)}, f32[1536,128]{1,0:T(8,128)}, u32[]{:S(2)}) copy-start(f32[1536,128]{1,0:T(8,128)} %refs_2_.3) | copy-start | bytes 2359300
  89.5 66.0 %copy-start.1 = (f32[1536,128]{1,0:T(8,128)S(1)}, f32[1536,128]{1,0:T(8,128)}, u32[]{:S(2)}) copy-start(f32[1536,128]{1,0:T(8,128)} %refs_3_.1) | copy-start | bytes 2359300
  113.9 24.5 %all-to-all-start.3 = ((bf16[16,32,128]{2,1,0:T(8,128)(2,1)}), bf16[16,32,128]{2,1,0:T(8,128)(2,1)S(1)}, u32[]{:S(2)}, u32[]{:S(2)}) async-start(bf16[16,32,128]{2,1,0:T(8,128)(2,1)} %bitcast.16), calls=%async_computation.3 | async-start | bytes 262144 | tf_op jit(solution)/shard_map/all_to_all | solution.py:27
  121.4 17.1 %collective-permute-start.3 = (f32[48,128]{1,0:T(8,128)S(1)}, f32[48,128]{1,0:T(8,128)S(1)}, u32[]{:S(2)}, u32[]{:S(2)}) collective-permute-start(f32[48,128]{1,0:T(8,128)S(1)} %convert_reduce_fusion), channel_id=1, source_target_pairs={{0,16},{16,0},{1,17},{17,1},{2,18},{18,2},{3,19},{19,3},{4,20},{20... | collective-permute-start | bytes 73736 | tf_op jit(solution)/shard_map/ppermute | solution.py:306
  149.7 5.8 %collective-permute-start.4 = (bf16[16,80,128]{2,1,0:T(8,128)(2,1)S(1)}, bf16[16,80,128]{2,1,0:T(8,128)(2,1)S(1)}, u32[]{:S(2)}, u32[]{:S(2)}) collective-permute-start(bf16[16,80,128]{2,1,0:T(8,128)(2,1)S(1)} %all_to_all.26.refs_0_), channel_id=1, source_target_pairs={{0,8},{8,0},{1,9},{9,1},{2,10},{10,2},{3,11},{11,3},{4,12},{12,4},... | collective-permute-start | bytes 983048 | tf_op jit(solution)/shard_map/ppermute | solution.py:306

commit v10 on v9

--- a/solution.py
+++ b/solution.py
@@ -70,7 +70,7 @@
 
 
 def pack_kernel(*refs, capacity, rows_shard):
-    sources, (out_ref, pos_ref), buffers, sems = refs[:7], refs[7:9], refs[9:16], refs[16]
+    sources, (out_ref, pos_ref, sent_ref), buffers, sems = refs[:7], refs[7:10], refs[10:17], refs[17]
     copies = [
         pltpu.make_async_copy(source, buffer, sems.at[i])
         for i, (source, buffer) in enumerate(zip(sources, buffers, strict=True))
@@ -104,11 +104,12 @@
     out = jnp.concatenate([w_out_ref[...].astype(f32), jnp.zeros((12, 128), f32)], axis=0)
     tail_row = lax.broadcasted_iota(jnp.int32, (16, 128), 0)
     for shard in range(shards):
-        out_ref[shard, :capacity, :] = rows[shard * capacity : (shard + 1) * capacity]
-        out_ref[shard, capacity : capacity + 64, :] = own
-        tail = jnp.where(tail_row == 14, cur_code[shard : shard + 1], out)
-        tail = jnp.where(tail_row == 15, prev_code[shard : shard + 1], tail)
-        out_ref[shard, capacity + 64 : capacity + 80, :] = tail.astype(bf16)
+        sent_ref[shard, :capacity, :] = rows[shard * capacity : (shard + 1) * capacity]
+        tail = jnp.where(tail_row == 15, prev_code[shard : shard + 1], 0.0)
+        sent_ref[shard, capacity : capacity + 16, :] = tail.astype(bf16)
+        out_ref[shard, :64, :] = own
+        tail = jnp.where(tail_row == 15, cur_code[shard : shard + 1], out)
+        out_ref[shard, 64:80, :] = tail.astype(bf16)
 
 
 def pack(cur_ids, prev_ids, prev_grads, row_place, w_gate, w_up, w_out, shards, capacity, rows_shard):
@@ -121,11 +122,12 @@
     return pl.pallas_call(
         lambda *refs: pack_kernel(*refs, capacity=capacity, rows_shard=rows_shard),
         out_shape=(
-            jax.ShapeDtypeStruct((shards, capacity + 80, 128), bf16),
+            jax.ShapeDtypeStruct((shards, 80, 128), bf16),
             jax.ShapeDtypeStruct((1, tok), jnp.int32),
+            jax.ShapeDtypeStruct((shards, capacity + 16, 128), bf16),
         ),
         in_specs=[pl.BlockSpec(memory_space=pltpu.HBM)] * len(arrays),
-        out_specs=(vmem, vmem),
+        out_specs=(vmem, vmem, vmem),
         scratch_shapes=[pltpu.VMEM(array.shape, array.dtype) for array in arrays]
         + [pltpu.SemaphoreType.DMA((len(arrays),))],
         compiler_params=pltpu.CompilerParams(vmem_limit_bytes=62 * 1024 * 1024),
@@ -317,20 +319,32 @@
     slots = shards * capacity
     core = lax.axis_index("core")
     home = lax.axis_index("emb")
-    payload, cur_pos = pack(
+    payload, cur_pos, prev_payload = pack(
         cur_ids, prev_ids, prev_grads, row_place, w_gate, w_up, w_out,
         shards, capacity, rows_shard,
     )
     first = exchange(payload, "emb")
     rows_table = lax.optimization_barrier(table.astype(bf16))
-    got_rows = first[:, :capacity].reshape(slots, width)
-    slices = first[:, capacity : capacity + 64]
-    wanted = decoded(first[:, capacity + 78], capacity)
-    got_slots = decoded(first[:, capacity + 79], capacity)
+    slices = first[:, :64]
+    wanted = decoded(first[:, 79], capacity)
 
     row_ids = jnp.arange(rows_shard, dtype=jnp.int32)
     hot = (wanted[:, None] == row_ids[None, :]).astype(bf16)
     fetched = dot32(hot, rows_table).astype(bf16)
+    foreign = lax.dynamic_slice(
+        jnp.concatenate([slices, slices], axis=0), (home + 1, 0, 0), (shards - 1, 64, 128)
+    ).reshape((shards - 1) * 64, 128)
+    beside = lax.ppermute(foreign, "x", [(i, i ^ 1) for i in range(lax.axis_size("x"))])
+    both = exchange(
+        jnp.concatenate([fetched.reshape(shards, capacity, width), prev_payload], axis=1), "emb"
+    )
+    answers = both[:, :capacity].reshape(slots, width)
+    got_rows = both[:, capacity : 2 * capacity].reshape(slots, width)
+    got_slots = decoded(both[:, 2 * capacity + 15], capacity)
+    own_weights = lax.all_gather(
+        jnp.concatenate([foreign, beside], axis=0), "y", axis=0, tiled=True
+    )
+    other_weights = swapped(own_weights, "core")
     span = rows_shard // plane // 2
     half_ids = jnp.arange(rows_shard // 2, dtype=jnp.int32)
     half_ids = half_ids // span * (2 * span) + half_ids % span
@@ -338,15 +352,6 @@
     table_part = dot32((part_ids[:, None] == got_slots[None, :]).astype(bf16), got_rows)
     table_part = table_part.astype(bf16).reshape(2, plane, span, width)
 
-    foreign = lax.dynamic_slice(
-        jnp.concatenate([slices, slices], axis=0), (home + 1, 0, 0), (shards - 1, 64, 128)
-    ).reshape((shards - 1) * 64, 128)
-    beside = lax.ppermute(foreign, "x", [(i, i ^ 1) for i in range(lax.axis_size("x"))])
-    answers = exchange(fetched.reshape(shards, capacity, width), "emb").reshape(slots, width)
-    own_weights = lax.all_gather(
-        jnp.concatenate([foreign, beside], axis=0), "y", axis=0, tiled=True
-    )
-    other_weights = swapped(own_weights, "core")
     emb_grad, tower_grads = tower(
         answers, cur_pos, own_weights, other_weights, w_gate, w_up, first, gain, labels,
         table_part,

time: 158 us -> 145 us (0.918)
  waiting for transfers between devices: 34 us -> 21.9 us
    all_to_all x3, waiting for transfers between devices: 22.8 us -> 9.47 us  [exchange(): return lax.all_to_all(pieces, axis, 0, 0, tiled=True)]
    all_to_all x3, starting transfers between devices: 25.3 us -> 30.1 us  [exchange(): return lax.all_to_all(pieces, axis, 0, 0, tiled=True)]
    ppermute x4, starting transfers between devices: 30.3 us -> 26.1 us  [swapped(): return lax.ppermute(array, axis, [(0, 1), (1, 0)])]
  transfers between devices with their start and end apart: 8 -> 8, of which waited for: 6 -> 6; matrix products, arithmetic and copies ran while one was open for 3% -> 2% of each run, Pallas kernels for 0% -> 0%
where the time goes in v10:
time: 145 us; the launch traced here: 144 us
  starting transfers between devices  59.3 us (41%)
  blocking collectives  46.5 us (32%)
  waiting for transfers between devices  21.9 us (15%)
  Pallas kernels  10.6 us (7%)
  other arithmetic  2.72 us (2%)
    all_to_all x2, blocking collectives, exchange(): return lax.all_to_all(pieces, axis, 0, 0, tiled=True)  34.5 us
    all_to_all x3, starting transfers between devices, exchange(): return lax.all_to_all(pieces, axis, 0, 0, tiled=True)  30.1 us
    ppermute x4, starting transfers between devices, swapped(): return lax.ppermute(array, axis, [(0, 1), (1, 0)])  26.1 us
    all_gather x1, blocking collectives, step(): lax.all_gather(jnp.concatenate([foreign, beside], axis=0), 'y', axis=0, t...  11.9 us
    ppermute x4, waiting for transfers between devices, swapped(): return lax.ppermute(array, axis, [(0, 1), (1, 0)])  10 us
    all_to_all x3, waiting for transfers between devices, exchange(): return lax.all_to_all(pieces, axis, 0, 0, tiled=True)  9.47 us
    pallas_call x1, Pallas kernels, tower(): pl.pallas_call(tower_kernel, out_shape=(jax.ShapeDtypeStruct((tok, width)...  6.27 us
    ppermute x1, starting transfers between devices, step(): lax.ppermute(foreign, 'x', [(i, i ^ 1) for i in range(lax.axis_size('x'))])  3.13 us
  transfers between devices with their start and end apart: 8, of which 6 were waited for; matrix products, arithmetic and copies ran while one was open for 2% of the time, Pallas kernels for 0%

profile of v10, /device:TPU:1, one launch (start us, length us, event | category | flops | bytes accessed | tf_op | source)
XLA Modules:
  0.0 144.2 jit_solution(16477391426885007407)
XLA Ops:
  0.6 2.8 %pack.1 = (bf16[8,80,128]{2,1,0:T(8,128)(2,1)}, s32[1,256]{1,0:T(1,128)}, bf16[8,80,128]{2,1,0:T(8,128)(2,1)}) custom-call(s32[1,256]{1,0:T(1,128)} %bitcast.35, s32[1,256]{1,0:T(1,128)} %bitcast.36, bf16[256,128]{1,0:T(8,128)(2,1)} %refs_2_.2, s32[96,128]{1,0:T(8,128)} %bitcast.33, bf16[128,512]{1,0:T(8,128)(2,1)} %w_gate_ref.1, bf16[128,512]{1,0:T(8,128)(2,1)} %w_up_ref.1, ...), custom_call_target="tpu_custom_call" | custom-call | tf_op jit(solution)/shard_map/pack/pallas_call | solution.py:122
  3.4 0.0 copy-start.6
  3.4 0.0 copy-start.7
  3.4 13.2 %all-to-all-start = ((bf16[8,80,128]{2,1,0:T(8,128)(2,1)}), bf16[8,80,128]{2,1,0:T(8,128)(2,1)S(1)}, u32[]{:S(2)}, u32[]{:S(2)}) async-start(bf16[8,80,128]{2,1,0:T(8,128)(2,1)} %get-tuple-element.14), calls=%async_computation | async-start | bytes 327680 | tf_op jit(solution)/shard_map/all_to_all | solution.py:27
  16.6 1.2 convert_element_type.47
  17.8 9.5 %all-to-all-done.shared_ref = bf16[8,80,128]{2,1,0:T(8,128)(2,1)S(1)} async-done(((bf16[8,80,128]{2,1,0:T(8,128)(2,1)}), bf16[8,80,128]{2,1,0:T(8,128)(2,1)S(1)}, u32[]{:S(2)}, u32[]{:S(2)}) %all-to-all-start) | async-done | bytes 163872 | tf_op jit(solution)/shard_map/all_to_all | solution.py:27
  27.3 0.1 slice_add_fusion.1
  27.4 0.1 eq.32
  27.4 0.7 fusion.10
  28.1 0.0 copy-done.6
  28.1 0.7 pad_maximum_fusion
  28.9 0.0 copy-start.2
  28.9 6.9 %all-to-all-start.1 = ((bf16[8,144,128]{2,1,0:T(8,128)(2,1)}), bf16[8,144,128]{2,1,0:T(8,128)(2,1)S(1)}, u32[]{:S(2)}, u32[]{:S(2)}) async-start(bf16[8,144,128]{2,1,0:T(8,128)(2,1)} %pad_maximum_fusion), calls=%async_computation.1 | async-start | bytes 589824 | tf_op jit(solution)/shard_map/all_to_all | solution.py:27
  35.8 0.1 fusion.11
  35.8 3.1 %collective-permute-start = (bf16[448,128]{1,0:T(8,128)(2,1)S(1)}, bf16[448,128]{1,0:T(8,128)(2,1)S(1)}, u32[]{:S(2)}, u32[]{:S(2)}) collective-permute-start(bf16[448,128]{1,0:T(8,128)(2,1)S(1)} %bitcast.28), channel_id=1, source_target_pairs={{0,128},{128,0},{256,384},{384,256},{1,129},{129,1},{257,385},{385... | collective-permute-start | bytes 344072 | tf_op jit(solution)/shard_map/ppermute | solution.py:337
  39.0 0.0 copy-done.7
  39.0 2.3 %collective-permute-done = bf16[448,128]{1,0:T(8,128)(2,1)S(1)} collective-permute-done((bf16[448,128]{1,0:T(8,128)(2,1)S(1)}, bf16[448,128]{1,0:T(8,128)(2,1)S(1)}, u32[]{:S(2)}, u32[]{:S(2)}) %collective-permute-start) | collective-permute-done | bytes 114720 | tf_op jit(solution)/shard_map/ppermute | solution.py:337
  41.4 11.9 %all_gather.3.own_ref = bf16[3584,128]{1,0:T(8,128)(2,1)S(1)} all-gather(bf16[896,128]{1,0:T(8,128)(2,1)S(1)} %pad_maximum_fusion.1), channel_id=1, replica_groups=mesh['x'=4,'y'=4,'zh'=2,'core'=2,'emb'=8] {'y'}, dimensions={0}, use_global_device_ids=true | all-gather | bytes 1146880 | tf_op jit(solution)/shard_map/all_gather | solution.py:344
  53.3 7.3 %collective-permute-start.1 = (bf16[3584,128]{1,0:T(8,128)(2,1)S(1)}, bf16[3584,128]{1,0:T(8,128)(2,1)S(1)}, u32[]{:S(2)}, u32[]{:S(2)}) collective-permute-start(bf16[3584,128]{1,0:T(8,128)(2,1)S(1)} %all_gather.3.own_ref), channel_id=1, source_target_pairs={{0,8},{8,0},{1,9},{9,1},{2,10},{10,2},{3,11},{11,3},{4,12},{12,4},... | collective-permute-start | bytes 2752520 | tf_op jit(solution)/shard_map/ppermute | solution.py:308
  60.6 0.0 all-to-all-done.1
  60.6 0.1 slice_add_fusion
  60.7 0.1 eq.37
  60.8 0.7 fusion.4
  61.5 1.2 collective-permute-done.1.other_ref
  62.7 0.0 copy-done.2
  62.7 0.0 copy-done.3
  62.7 0.0 copy-done.4
  62.7 0.0 copy-done.5
  62.7 6.3 %tower.1 = (f32[256,128]{1,0:T(8,128)}, bf16[2,16,304,128]{3,2,1,0:T(8,128)(2,1)S(1)}) custom-call(bf16[512,128]{1,0:T(8,128)(2,1)S(1)} %bitcast.25, s32[1,256]{1,0:T(1,128)S(1)} %copy-done.4, bf16[3584,128]{1,0:T(8,128)(2,1)S(1)} %all_gather.3.own_ref, bf16[3584,128]{1,0:T(8,128)(2,1)S(1)} %collective-permute-done.1.other_ref, ...), custom_call_target="tpu_custom_call" | custom-call | flops 1610612736 | bytes 5242880 | tf_op jit(solution)/shard_map/tower/pallas_call | solution.py:245
  69.0 0.1 slice_bitcast_fusion
  69.0 2.3 %collective-permute-start.2 = (bf16[16,304,128]{2,1,0:T(8,128)(2,1)S(1)}, bf16[16,304,128]{2,1,0:T(8,128)(2,1)S(1)}, u32[]{:S(2)}, u32[]{:S(2)}) collective-permute-start(bf16[16,304,128]{2,1,0:T(8,128)(2,1)S(1)} %slice_bitcast_fusion), channel_id=1, source_target_pairs={{0,8},{8,0},{1,9},{9,1},{2,10},{10,2},{3,11},{11,3},{4,12},{12,4},... | collective-permute-start | bytes 3735560 | tf_op jit(solution)/shard_map/ppermute | solution.py:308
  71.3 2.5 %collective-permute-done.2 = bf16[16,304,128]{2,1,0:T(8,128)(2,1)S(1)} collective-permute-done((bf16[16,304,128]{2,1,0:T(8,128)(2,1)S(1)}, bf16[16,304,128]{2,1,0:T(8,128)(2,1)S(1)}, u32[]{:S(2)}, u32[]{:S(2)}) %collective-permute-start.2) | collective-permute-done | bytes 1245216 | tf_op jit(solution)/shard_map/ppermute | solution.py:308
  73.9 0.3 fusion.3
  74.2 0.0 copy-start
  74.2 0.0 copy-start.1
  74.2 23.4 %all_to_all.25 = bf16[16,304,128]{2,1,0:T(8,128)(2,1)S(1)} all-to-all(bf16[16,304,128]{2,1,0:T(8,128)(2,1)S(1)} %fusion.3), channel_id=1, replica_groups=mesh['x'=4,'y'=4,'zh'=2,'core'=2,'emb'=8] {'x','y'}, dimensions={0} | all-to-all | bytes 2490368 | tf_op jit(solution)/shard_map/all_to_all | solution.py:27
  97.6 0.1 slice_reduce_fusion
  97.8 0.7 broadcast_in_dim.7
  98.5 10.0 %all-to-all-start.3 = ((bf16[16,32,128]{2,1,0:T(8,128)(2,1)}), bf16[16,32,128]{2,1,0:T(8,128)(2,1)S(1)}, u32[]{:S(2)}, u32[]{:S(2)}) async-start(bf16[16,32,128]{2,1,0:T(8,128)(2,1)} %bitcast.16), calls=%async_computation.3 | async-start | bytes 262144 | tf_op jit(solution)/shard_map/all_to_all | solution.py:27
  108.5 12.0 %collective-permute-start.3 = (f32[48,128]{1,0:T(8,128)S(1)}, f32[48,128]{1,0:T(8,128)S(1)}, u32[]{:S(2)}, u32[]{:S(2)}) collective-permute-start(f32[48,128]{1,0:T(8,128)S(1)} %convert_reduce_fusion), channel_id=1, source_target_pairs={{0,16},{16,0},{1,17},{17,1},{2,18},{18,2},{3,19},{19,3},{4,20},{20... | collective-permute-start | bytes 73736 | tf_op jit(solution)/shard_map/ppermute | solution.py:308
  120.5 5.1 %collective-permute-done.3 = f32[48,128]{1,0:T(8,128)S(1)} collective-permute-done((f32[48,128]{1,0:T(8,128)S(1)}, f32[48,128]{1,0:T(8,128)S(1)}, u32[]{:S(2)}, u32[]{:S(2)}) %collective-permute-start.3) | collective-permute-done | bytes 24608 | tf_op jit(solution)/shard_map/ppermute | solution.py:308
  125.6 0.0 all-to-all-done.3
  125.7 11.1 %all_to_all.26.refs_0_ = bf16[16,80,128]{2,1,0:T(8,128)(2,1)S(1)} all-to-all(bf16[16,80,128]{2,1,0:T(8,128)(2,1)S(1)} %broadcast_in_dim.8), channel_id=1, replica_groups=mesh['x'=4,'y'=4,'zh'=2,'core'=2,'emb'=8] {'x','y'}, dimensions={0} | all-to-all | bytes 655360 | tf_op jit(solution)/shard_map/all_to_all | solution.py:27
  136.8 4.6 %collective-permute-start.4 = (bf16[16,80,128]{2,1,0:T(8,128)(2,1)S(1)}, bf16[16,80,128]{2,1,0:T(8,128)(2,1)S(1)}, u32[]{:S(2)}, u32[]{:S(2)}) collective-permute-start(bf16[16,80,128]{2,1,0:T(8,128)(2,1)S(1)} %all_to_all.26.refs_0_), channel_id=1, source_target_pairs={{0,8},{8,0},{1,9},{9,1},{2,10},{10,2},{3,11},{11,3},{4,12},{12,4},... | collective-permute-start | bytes 983048 | tf_op jit(solution)/shard_map/ppermute | solution.py:308
  141.4 1.2 collective-permute-done.4.refs_1_
  142.7 0.0 copy-done
  142.7 0.0 copy-done.1
  142.7 1.5 %update.1 = (f32[1536,128]{1,0:T(8,128)}, f32[1536,128]{1,0:T(8,128)}, f32[128,512]{1,0:T(8,128)}, f32[128,512]{1,0:T(8,128)}) custom-call(bf16[16,80,128]{2,1,0:T(8,128)(2,1)S(1)} %all_to_all.26.refs_0_, bf16[16,80,128]{2,1,0:T(8,128)(2,1)S(1)} %collective-permute-done.4.refs_1_, f32[1536,128]{1,0:T(8,128)S(1)} %copy-done, f32[1536,128]{1,0:T(8,128)S(1)} %copy-done.1), custom_call_target="tpu_custom_call" | custom-call | tf_op jit(solution)/shard_map/update/pallas_call | solution.py:291
  (17 shorter events, 0.2 us)
Async XLA Ops:
  3.4 24.7 %copy-start.6 = (bf16[8,80,128]{2,1,0:T(8,128)(2,1)S(1)}, bf16[8,80,128]{2,1,0:T(8,128)(2,1)}, u32[]{:S(2)}) copy-start(bf16[8,80,128]{2,1,0:T(8,128)(2,1)} %get-tuple-element.15) | copy-start | bytes 491524
  3.4 35.6 %copy-start.7 = (f32[2048]{0:T(1024)S(1)}, f32[2048]{0:T(1024)}, u32[]{:S(2)}) copy-start(f32[2048]{0:T(1024)} %param.17) | copy-start | bytes 24580
  3.4 23.8 %all-to-all-start = ((bf16[8,80,128]{2,1,0:T(8,128)(2,1)}), bf16[8,80,128]{2,1,0:T(8,128)(2,1)S(1)}, u32[]{:S(2)}, u32[]{:S(2)}) async-start(bf16[8,80,128]{2,1,0:T(8,128)(2,1)} %get-tuple-element.14), calls=%async_computation | async-start | bytes 327680 | tf_op jit(solution)/shard_map/all_to_all | solution.py:27
  28.9 33.8 %copy-start.2 = (bf16[128,512]{1,0:T(8,128)(2,1)S(1)}, bf16[128,512]{1,0:T(8,128)(2,1)}, u32[]{:S(2)}) copy-start(bf16[128,512]{1,0:T(8,128)(2,1)} %w_gate_ref.1) | copy-start | bytes 393220
  28.9 33.8 %copy-start.3 = (bf16[128,512]{1,0:T(8,128)(2,1)S(1)}, bf16[128,512]{1,0:T(8,128)(2,1)}, u32[]{:S(2)}) copy-start(bf16[128,512]{1,0:T(8,128)(2,1)} %w_up_ref.1) | copy-start | bytes 393220
  28.9 33.8 %copy-start.4 = (s32[1,256]{1,0:T(1,128)S(1)}, s32[1,256]{1,0:T(1,128)}, u32[]{:S(2)}) copy-start(s32[1,256]{1,0:T(1,128)} %get-tuple-element.16.target_ref) | copy-start | bytes 3076
  28.9 33.8 %copy-start.5 = (f32[128]{0:T(128)S(1)}, f32[128]{0:T(128)}, u32[]{:S(2)}) copy-start(f32[128]{0:T(128)} %param.18) | copy-start | bytes 1540
  28.9 31.7 %all-to-all-start.1 = ((bf16[8,144,128]{2,1,0:T(8,128)(2,1)}), bf16[8,144,128]{2,1,0:T(8,128)(2,1)S(1)}, u32[]{:S(2)}, u32[]{:S(2)}) async-start(bf16[8,144,128]{2,1,0:T(8,128)(2,1)} %pad_maximum_fusion), calls=%async_computation.1 | async-start | bytes 589824 | tf_op jit(solution)/shard_map/all_to_all | solution.py:27
  35.8 5.5 %collective-permute-start = (bf16[448,128]{1,0:T(8,128)(2,1)S(1)}, bf16[448,128]{1,0:T(8,128)(2,1)S(1)}, u32[]{:S(2)}, u32[]{:S(2)}) collective-permute-start(bf16[448,128]{1,0:T(8,128)(2,1)S(1)} %bitcast.28), channel_id=1, source_target_pairs={{0,128},{128,0},{256,384},{384,256},{1,129},{129,1},{257,385},{385... | collective-permute-start | bytes 344072 | tf_op jit(solution)/shard_map/ppermute | solution.py:337
  53.3 9.3 %collective-permute-start.1 = (bf16[3584,128]{1,0:T(8,128)(2,1)S(1)}, bf16[3584,128]{1,0:T(8,128)(2,1)S(1)}, u32[]{:S(2)}, u32[]{:S(2)}) collective-permute-start(bf16[3584,128]{1,0:T(8,128)(2,1)S(1)} %all_gather.3.own_ref), channel_id=1, source_target_pairs={{0,8},{8,0},{1,9},{9,1},{2,10},{10,2},{3,11},{11,3},{4,12},{12,4},... | collective-permute-start | bytes 2752520 | tf_op jit(solution)/shard_map/ppermute | solution.py:308
  69.0 4.8 %collective-permute-start.2 = (bf16[16,304,128]{2,1,0:T(8,128)(2,1)S(1)}, bf16[16,304,128]{2,1,0:T(8,128)(2,1)S(1)}, u32[]{:S(2)}, u32[]{:S(2)}) collective-permute-start(bf16[16,304,128]{2,1,0:T(8,128)(2,1)S(1)} %slice_bitcast_fusion), channel_id=1, source_target_pairs={{0,8},{8,0},{1,9},{9,1},{2,10},{10,2},{3,11},{11,3},{4,12},{12,4},... | collective-permute-start | bytes 3735560 | tf_op jit(solution)/shard_map/ppermute | solution.py:308
  74.2 68.5 %copy-start = (f32[1536,128]{1,0:T(8,128)S(1)}, f32[1536,128]{1,0:T(8,128)}, u32[]{:S(2)}) copy-start(f32[1536,128]{1,0:T(8,128)} %refs_2_.3) | copy-start | bytes 2359300
  74.2 68.5 %copy-start.1 = (f32[1536,128]{1,0:T(8,128)S(1)}, f32[1536,128]{1,0:T(8,128)}, u32[]{:S(2)}) copy-start(f32[1536,128]{1,0:T(8,128)} %refs_3_.1) | copy-start | bytes 2359300
  98.5 27.2 %all-to-all-start.3 = ((bf16[16,32,128]{2,1,0:T(8,128)(2,1)}), bf16[16,32,128]{2,1,0:T(8,128)(2,1)S(1)}, u32[]{:S(2)}, u32[]{:S(2)}) async-start(bf16[16,32,128]{2,1,0:T(8,128)(2,1)} %bitcast.16), calls=%async_computation.3 | async-start | bytes 262144 | tf_op jit(solution)/shard_map/all_to_all | solution.py:27
  108.5 17.1 %collective-permute-start.3 = (f32[48,128]{1,0:T(8,128)S(1)}, f32[48,128]{1,0:T(8,128)S(1)}, u32[]{:S(2)}, u32[]{:S(2)}) collective-permute-start(f32[48,128]{1,0:T(8,128)S(1)} %convert_reduce_fusion), channel_id=1, source_target_pairs={{0,16},{16,0},{1,17},{17,1},{2,18},{18,2},{3,19},{19,3},{4,20},{20... | collective-permute-start | bytes 73736 | tf_op jit(solution)/shard_map/ppermute | solution.py:308
  136.8 5.8 %collective-permute-start.4 = (bf16[16,80,128]{2,1,0:T(8,128)(2,1)S(1)}, bf16[16,80,128]{2,1,0:T(8,128)(2,1)S(1)}, u32[]{:S(2)}, u32[]{:S(2)}) collective-permute-start(bf16[16,80,128]{2,1,0:T(8,128)(2,1)S(1)} %all_to_all.26.refs_0_), channel_id=1, source_target_pairs={{0,8},{8,0},{1,9},{9,1},{2,10},{10,2},{3,11},{11,3},{4,12},{12,4},... | collective-permute-start | bytes 983048 | tf_op jit(solution)/shard_map/ppermute | solution.py:308

commit v11 on v10

--- a/solution.py
+++ b/solution.py
@@ -361,11 +361,20 @@
     core_sum = (tower_grads[0].astype(f32) + received.astype(f32)).astype(bf16)
     second = exchange(core_sum, XY)
     plane_sum = second[:, : shards * 32].astype(f32).sum(axis=0).astype(bf16)
-    half_grad = second[:, shards * 32 :].astype(f32).sum(axis=0)
-    total_grad = (half_grad + swapped(half_grad, "zh")).astype(bf16)
-    for_z = jnp.broadcast_to(plane_sum.reshape(1, shards, 32, 128), (2, shards, 32, 128))
-    third = exchange(for_z.reshape(2 * shards, 32, 128), ZZ)
-    tower_sum = third.astype(f32).sum(axis=0).astype(bf16)
+    half_grad = second[:, shards * 32 :].astype(f32).sum(axis=0).astype(bf16)
+    for_z = jnp.concatenate(
+        [
+            plane_sum.reshape(shards, 32, 128),
+            jnp.broadcast_to(half_grad[None], (shards, *half_grad.shape)),
+        ],
+        axis=1,
+    )
+    for_z = jnp.broadcast_to(for_z[None], (2, *for_z.shape)).reshape(2 * shards, *for_z.shape[1:])
+    third = exchange(for_z, ZZ)
+    tower_sum = third[:, :32].astype(f32).sum(axis=0).astype(bf16)
+    halves = third[:, 32:].reshape(2, shards, *half_grad.shape)
+    halves = lax.dynamic_index_in_dim(halves, home, 1, keepdims=False).astype(f32)
+    total_grad = (halves[0] + halves[1]).astype(bf16)
     own = to_all(jnp.concatenate([tower_sum, total_grad], axis=0), XY)
     other = swapped(own, "core")
 

time: 145 us -> 149 us (1.028)
  waiting for transfers between devices: 21.9 us -> 30.6 us
  starting transfers between devices: 59.3 us -> 54.1 us
    all_to_all x3, waiting for transfers between devices: 9.47 us -> 23.3 us  [exchange(): return lax.all_to_all(pieces, axis, 0, 0, tiled=True)]
    ppermute x4 -> x3, starting transfers between devices: 26.1 us -> 20.8 us  [swapped(): return lax.ppermute(array, axis, [(0, 1), (1, 0)])]
    ppermute x4 -> x3, waiting for transfers between devices: 10 us -> 4.97 us  [swapped(): return lax.ppermute(array, axis, [(0, 1), (1, 0)])]
  transfers between devices with their start and end apart: 8 -> 7, of which waited for: 6 -> 6; matrix products, arithmetic and copies ran while one was open for 2% -> 1% of each run, Pallas kernels for 0% -> 0%
where the time goes in v11:
time: 149 us; the launch traced here: 148 us
  starting transfers between devices  54.1 us (36%)
  blocking collectives  46.6 us (31%)
  waiting for transfers between devices  30.6 us (21%)
  Pallas kernels  10.6 us (7%)
  other arithmetic  2.74 us (2%)
    all_to_all x2, blocking collectives, exchange(): return lax.all_to_all(pieces, axis, 0, 0, tiled=True)  34.7 us
    all_to_all x3, starting transfers between devices, exchange(): return lax.all_to_all(pieces, axis, 0, 0, tiled=True)  30.1 us
    all_to_all x3, waiting for transfers between devices, exchange(): return lax.all_to_all(pieces, axis, 0, 0, tiled=True)  23.3 us
    ppermute x3, starting transfers between devices, swapped(): return lax.ppermute(array, axis, [(0, 1), (1, 0)])  20.8 us
    all_gather x1, blocking collectives, step(): lax.all_gather(jnp.concatenate([foreign, beside], axis=0), 'y', axis=0, t...  11.9 us
    pallas_call x1, Pallas kernels, tower(): pl.pallas_call(tower_kernel, out_shape=(jax.ShapeDtypeStruct((tok, width)...  6.27 us
    ppermute x3, waiting for transfers between devices, swapped(): return lax.ppermute(array, axis, [(0, 1), (1, 0)])  4.97 us
    ppermute x1, starting transfers between devices, step(): lax.ppermute(foreign, 'x', [(i, i ^ 1) for i in range(lax.axis_size('x'))])  3.13 us
  transfers between devices with their start and end apart: 7, of which 6 were waited for; matrix products, arithmetic and copies ran while one was open for 1% of the time, Pallas kernels for 0%

profile of v11, /device:TPU:1, one launch (start us, length us, event | category | flops | bytes accessed | tf_op | source)
XLA Modules:
  0.0 148.0 jit_solution(55937279952786217)
XLA Ops:
  0.6 2.8 %pack.1 = (bf16[8,80,128]{2,1,0:T(8,128)(2,1)}, s32[1,256]{1,0:T(1,128)}, bf16[8,80,128]{2,1,0:T(8,128)(2,1)}) custom-call(s32[1,256]{1,0:T(1,128)} %bitcast.39, s32[1,256]{1,0:T(1,128)} %bitcast.40, bf16[256,128]{1,0:T(8,128)(2,1)} %refs_2_.2, s32[96,128]{1,0:T(8,128)} %bitcast.37, bf16[128,512]{1,0:T(8,128)(2,1)} %w_gate_ref.1, bf16[128,512]{1,0:T(8,128)(2,1)} %w_up_ref.1, ...), custom_call_target="tpu_custom_call" | custom-call | tf_op jit(solution)/shard_map/pack/pallas_call | solution.py:122
  3.4 0.0 copy-start.6
  3.4 0.0 copy-start.7
  3.4 13.2 %all-to-all-start = ((bf16[8,80,128]{2,1,0:T(8,128)(2,1)}), bf16[8,80,128]{2,1,0:T(8,128)(2,1)S(1)}, u32[]{:S(2)}, u32[]{:S(2)}) async-start(bf16[8,80,128]{2,1,0:T(8,128)(2,1)} %get-tuple-element.14), calls=%async_computation | async-start | bytes 327680 | tf_op jit(solution)/shard_map/all_to_all | solution.py:27
  16.6 1.2 convert_element_type.54
  17.8 9.5 %all-to-all-done.shared_ref = bf16[8,80,128]{2,1,0:T(8,128)(2,1)S(1)} async-done(((bf16[8,80,128]{2,1,0:T(8,128)(2,1)}), bf16[8,80,128]{2,1,0:T(8,128)(2,1)S(1)}, u32[]{:S(2)}, u32[]{:S(2)}) %all-to-all-start) | async-done | bytes 163872 | tf_op jit(solution)/shard_map/all_to_all | solution.py:27
  27.3 0.1 slice_add_fusion.2
  27.4 0.1 eq.32
  27.4 0.7 fusion.10
  28.1 0.0 copy-done.6
  28.1 0.7 pad_maximum_fusion
  28.9 0.0 copy-start.2
  28.9 0.0 copy-start.3
  28.9 0.0 copy-start.4
  28.9 0.0 copy-start.5
  28.9 6.9 %all-to-all-start.1 = ((bf16[8,144,128]{2,1,0:T(8,128)(2,1)}), bf16[8,144,128]{2,1,0:T(8,128)(2,1)S(1)}, u32[]{:S(2)}, u32[]{:S(2)}) async-start(bf16[8,144,128]{2,1,0:T(8,128)(2,1)} %pad_maximum_fusion), calls=%async_computation.1 | async-start | bytes 589824 | tf_op jit(solution)/shard_map/all_to_all | solution.py:27
  35.8 0.1 fusion.11
  35.8 3.1 %collective-permute-start = (bf16[448,128]{1,0:T(8,128)(2,1)S(1)}, bf16[448,128]{1,0:T(8,128)(2,1)S(1)}, u32[]{:S(2)}, u32[]{:S(2)}) collective-permute-start(bf16[448,128]{1,0:T(8,128)(2,1)S(1)} %bitcast.31), channel_id=1, source_target_pairs={{0,128},{128,0},{256,384},{384,256},{1,129},{129,1},{257,385},{385... | collective-permute-start | bytes 344072 | tf_op jit(solution)/shard_map/ppermute | solution.py:337
  39.0 0.0 copy-done.7
  39.0 2.3 %collective-permute-done = bf16[448,128]{1,0:T(8,128)(2,1)S(1)} collective-permute-done((bf16[448,128]{1,0:T(8,128)(2,1)S(1)}, bf16[448,128]{1,0:T(8,128)(2,1)S(1)}, u32[]{:S(2)}, u32[]{:S(2)}) %collective-permute-start) | collective-permute-done | bytes 114720 | tf_op jit(solution)/shard_map/ppermute | solution.py:337
  41.4 11.9 %all_gather.3.own_ref = bf16[3584,128]{1,0:T(8,128)(2,1)S(1)} all-gather(bf16[896,128]{1,0:T(8,128)(2,1)S(1)} %pad_maximum_fusion.1), channel_id=1, replica_groups=mesh['x'=4,'y'=4,'zh'=2,'core'=2,'emb'=8] {'y'}, dimensions={0}, use_global_device_ids=true | all-gather | bytes 1146880 | tf_op jit(solution)/shard_map/all_gather | solution.py:344
  53.3 7.3 %collective-permute-start.1 = (bf16[3584,128]{1,0:T(8,128)(2,1)S(1)}, bf16[3584,128]{1,0:T(8,128)(2,1)S(1)}, u32[]{:S(2)}, u32[]{:S(2)}) collective-permute-start(bf16[3584,128]{1,0:T(8,128)(2,1)S(1)} %all_gather.3.own_ref), channel_id=1, source_target_pairs={{0,8},{8,0},{1,9},{9,1},{2,10},{10,2},{3,11},{11,3},{4,12},{12,4},... | collective-permute-start | bytes 2752520 | tf_op jit(solution)/shard_map/ppermute | solution.py:308
  60.6 0.0 all-to-all-done.1
  60.6 0.1 slice_add_fusion.1
  60.7 0.1 eq.37
  60.8 0.7 fusion.4
  61.5 1.2 collective-permute-done.1.other_ref
  62.7 0.0 copy-done.2
  62.7 0.0 copy-done.3
  62.7 0.0 copy-done.4
  62.7 0.0 copy-done.5
  62.7 6.3 %tower.1 = (f32[256,128]{1,0:T(8,128)}, bf16[2,16,304,128]{3,2,1,0:T(8,128)(2,1)S(1)}) custom-call(bf16[512,128]{1,0:T(8,128)(2,1)S(1)} %bitcast.28, s32[1,256]{1,0:T(1,128)S(1)} %copy-done.4, bf16[3584,128]{1,0:T(8,128)(2,1)S(1)} %all_gather.3.own_ref, bf16[3584,128]{1,0:T(8,128)(2,1)S(1)} %collective-permute-done.1.other_ref, ...), custom_call_target="tpu_custom_call" | custom-call | flops 1610612736 | bytes 5242880 | tf_op jit(solution)/shard_map/tower/pallas_call | solution.py:245
  69.0 0.1 slice_bitcast_fusion
  69.0 2.3 %collective-permute-start.2 = (bf16[16,304,128]{2,1,0:T(8,128)(2,1)S(1)}, bf16[16,304,128]{2,1,0:T(8,128)(2,1)S(1)}, u32[]{:S(2)}, u32[]{:S(2)}) collective-permute-start(bf16[16,304,128]{2,1,0:T(8,128)(2,1)S(1)} %slice_bitcast_fusion), channel_id=1, source_target_pairs={{0,8},{8,0},{1,9},{9,1},{2,10},{10,2},{3,11},{11,3},{4,12},{12,4},... | collective-permute-start | bytes 3735560 | tf_op jit(solution)/shard_map/ppermute | solution.py:308
  71.3 2.5 %collective-permute-done.2 = bf16[16,304,128]{2,1,0:T(8,128)(2,1)S(1)} collective-permute-done((bf16[16,304,128]{2,1,0:T(8,128)(2,1)S(1)}, bf16[16,304,128]{2,1,0:T(8,128)(2,1)S(1)}, u32[]{:S(2)}, u32[]{:S(2)}) %collective-permute-start.2) | collective-permute-done | bytes 1245216 | tf_op jit(solution)/shard_map/ppermute | solution.py:308
  73.9 0.3 fusion.3
  74.2 23.3 %all_to_all.25 = bf16[16,304,128]{2,1,0:T(8,128)(2,1)S(1)} all-to-all(bf16[16,304,128]{2,1,0:T(8,128)(2,1)S(1)} %fusion.3), channel_id=1, replica_groups=mesh['x'=4,'y'=4,'zh'=2,'core'=2,'emb'=8] {'x','y'}, dimensions={0} | all-to-all | bytes 2490368 | tf_op jit(solution)/shard_map/all_to_all | solution.py:27
  97.5 0.0 copy-start
  97.5 0.1 slice_reduce_fusion
  97.7 0.8 broadcast_in_dim.7
  98.5 10.0 %all-to-all-start.3 = ((bf16[16,80,128]{2,1,0:T(8,128)(2,1)}), bf16[16,80,128]{2,1,0:T(8,128)(2,1)S(1)}, u32[]{:S(2)}, u32[]{:S(2)}) async-start(bf16[16,80,128]{2,1,0:T(8,128)(2,1)} %bitcast.16), calls=%async_computation.3 | async-start | bytes 655360 | tf_op jit(solution)/shard_map/all_to_all | solution.py:27
  108.5 13.8 %all-to-all-done.3 = bf16[16,80,128]{2,1,0:T(8,128)(2,1)S(1)} async-done(((bf16[16,80,128]{2,1,0:T(8,128)(2,1)}), bf16[16,80,128]{2,1,0:T(8,128)(2,1)S(1)}, u32[]{:S(2)}, u32[]{:S(2)}) %all-to-all-start.3) | async-done | bytes 327712 | tf_op jit(solution)/shard_map/all_to_all | solution.py:27
  122.5 11.4 %all_to_all.26.refs_0_ = bf16[16,80,128]{2,1,0:T(8,128)(2,1)S(1)} all-to-all(bf16[16,80,128]{2,1,0:T(8,128)(2,1)S(1)} %broadcast_in_dim.8), channel_id=1, replica_groups=mesh['x'=4,'y'=4,'zh'=2,'core'=2,'emb'=8] {'x','y'}, dimensions={0} | all-to-all | bytes 655360 | tf_op jit(solution)/shard_map/all_to_all | solution.py:27
  133.9 11.3 %collective-permute-start.3 = (bf16[16,80,128]{2,1,0:T(8,128)(2,1)S(1)}, bf16[16,80,128]{2,1,0:T(8,128)(2,1)S(1)}, u32[]{:S(2)}, u32[]{:S(2)}) collective-permute-start(bf16[16,80,128]{2,1,0:T(8,128)(2,1)S(1)} %all_to_all.26.refs_0_), channel_id=1, source_target_pairs={{0,8},{8,0},{1,9},{9,1},{2,10},{10,2},{3,11},{11,3},{4,12},{12,4},... | collective-permute-start | bytes 983048 | tf_op jit(solution)/shard_map/ppermute | solution.py:308
  145.2 1.2 collective-permute-done.3.refs_1_
  146.5 0.0 copy-done
  146.5 0.0 copy-done.1
  146.5 1.5 %update.1 = (f32[1536,128]{1,0:T(8,128)}, f32[1536,128]{1,0:T(8,128)}, f32[128,512]{1,0:T(8,128)}, f32[128,512]{1,0:T(8,128)}) custom-call(bf16[16,80,128]{2,1,0:T(8,128)(2,1)S(1)} %all_to_all.26.refs_0_, bf16[16,80,128]{2,1,0:T(8,128)(2,1)S(1)} %collective-permute-done.3.refs_1_, f32[1536,128]{1,0:T(8,128)S(1)} %copy-done, f32[1536,128]{1,0:T(8,128)S(1)} %copy-done.1), custom_call_target="tpu_custom_call" | custom-call | tf_op jit(solution)/shard_map/update/pallas_call | solution.py:291
  (19 shorter events, 0.3 us)
Async XLA Ops:
  3.4 24.7 %copy-start.6 = (bf16[8,80,128]{2,1,0:T(8,128)(2,1)S(1)}, bf16[8,80,128]{2,1,0:T(8,128)(2,1)}, u32[]{:S(2)}) copy-start(bf16[8,80,128]{2,1,0:T(8,128)(2,1)} %get-tuple-element.15) | copy-start | bytes 491524
  3.4 35.6 %copy-start.7 = (f32[2048]{0:T(1024)S(1)}, f32[2048]{0:T(1024)}, u32[]{:S(2)}) copy-start(f32[2048]{0:T(1024)} %param.17) | copy-start | bytes 24580
  3.4 23.8 %all-to-all-start = ((bf16[8,80,128]{2,1,0:T(8,128)(2,1)}), bf16[8,80,128]{2,1,0:T(8,128)(2,1)S(1)}, u32[]{:S(2)}, u32[]{:S(2)}) async-start(bf16[8,80,128]{2,1,0:T(8,128)(2,1)} %get-tuple-element.14), calls=%async_computation | async-start | bytes 327680 | tf_op jit(solution)/shard_map/all_to_all | solution.py:27
  28.9 33.8 %copy-start.2 = (bf16[128,512]{1,0:T(8,128)(2,1)S(1)}, bf16[128,512]{1,0:T(8,128)(2,1)}, u32[]{:S(2)}) copy-start(bf16[128,512]{1,0:T(8,128)(2,1)} %w_gate_ref.1) | copy-start | bytes 393220
  28.9 33.8 %copy-start.3 = (bf16[128,512]{1,0:T(8,128)(2,1)S(1)}, bf16[128,512]{1,0:T(8,128)(2,1)}, u32[]{:S(2)}) copy-start(bf16[128,512]{1,0:T(8,128)(2,1)} %w_up_ref.1) | copy-start | bytes 393220
  28.9 33.8 %copy-start.4 = (s32[1,256]{1,0:T(1,128)S(1)}, s32[1,256]{1,0:T(1,128)}, u32[]{:S(2)}) copy-start(s32[1,256]{1,0:T(1,128)} %get-tuple-element.16.target_ref) | copy-start | bytes 3076
  28.9 33.8 %copy-start.5 = (f32[128]{0:T(128)S(1)}, f32[128]{0:T(128)}, u32[]{:S(2)}) copy-start(f32[128]{0:T(128)} %param.18) | copy-start | bytes 1540
  28.9 31.7 %all-to-all-start.1 = ((bf16[8,144,128]{2,1,0:T(8,128)(2,1)}), bf16[8,144,128]{2,1,0:T(8,128)(2,1)S(1)}, u32[]{:S(2)}, u32[]{:S(2)}) async-start(bf16[8,144,128]{2,1,0:T(8,128)(2,1)} %pad_maximum_fusion), calls=%async_computation.1 | async-start | bytes 589824 | tf_op jit(solution)/shard_map/all_to_all | solution.py:27
  35.8 5.5 %collective-permute-start = (bf16[448,128]{1,0:T(8,128)(2,1)S(1)}, bf16[448,128]{1,0:T(8,128)(2,1)S(1)}, u32[]{:S(2)}, u32[]{:S(2)}) collective-permute-start(bf16[448,128]{1,0:T(8,128)(2,1)S(1)} %bitcast.31), channel_id=1, source_target_pairs={{0,128},{128,0},{256,384},{384,256},{1,129},{129,1},{257,385},{385... | collective-permute-start | bytes 344072 | tf_op jit(solution)/shard_map/ppermute | solution.py:337
  53.3 9.3 %collective-permute-start.1 = (bf16[3584,128]{1,0:T(8,128)(2,1)S(1)}, bf16[3584,128]{1,0:T(8,128)(2,1)S(1)}, u32[]{:S(2)}, u32[]{:S(2)}) collective-permute-start(bf16[3584,128]{1,0:T(8,128)(2,1)S(1)} %all_gather.3.own_ref), channel_id=1, source_target_pairs={{0,8},{8,0},{1,9},{9,1},{2,10},{10,2},{3,11},{11,3},{4,12},{12,4},... | collective-permute-start | bytes 2752520 | tf_op jit(solution)/shard_map/ppermute | solution.py:308
  69.0 4.8 %collective-permute-start.2 = (bf16[16,304,128]{2,1,0:T(8,128)(2,1)S(1)}, bf16[16,304,128]{2,1,0:T(8,128)(2,1)S(1)}, u32[]{:S(2)}, u32[]{:S(2)}) collective-permute-start(bf16[16,304,128]{2,1,0:T(8,128)(2,1)S(1)} %slice_bitcast_fusion), channel_id=1, source_target_pairs={{0,8},{8,0},{1,9},{9,1},{2,10},{10,2},{3,11},{11,3},{4,12},{12,4},... | collective-permute-start | bytes 3735560 | tf_op jit(solution)/shard_map/ppermute | solution.py:308
  97.5 49.0 %copy-start = (f32[1536,128]{1,0:T(8,128)S(1)}, f32[1536,128]{1,0:T(8,128)}, u32[]{:S(2)}) copy-start(f32[1536,128]{1,0:T(8,128)} %refs_2_.3) | copy-start | bytes 2359300
  97.5 49.0 %copy-start.1 = (f32[1536,128]{1,0:T(8,128)S(1)}, f32[1536,128]{1,0:T(8,128)}, u32[]{:S(2)}) copy-start(f32[1536,128]{1,0:T(8,128)} %refs_3_.1) | copy-start | bytes 2359300
  98.5 23.9 %all-to-all-start.3 = ((bf16[16,80,128]{2,1,0:T(8,128)(2,1)}), bf16[16,80,128]{2,1,0:T(8,128)(2,1)S(1)}, u32[]{:S(2)}, u32[]{:S(2)}) async-start(bf16[16,80,128]{2,1,0:T(8,128)(2,1)} %bitcast.16), calls=%async_computation.3 | async-start | bytes 655360 | tf_op jit(solution)/shard_map/all_to_all | solution.py:27
  133.9 12.5 %collective-permute-start.3 = (bf16[16,80,128]{2,1,0:T(8,128)(2,1)S(1)}, bf16[16,80,128]{2,1,0:T(8,128)(2,1)S(1)}, u32[]{:S(2)}, u32[]{:S(2)}) collective-permute-start(bf16[16,80,128]{2,1,0:T(8,128)(2,1)S(1)} %all_to_all.26.refs_0_), channel_id=1, source_target_pairs={{0,8},{8,0},{1,9},{9,1},{2,10},{10,2},{3,11},{11,3},{4,12},{12,4},... | collective-permute-start | bytes 983048 | tf_op jit(solution)/shard_map/ppermute | solution.py:308
